TPU v7x, 32 devices: a whole 2x2x4 slice. The times are simulated.
32 devices in a mesh: seq: 4 (over y, x), seg: 4 (over z), head: 2 (over core).
Axes of the slice: x: 2, y: 2, z: 4, core: 2. Of those that a mesh axis runs over, the one named last changes fastest.
Arguments:
- queries: bfloat16 [8, 16384, 128], P('head', ('seg', 'seq')), may hold values from -6 to 6
- keys: bfloat16 [8, 16384, 128], P('head', ('seg', 'seq')), may hold values from -6 to 6
- values: bfloat16 [8, 16384, 128], P('head', ('seg', 'seq')), may hold values from -8 to 8
- teacher: bfloat16 [8, 16384, 128], P('head', ('seg', 'seq')), may hold values from -6 to 6
- query_proj: float32 [128, 16], replicated, may hold values from -0.5 to 0.5
- key_proj: float32 [128, 16], replicated, may hold values from -0.5 to 0.5
Outputs:
- student: bfloat16 [8, 16384, 128], P('head', ('seg', 'seq'))
- query_grad: float32 [128, 16], replicated
- key_grad: float32 [128, 16], replicated
All inputs are finite; a program needn't handle non-finite values.
Results may differ from a plain program's by a relative error of at most 0.0014.
The roundings to bfloat16 on the way count: a program that leaves them out, or rounds other values in their place, can miss the bound.
Values sent between devices are 32-bit elements; how exact they have to be, the bound alone decides.
No kernel may reach another device: no remote copies, remote signals or barrier semaphores. Data moves between devices by JAX's collectives and lax.ppermute only.
A program may use at most 64 MiB of HBM per device.

v0:
```python
import math

import jax
import jax.numpy as jnp
import numpy as np
from jax import lax
from jax.sharding import PartitionSpec as P

highest = lax.Precision.HIGHEST


def carried_in(value, axis, join, neutral, backward):
    count, mine = (lax.axis_size(axis), lax.axis_index(axis))
    pieces = jax.tree.map(lambda part: lax.all_gather(part, axis), value)
    if backward:
        pieces = jax.tree.map(lambda part: part[::-1], pieces)
        mine = count - 1 - mine
    running = jax.tree.map(
        lambda part, zero: jnp.full_like(part, 0) + jnp.asarray(zero, part.dtype), value, neutral
    )

    def step(position, running):
        longer = join(running, jax.tree.map(lambda part: part[position], pieces))
        return jax.tree.map(lambda new, old: jnp.where(position < mine, new, old), longer, running)

    return lax.fori_loop(0, count - 1, step, running)


def feature_tables(width):
    first, second = np.triu_indices(width)
    eye = np.eye(width)
    coef = np.where(first == second, 0.5**0.5, 1.0)
    return (
        jnp.asarray(eye[first], jnp.float32),
        jnp.asarray(eye[second], jnp.float32),
        jnp.asarray(coef, jnp.float32),
    )


def features(proj_t, tables):
    sel_a, sel_b, coef = tables
    left = jnp.dot(sel_a, proj_t, precision=highest)
    right = jnp.dot(sel_b, proj_t, precision=highest)
    return jnp.concatenate([jnp.ones_like(proj_t[:1]), proj_t, coef[:, None] * left * right], 0)


def feature_grad(proj_t, grad_phi, tables):
    sel_a, sel_b, coef = tables
    width = proj_t.shape[0]
    left = jnp.dot(sel_a, proj_t, precision=highest)
    right = jnp.dot(sel_b, proj_t, precision=highest)
    quad = grad_phi[1 + width :] * coef[:, None]
    return (
        grad_phi[1 : 1 + width]
        + jnp.dot(sel_a.T, quad * right, precision=highest)
        + jnp.dot(sel_b.T, quad * left, precision=highest)
    )


def project(weight_b, rows):
    return lax.dot_general(
        weight_b, rows, (((0,), (1,)), ((), ())), preferred_element_type=jnp.float32
    )


def head_state(q_h, k_h, v_h, wq_b, wk_b, tables):
    q_t = project(wq_b, q_h)
    k_t = project(wk_b, k_h)
    phi_k = features(k_t, tables)
    state = jnp.dot(phi_k.astype(jnp.bfloat16), v_h, preferred_element_type=jnp.float32)
    return (q_t, k_t, state, jnp.sum(phi_k, 1))


def head_forward(q_t, k_t, v_h, teacher_h, s_prev, z_prev, scale, tables):
    phi_q = features(q_t, tables)
    length = q_t.shape[1]
    scores = lax.dot_general(q_t, k_t, (((0,), (0,)), ((), ())), precision=highest)
    causal = jnp.arange(length)[:, None] >= jnp.arange(length)[None, :]
    weights = jnp.where(causal, 1.0 + scores + 0.5 * scores * scores, 0.0)
    numer = jnp.dot(weights.astype(jnp.bfloat16), v_h, preferred_element_type=jnp.float32)
    numer = numer + lax.dot_general(phi_q, s_prev, (((0,), (0,)), ((), ())), precision=highest)
    denom = jnp.sum(weights, 1) + jnp.dot(z_prev, phi_q, precision=highest)
    student = numer / denom[:, None]
    g_out = scale * (student - teacher_h.astype(jnp.float32))
    g_numer = g_out / denom[:, None]
    g_denom = -jnp.sum(g_out * student, 1) / denom
    g_weights = (
        lax.dot_general(
            g_numer.astype(jnp.bfloat16),
            v_h,
            (((1,), (1,)), ((), ())),
            preferred_element_type=jnp.float32,
        )
        + g_denom[:, None]
    )
    g_scores = jnp.where(causal, g_weights * (1.0 + scores), 0.0)
    g_q = lax.dot_general(k_t, g_scores, (((1,), (1,)), ((), ())), precision=highest)
    g_k = jnp.dot(q_t, g_scores, precision=highest)
    g_phi_q = (
        lax.dot_general(s_prev, g_numer, (((1,), (1,)), ((), ())), precision=highest)
        + z_prev[:, None] * g_denom[None, :]
    )
    g_q = g_q + feature_grad(q_t, g_phi_q, tables)
    g_state = jnp.dot(phi_q, g_numer, precision=highest)
    h_state = jnp.dot(phi_q, g_denom, precision=highest)
    return (student, g_q, g_k, g_state, h_state)


def head_grads(q_h, k_h, v_h, k_t, g_q, g_k, g_next, h_next, tables):
    g_phi_k = (
        lax.dot_general(
            g_next.astype(jnp.bfloat16),
            v_h,
            (((1,), (1,)), ((), ())),
            preferred_element_type=jnp.float32,
        )
        + h_next[:, None]
    )
    g_k = g_k + feature_grad(k_t, g_phi_k, tables)
    grad_q = lax.dot_general(
        q_h, g_q.astype(jnp.bfloat16), (((0,), (1,)), ((), ())), preferred_element_type=jnp.float32
    )
    grad_k = lax.dot_general(
        k_h, g_k.astype(jnp.bfloat16), (((0,), (1,)), ((), ())), preferred_element_type=jnp.float32
    )
    return (grad_q, grad_k)


def add_trees(first, second):
    return jax.tree.map(jnp.add, first, second)


def masked_fold(mine, backward, carry, piece):
    rows = piece[0].shape[0]
    index = jnp.arange(rows)
    keep = index > mine if backward else index < mine

    def pick(array):
        shaped = keep.reshape((rows,) + (1,) * (array.ndim - 1))
        return jnp.sum(jnp.where(shaped, array, 0.0), 0)

    part = jax.tree.map(pick, piece)
    whole = jax.tree.map(lambda array: jnp.sum(array, 0), piece)
    return (add_trees(carry[0], part), add_trees(carry[1], whole))


def carried(local, backward):
    zeros = jax.tree.map(jnp.zeros_like, local)
    stacked = jax.tree.map(lambda array: array[None], local)
    inner, totals = masked_fold(
        lax.axis_index("seq"),
        backward,
        (zeros, zeros),
        (
            lax.all_gather(stacked[0], "seq", axis=0, tiled=True),
            lax.all_gather(stacked[1], "seq", axis=0, tiled=True),
        ),
    )
    outer = carried_in(totals, "seg", add_trees, zeros, backward)
    return add_trees(inner, outer)


def shards(queries, keys, values, teacher, query_proj, key_proj):
    tables = feature_tables(query_proj.shape[1])
    wq_b = query_proj.astype(jnp.bfloat16)
    wk_b = key_proj.astype(jnp.bfloat16)
    q_t, k_t, states, counts = lax.map(
        lambda xs: head_state(xs[0], xs[1], xs[2], wq_b, wk_b, tables), (queries, keys, values)
    )
    s_prev, z_prev = carried((states, counts), False)
    heads_all = queries.shape[0] * lax.axis_size("head")
    tokens_all = queries.shape[1] * lax.axis_size("seq") * lax.axis_size("seg")
    scale = 1.0 / math.sqrt(heads_all * tokens_all)
    student, g_q, g_k, g_state, h_state = lax.map(
        lambda xs: head_forward(xs[0], xs[1], xs[2], xs[3], xs[4], xs[5], scale, tables),
        (q_t, k_t, values, teacher, s_prev, z_prev),
    )
    g_next, h_next = carried((g_state, h_state), True)
    grad_q, grad_k = lax.map(
        lambda xs: head_grads(xs[0], xs[1], xs[2], xs[3], xs[4], xs[5], xs[6], xs[7], tables),
        (queries, keys, values, k_t, g_q, g_k, g_next, h_next),
    )
    summed = lax.psum((jnp.sum(grad_q, 0), jnp.sum(grad_k, 0)), ("seq", "seg", "head"))
    return (student.astype(jnp.bfloat16), summed[0], summed[1])


def solution(mesh):
    in_specs = (
        P("head", ("seg", "seq"), None),
        P("head", ("seg", "seq"), None),
        P("head", ("seg", "seq"), None),
        P("head", ("seg", "seq"), None),
        P(),
        P(),
    )
    out_specs = (P("head", ("seg", "seq"), None), P(), P())
    return jax.shard_map(shards, mesh=mesh, in_specs=in_specs, out_specs=out_specs, check_vma=False)
```

profile of v0, /device:TPU:0, one launch (start us, length us, event | category | flops | bytes accessed | tf_op | source)
XLA Modules:
  0.0 344.7 jit_solution(8274270570329167139)
XLA Ops:
  8.7 27.1 %while.81 = (s32[]{:T(128)}, f32[4,16,1024]{2,1,0:T(8,128)S(1)}, f32[4,16,1024]{2,1,0:T(8,128)S(1)}, f32[4,153,128]{2,1,0:T(8,128)S(1)}, f32[4,153]{1,0:T(4,128)...) while((s32[]{:T(128)}, f32[4,16,1024]{2,1,0:T(8,128)S(1)}, ...), condition=%wide.region_2.3_spmd.clone, body=%wide.region_0.2_spmd.sunk.clone.sunk | while | flops 103662440 | bytes 4145861 | solution.py:167
  11.0 1.5 convolution_multiply_fusion.7
  12.5 1.5 fusion.187
  17.7 1.5 convolution_multiply_fusion.7
  24.5 1.5 convolution_multiply_fusion.7
  31.3 1.5 convolution_multiply_fusion.7
  36.6 31.5 %all-gather.17.cloned.1.call-done = f32[16,153,128]{2,1,0:T(8,128)} async-done(((f32[4,153,128]{2,1,0:T(8,128)}), f32[16,153,128]{2,1,0:T(8,128)}) %all-gather.17.cloned.1.call-update) | async-done | bytes 1253392 | tf_op jit(solution)/shard_map/all_gather | solution.py:155
  68.1 2.4 fusion.90
  70.6 8.1 %all-gather.8 = f32[4,4,153]{2,1,0:T(4,128)S(1)} all-gather(f32[1,4,153]{2,1,0:T(4,128)S(1)} %bitcast.304), channel_id=4, replica_groups=mesh['seq'=4,'seg'=4,'head'=2] {'seq'}, dimensions={0}, use_global_device_ids=true | all-gather | bytes 12240 | tf_op jit(solution)/shard_map/all_gather | solution.py:156
  78.8 13.7 %all-gather.9 = f32[4,4,153]{2,1,0:T(4,128)S(1)} all-gather(f32[1,4,153]{2,1,0:T(4,128)S(1)} %bitcast.301), channel_id=5, replica_groups=mesh['seq'=4,'seg'=4,'head'=2] {'seg'}, dimensions={0}, use_global_device_ids=true | all-gather | bytes 12240 | tf_op jit(solution)/shard_map/all_gather | solution.py:14
  93.2 10.2 %all-gather.19.cloned.1.call-done = f32[16,153,128]{2,1,0:T(8,128)} async-done(((f32[4,153,128]{2,1,0:T(8,128)}), f32[16,153,128]{2,1,0:T(8,128)}) %all-gather.19.cloned.1.call-update) | async-done | bytes 1253392 | tf_op jit(solution)/shard_map/all_gather | solution.py:14
  103.4 3.4 while.84
  109.1 98.5 %while.82 = (s32[]{:T(128)}, bf16[4,1024,128]{2,1,0:T(8,128)(2,1)}, bf16[4,16,1024]{2,1,0:T(8,128)(2,1)}, f32[4,16,1024]{2,1,0:T(8,128)}, f32[4,153,128]{2,1,0:T...) while((s32[]{:T(128)}, bf16[4,1024,128]{2,1,0:T(8,128)(2,1)}, ...), condition=%wide.region_12.13_spmd.clone, body=%wide.region_9.12_spmd.sunk.clone.sunk | while | flops 1998507008 | bytes 75882544 | solution.py:174
  110.4 3.8 %fusion.212 = (f32[1024]{0:T(1024)S(1)}, f32[1024,1024]{0,1:T(8,128)S(1)}) fusion(f32[16,1024]{1,0:T(8,128)S(1)} %dynamic-slice_bitcast_fusion.2, f32[4,16,1024]{2,1,0:T(8,128)S(1)} %get-tuple-element.1167, s32[]{:T(128)S(6)} %copy.77), kind=kOutput, calls=%fused_computation.28.clone.1 | convolution fusion | flops 208665600 | bytes 4329476 | tf_op jit(solution)/shard_map/while/body/eval_jaxpr/dot_general | solution.py:77
  116.0 1.6 fusion.215
  117.6 1.8 fusion.216
  120.3 2.1 convolution_add_fusion.13
  123.5 1.8 multiply_select_fusion.2
  125.3 2.1 fusion.217
  127.4 4.2 %fusion.218 = f32[4,16,1024]{2,1,0:T(8,128)} fusion(f32[4,16,1024]{2,1,0:T(8,128)} %get-tuple-element.1144, s32[]{:T(128)S(6)} %copy.77, f32[16,1024]{1,0:T(8,128)S(1)} %dynamic-slice_bitcast_fusion.2, f32[1024,1024]{0,1:T(8,128)S(1)} %multiply_select_fusion.2), kind=kOutput, calls=%fused_computation.37.clone.1 | convolution fusion | flops 201326592 | bytes 4325380 | tf_op jit(solution)/shard_map/while/body/eval_jaxpr/dot_general | solution.py:98
  134.9 3.8 %fusion.212 = (f32[1024]{0:T(1024)S(1)}, f32[1024,1024]{0,1:T(8,128)S(1)}) fusion(f32[16,1024]{1,0:T(8,128)S(1)} %dynamic-slice_bitcast_fusion.2, f32[4,16,1024]{2,1,0:T(8,128)S(1)} %get-tuple-element.1167, s32[]{:T(128)S(6)} %copy.77), kind=kOutput, calls=%fused_computation.28.clone.1 | convolution fusion | flops 208665600 | bytes 4329476 | tf_op jit(solution)/shard_map/while/body/eval_jaxpr/dot_general | solution.py:77
  140.6 1.6 fusion.215
  142.2 1.8 fusion.216
  144.8 2.1 convolution_add_fusion.13
  148.0 1.8 multiply_select_fusion.2
  149.9 2.1 fusion.217
  152.0 4.2 %fusion.218 = f32[4,16,1024]{2,1,0:T(8,128)} fusion(f32[4,16,1024]{2,1,0:T(8,128)} %get-tuple-element.1144, s32[]{:T(128)S(6)} %copy.77, f32[16,1024]{1,0:T(8,128)S(1)} %dynamic-slice_bitcast_fusion.2, f32[1024,1024]{0,1:T(8,128)S(1)} %multiply_select_fusion.2), kind=kOutput, calls=%fused_computation.37.clone.1 | convolution fusion | flops 201326592 | bytes 4325380 | tf_op jit(solution)/shard_map/while/body/eval_jaxpr/dot_general | solution.py:98
  159.5 3.8 %fusion.212 = (f32[1024]{0:T(1024)S(1)}, f32[1024,1024]{0,1:T(8,128)S(1)}) fusion(f32[16,1024]{1,0:T(8,128)S(1)} %dynamic-slice_bitcast_fusion.2, f32[4,16,1024]{2,1,0:T(8,128)S(1)} %get-tuple-element.1167, s32[]{:T(128)S(6)} %copy.77), kind=kOutput, calls=%fused_computation.28.clone.1 | convolution fusion | flops 208665600 | bytes 4329476 | tf_op jit(solution)/shard_map/while/body/eval_jaxpr/dot_general | solution.py:77
  165.1 1.6 fusion.215
  166.7 1.8 fusion.216
  169.4 2.1 convolution_add_fusion.13
  172.5 1.8 multiply_select_fusion.2
  174.4 2.1 fusion.217
  176.5 4.2 %fusion.218 = f32[4,16,1024]{2,1,0:T(8,128)} fusion(f32[4,16,1024]{2,1,0:T(8,128)} %get-tuple-element.1144, s32[]{:T(128)S(6)} %copy.77, f32[16,1024]{1,0:T(8,128)S(1)} %dynamic-slice_bitcast_fusion.2, f32[1024,1024]{0,1:T(8,128)S(1)} %multiply_select_fusion.2), kind=kOutput, calls=%fused_computation.37.clone.1 | convolution fusion | flops 201326592 | bytes 4325380 | tf_op jit(solution)/shard_map/while/body/eval_jaxpr/dot_general | solution.py:98
  184.0 3.8 %fusion.212 = (f32[1024]{0:T(1024)S(1)}, f32[1024,1024]{0,1:T(8,128)S(1)}) fusion(f32[16,1024]{1,0:T(8,128)S(1)} %dynamic-slice_bitcast_fusion.2, f32[4,16,1024]{2,1,0:T(8,128)S(1)} %get-tuple-element.1167, s32[]{:T(128)S(6)} %copy.77), kind=kOutput, calls=%fused_computation.28.clone.1 | convolution fusion | flops 208665600 | bytes 4329476 | tf_op jit(solution)/shard_map/while/body/eval_jaxpr/dot_general | solution.py:77
  189.6 1.6 fusion.215
  191.2 1.8 fusion.216
  193.9 2.1 convolution_add_fusion.13
  197.1 1.8 multiply_select_fusion.2
  198.9 2.1 fusion.217
  201.0 4.2 %fusion.218 = f32[4,16,1024]{2,1,0:T(8,128)} fusion(f32[4,16,1024]{2,1,0:T(8,128)} %get-tuple-element.1144, s32[]{:T(128)S(6)} %copy.77, f32[16,1024]{1,0:T(8,128)S(1)} %dynamic-slice_bitcast_fusion.2, f32[1024,1024]{0,1:T(8,128)S(1)} %multiply_select_fusion.2), kind=kOutput, calls=%fused_computation.37.clone.1 | convolution fusion | flops 201326592 | bytes 4325380 | tf_op jit(solution)/shard_map/while/body/eval_jaxpr/dot_general | solution.py:98
  207.7 27.9 %all-gather.21.cloned.1.call-done = f32[16,153,128]{2,1,0:T(8,128)} async-done(((f32[4,153,128]{2,1,0:T(8,128)}), f32[16,153,128]{2,1,0:T(8,128)}) %all-gather.21.cloned.1.call-update) | async-done | bytes 1253392 | tf_op jit(solution)/shard_map/all_gather | solution.py:155
  235.6 2.3 fusion.89
  238.0 8.1 %all-gather.10 = f32[4,4,153]{2,1,0:T(4,128)S(1)} all-gather(f32[1,4,153]{2,1,0:T(4,128)S(1)} %bitcast.303), channel_id=8, replica_groups=mesh['seq'=4,'seg'=4,'head'=2] {'seq'}, dimensions={0}, use_global_device_ids=true | all-gather | bytes 12240 | tf_op jit(solution)/shard_map/all_gather | solution.py:156
  246.2 13.7 %all-gather.11 = f32[4,4,153]{2,1,0:T(4,128)S(1)} all-gather(f32[1,4,153]{2,1,0:T(4,128)S(1)} %bitcast.302), channel_id=9, replica_groups=mesh['seq'=4,'seg'=4,'head'=2] {'seg'}, dimensions={0}, use_global_device_ids=true | all-gather | bytes 12240 | tf_op jit(solution)/shard_map/all_gather | solution.py:14
  259.9 10.9 %all-gather.23.cloned.1.call-done = f32[16,153,128]{2,1,0:T(8,128)} async-done(((f32[4,153,128]{2,1,0:T(8,128)}), f32[16,153,128]{2,1,0:T(8,128)}) %all-gather.23.cloned.1.call-update) | async-done | bytes 1253392 | tf_op jit(solution)/shard_map/all_gather | solution.py:14
  272.7 25.7 %while.83 = (s32[]{:T(128)}, f32[4,128,16]{1,2,0:T(8,128)S(1)}, f32[4,128,16]{1,2,0:T(8,128)S(1)}, bf16[4,1024,128]{2,1,0:T(8,128)(2,1)}, bf16[4,16,1024]{2,1,0:...) while((s32[]{:T(128)}, f32[4,128,16]{1,2,0:T(8,128)S(1)}, ...), condition=%wide.region_20.21_spmd.clone, body=%wide.region_19.20_spmd.sunk.clone.sunk | while | flops 156230656 | bytes 5469037 | solution.py:179
  298.4 39.8 %all-reduce = (f32[128,16]{0,1:T(8,128)}, f32[128,16]{0,1:T(8,128)}) all-reduce(f32[128,16]{0,1:T(8,128)S(1)} %reduce_sum.125, f32[128,16]{0,1:T(8,128)S(1)} %reduce_sum.126), channel_id=1, replica_groups=mesh['seq'=4,'seg'=4,'head'=2] {'seq','seg','head'}, use_global_device_ids=true, to_apply=%region_22.23 | all-reduce | flops 4096 | bytes 32768 | tf_op jit(solution)/shard_map/psum | solution.py:183
  (217 shorter events, 84.3 us)
Async XLA Ops:
  7.2 61.0 %all-gather.17.cloned.1.call-start = ((), (), s32[]{:S(2)}) async-start(), calls=%async_computation | async-start | bytes 1638400 | tf_op jit(solution)/shard_map/all_gather | solution.py:155
  35.8 0.7 copy-start.4
  36.6 66.9 %all-gather.19.cloned.1.call-start = ((), (), s32[]{:S(2)}) async-start(), calls=%async_computation.1 | async-start | bytes 1638400 | tf_op jit(solution)/shard_map/all_gather | solution.py:14
  68.1 40.9 %copy-start.2 = (f32[136,16]{1,0:T(8,128)S(1)}, f32[136,16]{1,0:T(8,128)}, u32[]{:S(2)}) copy-start(f32[136,16]{1,0:T(8,128)} %get-tuple-element.1252) | copy-start | bytes 26116
  68.1 40.9 %copy-start.3 = (f32[136,16]{1,0:T(8,128)S(1)}, f32[136,16]{1,0:T(8,128)}, u32[]{:S(2)}) copy-start(f32[136,16]{1,0:T(8,128)} %get-tuple-element.1254) | copy-start | bytes 26116
  68.1 40.9 %copy-start.5 = (f32[136]{0:T(256)S(1)}, f32[136]{0:T(256)}, u32[]{:S(2)}) copy-start(f32[136]{0:T(256)} %get-tuple-element.1271) | copy-start | bytes 1636
  70.5 165.0 %all-gather.21.cloned.1.call-start = ((), (), s32[]{:S(2)}) async-start(), calls=%async_computation.2 | async-start | bytes 1638400 | tf_op jit(solution)/shard_map/all_gather | solution.py:155
  114.3 3.4 copy-start
  119.6 3.9 %copy-start.1 = (f32[1024,1024]{0,1:T(8,128)S(1)}, f32[1024,1024]{0,1:T(8,128)}, u32[]{:S(2)}) copy-start(f32[1024,1024]{0,1:T(8,128)} %copy-done) | copy-start | bytes 12582916 | tf_op jit(solution)/shard_map/while
  123.5 1.9 copy-start.6
  127.4 6.3 %copy-start.7 = (bf16[4,16,1024]{2,1,0:T(8,128)(2,1)}, bf16[4,16,1024]{2,1,0:T(8,128)(2,1)S(1)}, u32[]{:S(2)}) copy-start(bf16[4,16,1024]{2,1,0:T(8,128)(2,1)S(1)} %fusion.217) | copy-start | bytes 393220 | tf_op jit(solution)/shard_map/while
  138.8 3.4 copy-start
  144.1 3.9 %copy-start.1 = (f32[1024,1024]{0,1:T(8,128)S(1)}, f32[1024,1024]{0,1:T(8,128)}, u32[]{:S(2)}) copy-start(f32[1024,1024]{0,1:T(8,128)} %copy-done) | copy-start | bytes 12582916 | tf_op jit(solution)/shard_map/while
  148.0 1.9 copy-start.6
  152.0 6.3 %copy-start.7 = (bf16[4,16,1024]{2,1,0:T(8,128)(2,1)}, bf16[4,16,1024]{2,1,0:T(8,128)(2,1)S(1)}, u32[]{:S(2)}) copy-start(bf16[4,16,1024]{2,1,0:T(8,128)(2,1)S(1)} %fusion.217) | copy-start | bytes 393220 | tf_op jit(solution)/shard_map/while
  163.3 3.4 copy-start
  168.6 3.9 %copy-start.1 = (f32[1024,1024]{0,1:T(8,128)S(1)}, f32[1024,1024]{0,1:T(8,128)}, u32[]{:S(2)}) copy-start(f32[1024,1024]{0,1:T(8,128)} %copy-done) | copy-start | bytes 12582916 | tf_op jit(solution)/shard_map/while
  172.5 1.9 copy-start.6
  176.5 6.3 %copy-start.7 = (bf16[4,16,1024]{2,1,0:T(8,128)(2,1)}, bf16[4,16,1024]{2,1,0:T(8,128)(2,1)S(1)}, u32[]{:S(2)}) copy-start(bf16[4,16,1024]{2,1,0:T(8,128)(2,1)S(1)} %fusion.217) | copy-start | bytes 393220 | tf_op jit(solution)/shard_map/while
  187.8 3.4 copy-start
  193.2 3.9 %copy-start.1 = (f32[1024,1024]{0,1:T(8,128)S(1)}, f32[1024,1024]{0,1:T(8,128)}, u32[]{:S(2)}) copy-start(f32[1024,1024]{0,1:T(8,128)} %copy-done) | copy-start | bytes 12582916 | tf_op jit(solution)/shard_map/while
  197.1 1.9 copy-start.6
  201.0 6.3 %copy-start.7 = (bf16[4,16,1024]{2,1,0:T(8,128)(2,1)}, bf16[4,16,1024]{2,1,0:T(8,128)(2,1)S(1)}, u32[]{:S(2)}) copy-start(bf16[4,16,1024]{2,1,0:T(8,128)(2,1)S(1)} %fusion.217) | copy-start | bytes 393220 | tf_op jit(solution)/shard_map/while
  207.6 63.2 %all-gather.23.cloned.1.call-start = ((), (), s32[]{:S(2)}) async-start(), calls=%async_computation.3 | async-start | bytes 1638400 | tf_op jit(solution)/shard_map/all_gather | solution.py:14
Sparse Core Ops, SparseCore 0:
  36.7 31.3 all-gather.16
  70.7 32.7 all-gather.18
  207.7 27.7 all-gather.20
  238.1 32.7 all-gather.22
where the time goes:
time: 347 us; the launch traced here: 345 us
  matrix products  140 us (40%)
  blocking collectives  83.4 us (24%)
  waiting for transfers between devices  80.6 us (23%)
  between operations  14 us (4%)
  other arithmetic  12.4 us (4%)
  local copies, waits for them, and re-layouts  12.3 us (4%)
    all_gather x2, waiting for transfers between devices, carried(): lax.all_gather(stacked[0], 'seq', axis=0, tiled=True)  59.4 us
    psum x1, blocking collectives, shards(): lax.psum((jnp.sum(grad_q, 0), jnp.sum(grad_k, 0)), ('seq', 'seg', 'head'))  39.8 us
    all_gather x2, blocking collectives, carried_in(): pieces = jax.tree.map(lambda part: lax.all_gather(part, axis), value)  27.4 us
    all_gather x2, waiting for transfers between devices, carried_in(): pieces = jax.tree.map(lambda part: lax.all_gather(part, axis), value)  21.2 us
    dot_general x4, matrix products, head_forward(): g_k = jnp.dot(q_t, g_scores, precision=highest)  16.6 us
    all_gather x2, blocking collectives, carried(): lax.all_gather(stacked[1], 'seq', axis=0, tiled=True)  16.3 us
    dot_general x4, matrix products, head_forward(): lax.dot_general(q_t, k_t, (((0,), (0,)), ((), ())), precision=highest)  15.3 us
    dot_general x8, matrix products, project(): lax.dot_general(weight_b, rows, (((0,), (1,)), ((), ())), preferred_eleme...  9.01 us
  transfers between devices with their start and end apart: 4, of which 4 were waited for; matrix products, arithmetic and copies ran while one was open for 0% of the time, Pallas kernels for 0%

commit v1 on v0

v1 whole, which is shorter than its diff:
```python
import functools
import math

import jax
import jax.numpy as jnp
import numpy as np
from jax import lax
from jax.experimental import pallas as pl
from jax.experimental.pallas import tpu as pltpu
from jax.sharding import PartitionSpec as P

f32 = jnp.float32
bf16 = jnp.bfloat16
HALF = 0.5**0.5
LANES = 128
NT = (((1,), (1,)), ((), ()))


class Dims:
    def __init__(self, width):
        self.width = width
        self.half = width // 2
        self.quad = width * (width + 1) // 2
        self.lin = self.quad
        self.const = self.quad + width
        self.feats = self.const + 1
        self.lanes = -(-self.feats // LANES) * LANES
        self.count_rows = self.lanes // LANES
        self.rows = -(-(self.feats + self.count_rows) // 8) * 8


def selections(dm):
    w = dm.width
    first = np.concatenate([np.tile(np.arange(w), dm.half), np.arange(dm.half)])
    shift = np.concatenate([np.repeat(np.arange(dm.half), w), np.full(dm.half, dm.half)])
    second = (first + shift) % w
    sel_a = np.zeros((w, dm.lanes), np.float32)
    sel_b = np.zeros((w, dm.lanes), np.float32)
    sel_a[first, np.arange(dm.quad)] = 1.0
    sel_b[second, np.arange(dm.quad)] = 1.0
    sel_a[np.arange(w), dm.lin + np.arange(w)] = 1.0
    table = np.zeros((8, dm.lanes), np.float32)
    table[0, dm.const] = 1.0
    table[1, dm.lin : dm.feats] = 1.0
    table[2, : dm.feats] = 1.0
    table[2, :w] = HALF
    rep = np.tile(np.eye(w, dtype=np.float32), (1, LANES // w))
    as_b = lambda a: jnp.asarray(a, bf16)
    return as_b(sel_a), as_b(sel_b), as_b(sel_b[:, : dm.quad].T), as_b(rep), jnp.asarray(table)


def dot(a, b, dims=(((1,), (0,)), ((), ()))):
    return lax.dot_general(a, b, dims, preferred_element_type=f32)


def split2(x):
    hi = x.astype(bf16)
    return hi, (x - hi.astype(f32)).astype(bf16)


def split3(x):
    hi = x.astype(bf16)
    rest = x - hi.astype(f32)
    mid = rest.astype(bf16)
    return hi, mid, (rest - mid.astype(f32)).astype(bf16)


def rolled(weight, sel_t):
    return dot(sel_t, weight, NT).astype(bf16)


def features_t(ext, dm):
    w = dm.width
    base = ext[:w]
    parts = [HALF * base * base]
    for d in range(1, dm.half):
        parts.append(ext[d * w : (d + 1) * w] * base)
    parts.append(ext[dm.half * w : dm.quad] * base[: dm.half])
    parts.append(base)
    tail = dm.rows - dm.const
    rows = lax.broadcasted_iota(jnp.int32, (tail, ext.shape[1]), 0)
    parts.append(jnp.where(rows == 0, 1.0, 0.0).astype(f32))
    return jnp.concatenate(parts, 0)


def features_rows(rows, weight, sel_a, sel_b, table):
    left = dot(rows, dot(weight, sel_a).astype(bf16)) + table[0:1]
    right = dot(rows, dot(weight, sel_b).astype(bf16)) + table[1:2]
    return table[2:3] * left * right


def feature_grad_t(ext, g, dm):
    w, half = dm.width, dm.half
    base = ext[:w]
    total = g[dm.lin : dm.lin + w] + (2.0 * HALF) * g[:w] * base
    for d in range(1, half):
        quad = g[d * w : (d + 1) * w]
        total = total + quad * ext[d * w : (d + 1) * w]
        back = quad * base
        total = total + jnp.concatenate([back[w - d :], back[: w - d]], 0)
    quad = g[half * w : dm.quad]
    return total + jnp.concatenate([quad * base[half:], quad * base[:half]], 0)


def with_count(state, count, dm):
    rows = lax.broadcasted_iota(jnp.int32, state.shape, 0)
    for c in range(dm.count_rows):
        state = jnp.where(rows == dm.feats + c, count[:, c * LANES : (c + 1) * LANES], state)
    return state


def count_of(state, dm):
    return jnp.concatenate([state[dm.feats + c : dm.feats + c + 1] for c in range(dm.count_rows)], 1)


def state_kernel(dm, k_ref, v_ref, wk_ref, selt_ref, out_ref):
    wk = wk_ref[...].astype(bf16)
    ext = dot(rolled(wk, selt_ref[...]), k_ref[0], NT)
    phi = features_t(ext, dm)
    state = dot(phi.astype(bf16), v_ref[0])
    part = phi[:, :LANES]
    for c in range(1, phi.shape[1] // LANES):
        part = part + phi[:, c * LANES : (c + 1) * LANES]
    count = lax.dot_general(
        jnp.ones((8, LANES), f32), part, NT, precision=lax.Precision.HIGHEST, preferred_element_type=f32
    )[0:1]
    count = jnp.concatenate([count, jnp.zeros((1, dm.lanes - dm.rows), f32)], 1)
    out_ref[0] = with_count(state, count, dm)


def packs(q, k, wq, wk, rep, selt, dm):
    w = dm.width
    q1, q2, q3 = split3(dot(q, dot(wq, rep).astype(bf16)))
    group = lax.broadcasted_iota(jnp.int32, (1, LANES), 1)
    zero = jnp.zeros((), bf16)

    def at(lo, hi):
        return (group >= lo * w) & (group < hi * w)

    q_pack = jnp.where(at(0, 3), q1, jnp.where(at(3, 5), q2, jnp.where(at(5, 6), q3, zero)))
    q_pack = jnp.where(group == 6 * w, jnp.ones((), bf16), q_pack)
    k_t = dot(rolled(wk, selt[:w]), k, NT)
    k1, k2, k3 = split3(k_t)
    rows = lax.broadcasted_iota(jnp.int32, (LANES - 6 * w, k_t.shape[1]), 0)
    last = jnp.where(rows == 0, 1.0, 0.0).astype(bf16)
    return q_pack, jnp.concatenate([k1, k2, k3, k1, k2, k1, last], 0), k1, k2


def intra_kernel(dm, tile, q_ref, k_ref, v_ref, wq_ref, wk_ref, rep_ref, selt_ref, numer_ref, denom_ref):
    q_pack, k_pack, _, _ = packs(
        q_ref[0], k_ref[0], wq_ref[...].astype(bf16), wk_ref[...].astype(bf16), rep_ref[...], selt_ref[...], dm
    )
    tokens = q_pack.shape[0]
    below = lax.broadcasted_iota(jnp.int32, (tile, tile), 0) >= lax.broadcasted_iota(jnp.int32, (tile, tile), 1)
    for i in range(tokens // tile):
        rows = slice(i * tile, (i + 1) * tile)
        numer = jnp.zeros((tile, v_ref.shape[2]), f32)
        denom = jnp.zeros((tile, LANES), f32)
        for j in range(i + 1):
            cols = slice(j * tile, (j + 1) * tile)
            t = dot(q_pack[rows], k_pack[:, cols])
            weight = (0.5 * t) * t + 0.5
            if j == i:
                weight = jnp.where(below, weight, 0.0)
            for c in range(tile // LANES):
                denom = denom + weight[:, c * LANES : (c + 1) * LANES]
            numer = numer + dot(weight.astype(bf16), v_ref[0, cols, :])
        numer_ref[0, rows, :] = numer
        denom_ref[0, rows, :] = denom


def gather_slots(me_ref, slots, scr):
    me = me_ref[0]
    size = slots[0].shape[0]
    for d, slot in enumerate(slots):
        scr[pl.ds(pl.multiple_of((me ^ d) * size, 8), size), :] = slot[...]


def head_rows(scr, dm):
    return scr[pl.ds(pl.multiple_of(pl.program_id(0) * dm.rows, 8), dm.rows), :]


def forward_kernel(
    dm, scale, n, me_ref, q_ref, wq_ref, sela_ref, selb_ref, selt_ref, table_ref, numer_ref, denom_ref, teacher_ref, *rest
):
    slots, (student_ref, g_ref, gd_ref, back_ref, scr) = rest[:n], rest[n:]

    @pl.when(pl.program_id(0) == 0)
    def _():
        gather_slots(me_ref, slots, scr)

    state = head_rows(scr, dm)
    wq = wq_ref[...].astype(bf16)
    q = q_ref[0]
    table = table_ref[...]
    phi = features_rows(q, wq, sela_ref[...], selb_ref[...], table)
    s1, s2 = split2(state)
    s_pack = jnp.concatenate([s1, s2], 1)
    s_pack = jnp.concatenate([s_pack, jnp.zeros((dm.lanes - dm.rows, s_pack.shape[1]), bf16)], 0)
    p1, p2 = split2(phi)
    prod = dot(p1, s_pack) + dot(p2, s_pack)
    hd = state.shape[1]
    numer = numer_ref[0] + (prod[:, :hd] + prod[:, hd:])
    weighted = phi * count_of(state, dm)
    part = denom_ref[0]
    for c in range(dm.lanes // LANES):
        part = part + weighted[:, c * LANES : (c + 1) * LANES]
    denom = jnp.sum(part, 1, keepdims=True)
    inv = 1.0 / denom
    y = numer * inv
    student_ref[0] = y.astype(bf16)
    g_out = scale * (y - teacher_ref[0].astype(f32))
    g_numer = g_out * inv
    g_denom = -jnp.sum(g_out * y, 1, keepdims=True) * inv
    g_ref[0] = g_numer
    gd_ref[0] = jnp.broadcast_to(g_denom, gd_ref.shape[1:])
    phi_t = features_t(dot(rolled(wq, selt_ref[...]), q, NT), dm)
    t1, t2 = split2(phi_t)
    g1, g2 = split2(g_numer)
    g_pack = jnp.concatenate([g1, g2], 1)
    prod = dot(t1, g_pack) + dot(t2, g_pack)
    back = prod[:, :hd] + prod[:, hd:]
    back_ref[0] = with_count(back, jnp.sum(phi * g_denom, 0, keepdims=True), dm)


def backward_kernel(
    dm, tile, n, me_ref, q_ref, k_ref, v_ref, wq_ref, wk_ref, rep_ref, selt_ref, g_ref, gd_ref, *rest
):
    slots, (gk_ref, wgrad_ref, scr) = rest[:n], rest[n:]

    @pl.when(pl.program_id(0) == 0)
    def _():
        gather_slots(me_ref, slots, scr)
        wgrad_ref[...] = jnp.zeros_like(wgrad_ref)

    state = head_rows(scr, dm)
    wq = wq_ref[...].astype(bf16)
    q = q_ref[0]
    selt = selt_ref[...]
    q_pack, k_pack, k1, k2 = packs(q, k_ref[0], wq, wk_ref[...].astype(bf16), rep_ref[...], selt, dm)
    k_two = jnp.concatenate([k1, k2], 0)
    ext = dot(rolled(wq, selt), q, NT)
    w = dm.width
    q1, q2 = split2(ext[:w])
    q_two = jnp.concatenate([q1, q2], 0)
    g_numer = g_ref[0]
    g_hi = g_numer.astype(bf16)
    tokens = q.shape[0]
    below = lax.broadcasted_iota(jnp.int32, (tile, tile), 0) >= lax.broadcasted_iota(jnp.int32, (tile, tile), 1)
    count = tokens // tile
    g_k = [jnp.zeros((w, tile), f32) for _ in range(count)]
    g_q = []
    for i in range(count):
        rows = slice(i * tile, (i + 1) * tile)
        gd = gd_ref[0, rows, :]
        gd = jnp.concatenate([gd] * (tile // LANES), 1)
        total = jnp.zeros((w, tile), f32)
        for j in range(i + 1):
            cols = slice(j * tile, (j + 1) * tile)
            t = dot(q_pack[rows], k_pack[:, cols])
            score = (dot(g_hi[rows], v_ref[0, cols, :], NT) + gd) * t
            if j == i:
                score = jnp.where(below, score, 0.0)
            hi, lo = split2(score)
            both = dot(k_two[:, cols], hi, NT)
            total = total + (both[:w] + both[w:]) + dot(k1[:, cols], lo, NT)
            both = dot(q_two[:, rows], hi)
            g_k[j] = g_k[j] + (both[:w] + both[w:]) + dot(q1[:, rows], lo)
        g_q.append(total)
    gk_ref[0] = jnp.concatenate(g_k, 1)
    row = lax.broadcasted_iota(jnp.int32, (dm.rows, dm.lanes), 0)
    lane = lax.broadcasted_iota(jnp.int32, (dm.rows, dm.lanes), 1)
    column = jnp.sum(jnp.where(row == lane, count_of(state, dm), 0.0), 1, keepdims=True)
    first = lax.broadcasted_iota(jnp.int32, (1, LANES), 1) == 0
    s_aug = jnp.concatenate([state, jnp.where(first, column, 0.0)], 1)
    g_aug = jnp.concatenate([g_numer, jnp.where(first, gd_ref[0], 0.0)], 1)
    s1, s2 = split2(s_aug)
    a1, a2 = split2(g_aug)
    both = dot(jnp.concatenate([s1, s2], 0), a1, NT)
    g_phi = both[: dm.rows] + both[dm.rows :] + dot(s1, a2, NT)
    total = jnp.concatenate(g_q, 1) + feature_grad_t(ext, g_phi, dm)
    wgrad_ref[...] += dot(total.astype(bf16), q)


def key_kernel(dm, n, me_ref, k_ref, v_ref, wk_ref, selt_ref, gk_ref, *rest):
    slots, (wgrad_ref, scr) = rest[:n], rest[n:]

    @pl.when(pl.program_id(0) == 0)
    def _():
        gather_slots(me_ref, slots, scr)
        wgrad_ref[...] = jnp.zeros_like(wgrad_ref)

    state = head_rows(scr, dm)
    k = k_ref[0]
    ext = dot(rolled(wk_ref[...].astype(bf16), selt_ref[...]), k, NT)
    row = lax.broadcasted_iota(jnp.int32, (dm.rows, dm.lanes), 0)
    lane = lax.broadcasted_iota(jnp.int32, (dm.rows, dm.lanes), 1)
    column = jnp.sum(jnp.where(row == lane, count_of(state, dm), 0.0), 1, keepdims=True)
    g_phi = dot(state.astype(bf16), v_ref[0], NT) + column
    total = gk_ref[0] + feature_grad_t(ext, g_phi, dm)
    wgrad_ref[...] += dot(total.astype(bf16), k)


VMEM_LIMIT = 24 * 1024 * 1024


def head_spec(array):
    return pl.BlockSpec((1,) + array.shape[1:], lambda h: (h, 0, 0))


def whole(array):
    return pl.BlockSpec(array.shape, lambda h: (0,) * array.ndim)


SMEM = pl.BlockSpec(memory_space=pltpu.SMEM)


def call(body, heads, args, specs, outs, out_specs, scratch, flops, name):
    moved = sum(math.prod(a.shape) * a.dtype.itemsize for a in list(args) + list(outs))
    return pl.pallas_call(
        body,
        grid=(heads,),
        in_specs=specs,
        out_specs=out_specs,
        out_shape=outs,
        scratch_shapes=scratch,
        compiler_params=pltpu.CompilerParams(
            dimension_semantics=("arbitrary",), vmem_limit_bytes=VMEM_LIMIT
        ),
        cost_estimate=pl.CostEstimate(flops=flops, bytes_accessed=moved, transcendentals=0),
        name=name,
    )(*args)


def shifted(array, axis, pairs):
    return lax.ppermute(array, axis, pairs)


def carried(local, backward):
    n, me = lax.axis_size("seq"), lax.axis_index("seq")
    size = local.shape[0] // n

    def swap(array, d):
        return array if d == 0 else shifted(array, "seq", [(i, i ^ d) for i in range(n)])

    got = [swap(lax.dynamic_slice_in_dim(local, (me ^ d) * size, size, 0), d) for d in range(n)]
    total = functools.reduce(jnp.add, got)
    before = []
    for d in range(n):
        order = me ^ d
        keep = [((me ^ e) > order) if backward else ((me ^ e) < order) for e in range(n)]
        before.append(functools.reduce(jnp.add, [jnp.where(k, g, 0.0) for k, g in zip(keep, got)]))
    m = lax.axis_size("seg")
    far = None
    for d in range(1, m):
        pairs = [(i, i - d) for i in range(d, m)] if backward else [(i, i + d) for i in range(m - d)]
        piece = shifted(total, "seg", pairs)
        far = piece if far is None else far + piece
    if far is not None:
        before = [b + far for b in before]
    return [swap(b, d) for d, b in enumerate(before)]


def summed(array):
    for axis in ("head", "seq", "seg"):
        n = lax.axis_size(axis)
        got = [shifted(array, axis, [(i, i ^ d) for i in range(n)]) for d in range(1, n)]
        array = functools.reduce(jnp.add, [array] + got)
    return array


def shards(queries, keys, values, teacher, query_proj, key_proj):
    heads, tokens, hd = queries.shape
    dm = Dims(query_proj.shape[1])
    n = lax.axis_size("seq")
    heads_all = heads * lax.axis_size("head")
    tokens_all = tokens * n * lax.axis_size("seg")
    scale = 1.0 / math.sqrt(heads_all * tokens_all)
    tile = min(256, tokens)
    sel_a, sel_b, sel_t, rep, table = selections(dm)
    me = jnp.reshape(lax.axis_index("seq").astype(jnp.int32), (1,))
    state_shape = jax.ShapeDtypeStruct((heads, dm.rows, hd), f32)
    tok_shape = jax.ShapeDtypeStruct((heads, tokens, hd), f32)
    lane_shape = jax.ShapeDtypeStruct((heads, tokens, LANES), f32)
    grad_shape = jax.ShapeDtypeStruct((dm.width, hd), f32)
    gk_shape = jax.ShapeDtypeStruct((heads, dm.width, tokens), f32)
    scratch = [pltpu.VMEM((heads * dm.rows, hd), f32)]
    square = heads * tokens * tokens

    states = call(
        functools.partial(state_kernel, dm),
        heads,
        (keys, values, key_proj, sel_t),
        [head_spec(keys), head_spec(values), whole(key_proj), whole(sel_t)],
        [state_shape],
        [head_spec(state_shape)],
        [],
        4 * heads * tokens * dm.rows * hd,
        "states",
    )[0]
    numer, denom = call(
        functools.partial(intra_kernel, dm, tile),
        heads,
        (queries, keys, values, query_proj, key_proj, rep, sel_t),
        [head_spec(queries), head_spec(keys), head_spec(values)]
        + [whole(a) for a in (query_proj, key_proj, rep, sel_t)],
        [tok_shape, lane_shape],
        [head_spec(tok_shape), head_spec(lane_shape)],
        [],
        4 * square * hd,
        "intra",
    )
    prev = carried(states.reshape(heads * dm.rows, hd), False)
    student, g_numer, g_denom, back = call(
        functools.partial(forward_kernel, dm, scale, n),
        heads,
        (me, queries, query_proj, sel_a, sel_b, sel_t, table, numer, denom, teacher, *prev),
        [SMEM, head_spec(queries)]
        + [whole(a) for a in (query_proj, sel_a, sel_b, sel_t, table)]
        + [head_spec(numer), head_spec(denom), head_spec(teacher)]
        + [whole(a) for a in prev],
        [jax.ShapeDtypeStruct(tok_shape.shape, bf16), tok_shape, lane_shape, state_shape],
        [head_spec(tok_shape), head_spec(tok_shape), head_spec(lane_shape), head_spec(state_shape)],
        scratch,
        8 * heads * tokens * dm.lanes * hd,
        "forward",
    )
    g_k, q_grad = call(
        functools.partial(backward_kernel, dm, tile, n),
        heads,
        (me, queries, keys, values, query_proj, key_proj, rep, sel_t, g_numer, g_denom, *prev),
        [SMEM, head_spec(queries), head_spec(keys), head_spec(values)]
        + [whole(a) for a in (query_proj, key_proj, rep, sel_t)]
        + [head_spec(g_numer), head_spec(g_denom)]
        + [whole(a) for a in prev],
        [gk_shape, grad_shape],
        [head_spec(gk_shape), whole(grad_shape)],
        scratch,
        8 * square * hd,
        "backward",
    )
    later = carried(back.reshape(heads * dm.rows, hd), True)
    k_grad = call(
        functools.partial(key_kernel, dm, n),
        heads,
        (me, keys, values, key_proj, sel_t, g_k, *later),
        [SMEM, head_spec(keys), head_spec(values), whole(key_proj), whole(sel_t), head_spec(g_k)]
        + [whole(a) for a in later],
        [grad_shape],
        [whole(grad_shape)],
        scratch,
        4 * heads * tokens * dm.rows * hd,
        "keygrad",
    )[0]
    grads = summed(jnp.concatenate([q_grad, k_grad], 0))
    return student, grads[: dm.width].T, grads[dm.width :].T


def solution(mesh):
    in_specs = (
        P("head", ("seg", "seq"), None),
        P("head", ("seg", "seq"), None),
        P("head", ("seg", "seq"), None),
        P("head", ("seg", "seq"), None),
        P(),
        P(),
    )
    out_specs = (P("head", ("seg", "seq"), None), P(), P())
    return jax.shard_map(shards, mesh=mesh, in_specs=in_specs, out_specs=out_specs, check_vma=False)
```

time: 347 us -> 123 us (0.35)
  matrix products: 140 us -> 0 us
  blocking collectives: 83.4 us -> 0 us
  waiting for transfers between devices: 80.6 us -> 24.8 us
  starting transfers between devices: 0.16 us -> 37.5 us
  Pallas kernels: 0 us -> 33.7 us
  between operations: 14 us -> 0.98 us
  local copies, waits for them, and re-layouts: 12.3 us -> 18.7 us
  other arithmetic: 12.4 us -> 6.49 us
    dot_general x104 -> x0, matrix products: 140 us -> none  [the longest x4 16.6 us: head_forward(): g_k = jnp.dot(q_t, g_scores, precision=highest)]
    all_gather x4 -> x0, waiting for transfers between devices: 80.6 us -> none  [the longest x2 59.4 us: carried(): lax.all_gather(stacked[0], 'seq', axis=0, tiled=True)]
    all_gather x4 -> x0, blocking collectives: 43.6 us -> none  [the longest x2 27.4 us: carried_in(): pieces = jax.tree.map(lambda part: lax.all_gather(part, axis), value)]
    psum x1 -> x0, blocking collectives: 39.8 us -> none  [shards(): lax.psum((jnp.sum(grad_q, 0), jnp.sum(grad_k, 0)), ('seq', 'seg', 'head'))]
    ppermute x0 -> x25, starting transfers between devices: none -> 37.5 us  [shifted(): return lax.ppermute(array, axis, pairs)]
    pallas_call x0 -> x5, Pallas kernels: none -> 33.7 us  [call(): pl.pallas_call(body, grid=(heads,), in_specs=specs, out_specs=out_specs,...]
    ppermute x0 -> x25, waiting for transfers between devices: none -> 24.8 us  [shifted(): return lax.ppermute(array, axis, pairs)]
    unnamed x8 -> x66, local copies, waits for them, and re-layouts: 0.73 us -> 17.4 us
  transfers between devices with their start and end apart: 4 -> 25, of which waited for: 4 -> 16; matrix products, arithmetic and copies ran while one was open for 0% -> 1% of each run, Pallas kernels for 0% -> 18%
where the time goes in v1:
time: 123 us; the launch traced here: 122 us
  starting transfers between devices  37.5 us (30%)
  Pallas kernels  33.7 us (27%)
  waiting for transfers between devices  24.8 us (20%)
  local copies, waits for them, and re-layouts  18.7 us (15%)
  other arithmetic  6.49 us (5%)
    ppermute x25, starting transfers between devices, shifted(): return lax.ppermute(array, axis, pairs)  37.5 us
    pallas_call x5, Pallas kernels, call(): pl.pallas_call(body, grid=(heads,), in_specs=specs, out_specs=out_specs,...  33.7 us
    ppermute x25, waiting for transfers between devices, shifted(): return lax.ppermute(array, axis, pairs)  24.8 us
    unnamed x66, local copies, waits for them, and re-layouts  17.4 us
    add x4, other arithmetic, carried(): before = [b + far for b in before]  4.17 us
  transfers between devices with their start and end apart: 25, of which 16 were waited for; matrix products, arithmetic and copies ran while one was open for 1% of the time, Pallas kernels for 18%

profile of v1, /device:TPU:0, one launch (start us, length us, event | category | flops | bytes accessed | tf_op | source)
XLA Modules:
  0.0 122.2 jit_solution(7739397084755150412)
XLA Ops:
  1.5 1.2 copy-done
  2.7 1.2 %copy-done.2 = bf16[4,1024,128]{2,1,0:T(8,128)(2,1)S(1)} copy-done((bf16[4,1024,128]{2,1,0:T(8,128)(2,1)S(1)}, bf16[4,1024,128]{2,1,0:T(8,128)(2,1)}, u32[]{:S(2)}) %copy-start.2) | copy-done | bytes 1048600
  4.7 2.8 %states.1 = f32[4,160,128]{2,1,0:T(8,128)S(1)} custom-call(bf16[4,1024,128]{2,1,0:T(8,128)(2,1)S(1)} %copy-done, bf16[4,1024,128]{2,1,0:T(8,128)(2,1)S(1)} %copy-done.2, f32[128,16]{1,0:T(8,128)S(1)} %copy.15.wk_ref, bf16[136,16]{1,0:T(8,128)(2,1)S(1)} %copy-done.8), custom_call_target="tpu_custom_call" | custom-call | flops 335544320 | bytes 2437376 | tf_op jit(solution)/shard_map/states/pallas_call | solution.py:320
  8.2 3.0 %collective-permute-start = (f32[160,128]{1,0:T(8,128)}, f32[160,128]{1,0:T(8,128)}, u32[]{:S(2)}, u32[]{:S(2)}) collective-permute-start(f32[160,128]{1,0:T(8,128)} %get-tuple-element.34), channel_id=1, source_target_pairs={{0,8},{8,0},{16,24},{24,16},{1,9},{9,1},{17,25},{25,17},{2,10},{10... | collective-permute-start | bytes 245768 | tf_op jit(solution)/shard_map/ppermute | solution.py:336
  11.2 1.5 %collective-permute-start.1 = (f32[160,128]{1,0:T(8,128)}, f32[160,128]{1,0:T(8,128)}, u32[]{:S(2)}, u32[]{:S(2)}) collective-permute-start(f32[160,128]{1,0:T(8,128)} %get-tuple-element.33), channel_id=1, source_target_pairs={{0,16},{8,24},{16,0},{24,8},{1,17},{9,25},{17,1},{25,9},{2,18},{10... | collective-permute-start | bytes 245768 | tf_op jit(solution)/shard_map/ppermute | solution.py:336
  12.7 1.5 %collective-permute-done = f32[160,128]{1,0:T(8,128)} collective-permute-done((f32[160,128]{1,0:T(8,128)}, f32[160,128]{1,0:T(8,128)}, u32[]{:S(2)}, u32[]{:S(2)}) %collective-permute-start) | collective-permute-done | bytes 81952 | tf_op jit(solution)/shard_map/ppermute | solution.py:336
  14.2 2.6 %collective-permute-done.1 = f32[160,128]{1,0:T(8,128)} collective-permute-done((f32[160,128]{1,0:T(8,128)}, f32[160,128]{1,0:T(8,128)}, u32[]{:S(2)}, u32[]{:S(2)}) %collective-permute-start.1) | collective-permute-done | bytes 81952 | tf_op jit(solution)/shard_map/ppermute | solution.py:336
  16.8 1.5 %collective-permute-done.2 = f32[160,128]{1,0:T(8,128)} collective-permute-done((f32[160,128]{1,0:T(8,128)}, f32[160,128]{1,0:T(8,128)}, u32[]{:S(2)}, u32[]{:S(2)}) %collective-permute-start.2) | collective-permute-done | bytes 81952 | tf_op jit(solution)/shard_map/ppermute | solution.py:336
  18.4 1.6 %add_add_fusion.10 = f32[160,128]{1,0:T(8,128)} fusion(f32[160,128]{1,0:T(8,128)} %collective-permute-done.2, f32[160,128]{1,0:T(8,128)} %collective-permute-done.1, f32[160,128]{1,0:T(8,128)} %collective-permute-done, f32[640,128]{1,0:T(8,128)S(1)} %bitcast.8, s32[]{:T(128)S(6)} %select_n.187), kind=kLoop, calls=%fused_computation.10 | loop fusion | flops 61440 | bytes 409604 | tf_op jit(solution)/shard_map/add | solution.py:347
  20.0 4.1 %collective-permute-start.3 = (f32[160,128]{1,0:T(8,128)}, f32[160,128]{1,0:T(8,128)}, u32[]{:S(2)}, u32[]{:S(2)}) collective-permute-start(f32[160,128]{1,0:T(8,128)} %add_add_fusion.10), channel_id=1, source_target_pairs={{0,2},{2,4},{4,6},{1,3},{3,5},{5,7},{8,10},{10,12},{12,14},{9,11},... | collective-permute-start | bytes 245768 | tf_op jit(solution)/shard_map/ppermute | solution.py:336
  24.1 4.5 %collective-permute-start.4 = (f32[160,128]{1,0:T(8,128)}, f32[160,128]{1,0:T(8,128)}, u32[]{:S(2)}, u32[]{:S(2)}) collective-permute-start(f32[160,128]{1,0:T(8,128)} %add_add_fusion.10), channel_id=1, source_target_pairs={{0,4},{2,6},{1,5},{3,7},{8,12},{10,14},{9,13},{11,15},{16,20},{18,... | collective-permute-start | bytes 245768 | tf_op jit(solution)/shard_map/ppermute | solution.py:336
  28.6 1.9 %collective-permute-start.5 = (f32[160,128]{1,0:T(8,128)}, f32[160,128]{1,0:T(8,128)}, u32[]{:S(2)}, u32[]{:S(2)}) collective-permute-start(f32[160,128]{1,0:T(8,128)} %add_add_fusion.10), channel_id=1, source_target_pairs={{0,6},{1,7},{8,14},{9,15},{16,22},{17,23},{24,30},{25,31}} | collective-permute-start | bytes 245768 | tf_op jit(solution)/shard_map/ppermute | solution.py:336
  31.3 1.0 collective-permute-done.5
  32.3 1.1 add_add_fusion.6
  33.3 1.0 add_add_fusion.7
  35.6 2.3 %collective-permute-start.8 = (f32[160,128]{1,0:T(8,128)S(1)}, f32[160,128]{1,0:T(8,128)S(1)}, u32[]{:S(2)}, u32[]{:S(2)}) collective-permute-start(f32[160,128]{1,0:T(8,128)S(1)} %get-tuple-element.21), channel_id=1, source_target_pairs={{0,24},{8,16},{16,8},{24,0},{1,25},{9,17},{17,9},{25,1},{2,26},{10... | collective-permute-start | bytes 245768 | tf_op jit(solution)/shard_map/ppermute | solution.py:336
  39.6 6.3 %intra.1 = (f32[4,1024,128]{2,1,0:T(8,128)S(1)}, f32[4,1024,128]{2,1,0:T(8,128)S(1)}) custom-call(bf16[4,1024,128]{2,1,0:T(8,128)(2,1)S(1)} %copy-done.5, bf16[4,1024,128]{2,1,0:T(8,128)(2,1)S(1)} %copy-done.1, bf16[4,1024,128]{2,1,0:T(8,128)(2,1)S(1)} %copy-done.3, f32[128,16]{1,0:T(8,128)S(1)} %copy-done.11, f32[128,16]{1,0:T(8,128)S(1)} %copy.15.wk_ref, ...), custom_call_target="tpu_custom_call" | custom-call | flops 2147483648 | bytes 7364864 | tf_op jit(solution)/shard_map/intra/pallas_call | solution.py:320
  46.0 6.8 %forward.1 = (bf16[4,1024,128]{2,1,0:T(8,128)(2,1)}, f32[4,1024,128]{2,1,0:T(8,128)S(1)}, f32[4,1024,128]{2,1,0:T(8,128)S(1)}, f32[4,160,128]{2,1,0:T(8,128)S(1)}) custom-call(s32[1]{0:T(128)} %bitcast.me_ref, bf16[4,1024,128]{2,1,0:T(8,128)(2,1)S(1)} %copy-done.5, f32[128,16]{1,0:T(8,128)S(1)} %copy-done.12, bf16[16,256]{1,0:T(8,128)(2,1)S(1)} %copy-done.20, ...), custom_call_target="tpu_custom_call" | custom-call | flops 1073741824 | bytes 12226820 | tf_op jit(solution)/shard_map/forward/pallas_call | solution.py:320
  52.9 1.3 %copy-done.23 = f32[4,1024,128]{2,1,0:T(8,128)} copy-done((f32[4,1024,128]{2,1,0:T(8,128)}, f32[4,1024,128]{2,1,0:T(8,128)S(1)}, u32[]{:S(2)}) %copy-start.23) | copy-done | bytes 2097176
  54.2 1.4 %copy-done.25 = f32[4,1024,128]{2,1,0:T(8,128)} copy-done((f32[4,1024,128]{2,1,0:T(8,128)}, f32[4,1024,128]{2,1,0:T(8,128)S(1)}, u32[]{:S(2)}) %copy-start.25) | copy-done | bytes 2097176
  56.2 1.4 %collective-permute-start.11 = (f32[160,128]{1,0:T(8,128)S(1)}, f32[160,128]{1,0:T(8,128)S(1)}, u32[]{:S(2)}, u32[]{:S(2)}) collective-permute-start(f32[160,128]{1,0:T(8,128)S(1)} %get-tuple-element.29), channel_id=1, source_target_pairs={{0,24},{8,16},{16,8},{24,0},{1,25},{9,17},{17,9},{25,1},{2,26},{10... | collective-permute-start | bytes 245768 | tf_op jit(solution)/shard_map/ppermute | solution.py:336
  57.6 1.5 %collective-permute-start.9 = (f32[160,128]{1,0:T(8,128)S(1)}, f32[160,128]{1,0:T(8,128)S(1)}, u32[]{:S(2)}, u32[]{:S(2)}) collective-permute-start(f32[160,128]{1,0:T(8,128)S(1)} %get-tuple-element.31), channel_id=1, source_target_pairs={{0,8},{8,0},{16,24},{24,16},{1,9},{9,1},{17,25},{25,17},{2,10},{10... | collective-permute-start | bytes 245768 | tf_op jit(solution)/shard_map/ppermute | solution.py:336
  59.1 1.0 collective-permute-done.10
  60.1 1.4 %collective-permute-done.11 = f32[160,128]{1,0:T(8,128)S(1)} collective-permute-done((f32[160,128]{1,0:T(8,128)S(1)}, f32[160,128]{1,0:T(8,128)S(1)}, u32[]{:S(2)}, u32[]{:S(2)}) %collective-permute-start.11) | collective-permute-done | bytes 81952 | tf_op jit(solution)/shard_map/ppermute | solution.py:336
  61.5 0.9 collective-permute-done.9
  63.1 1.3 %collective-permute-start.12 = (f32[160,128]{1,0:T(8,128)}, f32[160,128]{1,0:T(8,128)}, u32[]{:S(2)}, u32[]{:S(2)}) collective-permute-start(f32[160,128]{1,0:T(8,128)} %add_add_fusion.4), channel_id=1, source_target_pairs={{2,0},{4,2},{6,4},{3,1},{5,3},{7,5},{10,8},{12,10},{14,12},{11,9},... | collective-permute-start | bytes 245768 | tf_op jit(solution)/shard_map/ppermute | solution.py:336
  64.4 1.3 %collective-permute-start.13 = (f32[160,128]{1,0:T(8,128)}, f32[160,128]{1,0:T(8,128)}, u32[]{:S(2)}, u32[]{:S(2)}) collective-permute-start(f32[160,128]{1,0:T(8,128)} %add_add_fusion.4), channel_id=1, source_target_pairs={{4,0},{6,2},{5,1},{7,3},{12,8},{14,10},{13,9},{15,11},{20,16},{22,... | collective-permute-start | bytes 245768 | tf_op jit(solution)/shard_map/ppermute | solution.py:336
  65.7 1.3 %collective-permute-start.14 = (f32[160,128]{1,0:T(8,128)}, f32[160,128]{1,0:T(8,128)}, u32[]{:S(2)}, u32[]{:S(2)}) collective-permute-start(f32[160,128]{1,0:T(8,128)} %add_add_fusion.4), channel_id=1, source_target_pairs={{6,0},{7,1},{14,8},{15,9},{22,16},{23,17},{30,24},{31,25}} | collective-permute-start | bytes 245768 | tf_op jit(solution)/shard_map/ppermute | solution.py:336
  67.0 3.5 %collective-permute-done.12 = f32[160,128]{1,0:T(8,128)} collective-permute-done((f32[160,128]{1,0:T(8,128)}, f32[160,128]{1,0:T(8,128)}, u32[]{:S(2)}, u32[]{:S(2)}) %collective-permute-start.12) | collective-permute-done | bytes 81952 | tf_op jit(solution)/shard_map/ppermute | solution.py:336
  70.5 1.5 %collective-permute-done.13 = f32[160,128]{1,0:T(8,128)} collective-permute-done((f32[160,128]{1,0:T(8,128)}, f32[160,128]{1,0:T(8,128)}, u32[]{:S(2)}, u32[]{:S(2)}) %collective-permute-start.13) | collective-permute-done | bytes 81952 | tf_op jit(solution)/shard_map/ppermute | solution.py:336
  72.0 4.0 %collective-permute-done.14 = f32[160,128]{1,0:T(8,128)} collective-permute-done((f32[160,128]{1,0:T(8,128)}, f32[160,128]{1,0:T(8,128)}, u32[]{:S(2)}, u32[]{:S(2)}) %collective-permute-start.14) | collective-permute-done | bytes 81952 | tf_op jit(solution)/shard_map/ppermute | solution.py:336
  76.0 1.0 add_add_fusion
  77.0 1.0 add_add_fusion.1
  78.0 1.3 %collective-permute-start.15 = (f32[160,128]{1,0:T(8,128)S(1)}, f32[160,128]{1,0:T(8,128)S(1)}, u32[]{:S(2)}, u32[]{:S(2)}) collective-permute-start(f32[160,128]{1,0:T(8,128)S(1)} %get-tuple-element.24), channel_id=1, source_target_pairs={{0,8},{8,0},{16,24},{24,16},{1,9},{9,1},{17,25},{25,17},{2,10},{10... | collective-permute-start | bytes 245768 | tf_op jit(solution)/shard_map/ppermute | solution.py:336
  79.8 1.7 %collective-permute-start.17 = (f32[160,128]{1,0:T(8,128)S(1)}, f32[160,128]{1,0:T(8,128)S(1)}, u32[]{:S(2)}, u32[]{:S(2)}) collective-permute-start(f32[160,128]{1,0:T(8,128)S(1)} %get-tuple-element.19), channel_id=1, source_target_pairs={{0,24},{8,16},{16,8},{24,0},{1,25},{9,17},{17,9},{25,1},{2,26},{10... | collective-permute-start | bytes 245768 | tf_op jit(solution)/shard_map/ppermute | solution.py:336
  81.6 0.9 copy-done.7
  84.0 0.9 copy-done.15
  86.7 1.6 %copy-done.24 = f32[4,1024,128]{2,1,0:T(8,128)S(1)} copy-done((f32[4,1024,128]{2,1,0:T(8,128)S(1)}, f32[4,1024,128]{2,1,0:T(8,128)}, u32[]{:S(2)}) %copy-start.24) | copy-done | bytes 2097176
  88.3 1.6 %copy-done.26 = f32[4,1024,128]{2,1,0:T(8,128)S(1)} copy-done((f32[4,1024,128]{2,1,0:T(8,128)S(1)}, f32[4,1024,128]{2,1,0:T(8,128)}, u32[]{:S(2)}) %copy-start.26) | copy-done | bytes 2097176
  89.9 15.2 %backward.1 = (f32[4,16,1024]{2,1,0:T(8,128)S(1)}, f32[16,128]{1,0:T(8,128)S(1)}) custom-call(s32[1]{0:T(128)} %bitcast.me_ref, bf16[4,1024,128]{2,1,0:T(8,128)(2,1)S(1)} %copy-done.5, bf16[4,1024,128]{2,1,0:T(8,128)(2,1)S(1)} %copy-done.1, bf16[4,1024,128]{2,1,0:T(8,128)(2,1)S(1)} %copy-done.3, f32[128,16]{1,0:T(8,128)S(1)} %copy-done.13, ...), custom_call_target="tpu_custom_call" | custom-call | flops 4294967296 | bytes 7962884 | tf_op jit(solution)/shard_map/backward/pallas_call | solution.py:320
  105.1 2.6 %keygrad.1 = f32[16,128]{1,0:T(8,128)S(1)} custom-call(s32[1]{0:T(128)} %bitcast.me_ref, bf16[4,1024,128]{2,1,0:T(8,128)(2,1)S(1)} %copy-done.1, bf16[4,1024,128]{2,1,0:T(8,128)(2,1)S(1)} %copy-done.3, f32[128,16]{1,0:T(8,128)S(1)} %copy.15.wk_ref, bf16[136,16]{1,0:T(8,128)(2,1)S(1)} %copy-done.10, f32[4,16,1024]{2,1,0:T(8,128)S(1)} %get-tuple-element.17.gk_ref, ...), custom_call_target="tpu_custom_call" | custom-call | flops 335544320 | bytes 2707716 | tf_op jit(solution)/shard_map/keygrad/pallas_call | solution.py:320
  107.8 1.2 collective-permute-done.18
  108.9 1.2 collective-permute-start.19
  110.7 1.7 %collective-permute-start.21 = (f32[32,128]{1,0:T(8,128)S(1)}, f32[32,128]{1,0:T(8,128)S(1)}, u32[]{:S(2)}, u32[]{:S(2)}) collective-permute-start(f32[32,128]{1,0:T(8,128)S(1)} %fusion), channel_id=1, source_target_pairs={{0,24},{8,16},{16,8},{24,0},{1,25},{9,17},{17,9},{25,1},{2,26},{10... | collective-permute-start | bytes 49160 | tf_op jit(solution)/shard_map/ppermute | solution.py:336
  112.7 1.2 collective-permute-done.20
  113.9 1.4 %collective-permute-done.21 = f32[32,128]{1,0:T(8,128)S(1)} collective-permute-done((f32[32,128]{1,0:T(8,128)S(1)}, f32[32,128]{1,0:T(8,128)S(1)}, u32[]{:S(2)}, u32[]{:S(2)}) %collective-permute-start.21) | collective-permute-done | bytes 16416 | tf_op jit(solution)/shard_map/ppermute | solution.py:336
  115.5 4.2 %collective-permute-start.24 = (f32[32,128]{1,0:T(8,128)S(1)}, f32[32,128]{1,0:T(8,128)S(1)}, u32[]{:S(2)}, u32[]{:S(2)}) collective-permute-start(f32[32,128]{1,0:T(8,128)S(1)} %add_add_fusion.13), channel_id=1, source_target_pairs={{0,6},{2,4},{4,2},{6,0},{1,7},{3,5},{5,3},{7,1},{8,14},{10,12},{12... | collective-permute-start | bytes 49160 | tf_op jit(solution)/shard_map/ppermute | solution.py:336
  120.0 1.6 %collective-permute-done.24 = f32[32,128]{1,0:T(8,128)S(1)} collective-permute-done((f32[32,128]{1,0:T(8,128)S(1)}, f32[32,128]{1,0:T(8,128)S(1)}, u32[]{:S(2)}, u32[]{:S(2)}) %collective-permute-start.24) | collective-permute-done | bytes 16416 | tf_op jit(solution)/shard_map/ppermute | solution.py:336
  (86 shorter events, 13.2 us)
Async XLA Ops:
  0.6 29.9 %copy-start.31 = (f32[128,16]{0,1:T(8,128)S(1)}, f32[128,16]{0,1:T(8,128)}, u32[]{:S(2)}) copy-start(f32[128,16]{0,1:T(8,128)} %param.15) | copy-start | bytes 24580
  1.5 1.2 %copy-start = (bf16[4,1024,128]{2,1,0:T(8,128)(2,1)S(1)}, bf16[4,1024,128]{2,1,0:T(8,128)(2,1)}, u32[]{:S(2)}) copy-start(bf16[4,1024,128]{2,1,0:T(8,128)(2,1)} %k_ref.7) | copy-start | bytes 3145732
  2.7 1.2 %copy-start.2 = (bf16[4,1024,128]{2,1,0:T(8,128)(2,1)S(1)}, bf16[4,1024,128]{2,1,0:T(8,128)(2,1)}, u32[]{:S(2)}) copy-start(bf16[4,1024,128]{2,1,0:T(8,128)(2,1)} %v_ref.7) | copy-start | bytes 3145732
  4.7 33.3 %copy-start.1 = (bf16[4,1024,128]{2,1,0:T(8,128)(2,1)S(1)}, bf16[4,1024,128]{2,1,0:T(8,128)(2,1)}, u32[]{:S(2)}) copy-start(bf16[4,1024,128]{2,1,0:T(8,128)(2,1)} %k_ref.7) | copy-start | bytes 3145732
  4.7 33.3 %copy-start.3 = (bf16[4,1024,128]{2,1,0:T(8,128)(2,1)S(1)}, bf16[4,1024,128]{2,1,0:T(8,128)(2,1)}, u32[]{:S(2)}) copy-start(bf16[4,1024,128]{2,1,0:T(8,128)(2,1)} %v_ref.7) | copy-start | bytes 3145732
  4.7 33.3 %copy-start.5 = (bf16[4,1024,128]{2,1,0:T(8,128)(2,1)S(1)}, bf16[4,1024,128]{2,1,0:T(8,128)(2,1)}, u32[]{:S(2)}) copy-start(bf16[4,1024,128]{2,1,0:T(8,128)(2,1)} %q_ref.5) | copy-start | bytes 3145732
  4.7 33.3 %copy-start.27 = (bf16[16,128]{1,0:T(8,128)(2,1)S(1)}, bf16[16,128]{1,0:T(8,128)(2,1)}, u32[]{:S(2)}) copy-start(bf16[16,128]{1,0:T(8,128)(2,1)} %constant.39.clone.rep_ref) | copy-start | bytes 12292
  8.2 6.0 %collective-permute-start = (f32[160,128]{1,0:T(8,128)}, f32[160,128]{1,0:T(8,128)}, u32[]{:S(2)}, u32[]{:S(2)}) collective-permute-start(f32[160,128]{1,0:T(8,128)} %get-tuple-element.34), channel_id=1, source_target_pairs={{0,8},{8,0},{16,24},{24,16},{1,9},{9,1},{17,25},{25,17},{2,10},{10... | collective-permute-start | bytes 245768 | tf_op jit(solution)/shard_map/ppermute | solution.py:336
  11.2 5.6 %collective-permute-start.1 = (f32[160,128]{1,0:T(8,128)}, f32[160,128]{1,0:T(8,128)}, u32[]{:S(2)}, u32[]{:S(2)}) collective-permute-start(f32[160,128]{1,0:T(8,128)} %get-tuple-element.33), channel_id=1, source_target_pairs={{0,16},{8,24},{16,0},{24,8},{1,17},{9,25},{17,1},{25,9},{2,18},{10... | collective-permute-start | bytes 245768 | tf_op jit(solution)/shard_map/ppermute | solution.py:336
  12.7 5.7 %collective-permute-start.2 = (f32[160,128]{1,0:T(8,128)}, f32[160,128]{1,0:T(8,128)}, u32[]{:S(2)}, u32[]{:S(2)}) collective-permute-start(f32[160,128]{1,0:T(8,128)} %get-tuple-element.32), channel_id=1, source_target_pairs={{0,24},{8,16},{16,8},{24,0},{1,25},{9,17},{17,9},{25,1},{2,26},{10... | collective-permute-start | bytes 245768 | tf_op jit(solution)/shard_map/ppermute | solution.py:336
  20.0 11.2 %collective-permute-start.3 = (f32[160,128]{1,0:T(8,128)}, f32[160,128]{1,0:T(8,128)}, u32[]{:S(2)}, u32[]{:S(2)}) collective-permute-start(f32[160,128]{1,0:T(8,128)} %add_add_fusion.10), channel_id=1, source_target_pairs={{0,2},{2,4},{4,6},{1,3},{3,5},{5,7},{8,10},{10,12},{12,14},{9,11},... | collective-permute-start | bytes 245768 | tf_op jit(solution)/shard_map/ppermute | solution.py:336
  24.1 7.2 %collective-permute-start.4 = (f32[160,128]{1,0:T(8,128)}, f32[160,128]{1,0:T(8,128)}, u32[]{:S(2)}, u32[]{:S(2)}) collective-permute-start(f32[160,128]{1,0:T(8,128)} %add_add_fusion.10), channel_id=1, source_target_pairs={{0,4},{2,6},{1,5},{3,7},{8,12},{10,14},{9,13},{11,15},{16,20},{18,... | collective-permute-start | bytes 245768 | tf_op jit(solution)/shard_map/ppermute | solution.py:336
  28.6 3.6 %collective-permute-start.5 = (f32[160,128]{1,0:T(8,128)}, f32[160,128]{1,0:T(8,128)}, u32[]{:S(2)}, u32[]{:S(2)}) collective-permute-start(f32[160,128]{1,0:T(8,128)} %add_add_fusion.10), channel_id=1, source_target_pairs={{0,6},{1,7},{8,14},{9,15},{16,22},{17,23},{24,30},{25,31}} | collective-permute-start | bytes 245768 | tf_op jit(solution)/shard_map/ppermute | solution.py:336
  34.4 11.6 %copy-start.6 = (f32[160,128]{1,0:T(8,128)}, f32[160,128]{1,0:T(8,128)S(1)}, u32[]{:S(2)}) copy-start(f32[160,128]{1,0:T(8,128)S(1)} %get-tuple-element.27.rest_0_) | copy-start | bytes 245764
  34.4 11.5 %collective-permute-start.6 = (f32[160,128]{1,0:T(8,128)S(1)}, f32[160,128]{1,0:T(8,128)S(1)}, u32[]{:S(2)}, u32[]{:S(2)}) collective-permute-start(f32[160,128]{1,0:T(8,128)S(1)} %get-tuple-element.26), channel_id=1, source_target_pairs={{0,8},{8,0},{16,24},{24,16},{1,9},{9,1},{17,25},{25,17},{2,10},{10... | collective-permute-start | bytes 245768 | tf_op jit(solution)/shard_map/ppermute | solution.py:336
  35.0 11.0 %collective-permute-start.7 = (f32[160,128]{1,0:T(8,128)S(1)}, f32[160,128]{1,0:T(8,128)S(1)}, u32[]{:S(2)}, u32[]{:S(2)}) collective-permute-start(f32[160,128]{1,0:T(8,128)S(1)} %get-tuple-element.25), channel_id=1, source_target_pairs={{0,16},{8,24},{16,0},{24,8},{1,17},{9,25},{17,1},{25,9},{2,18},{10... | collective-permute-start | bytes 245768 | tf_op jit(solution)/shard_map/ppermute | solution.py:336
  35.6 10.3 %copy-start.4 = (bf16[4,1024,128]{2,1,0:T(8,128)(2,1)S(1)}, bf16[4,1024,128]{2,1,0:T(8,128)(2,1)}, u32[]{:S(2)}) copy-start(bf16[4,1024,128]{2,1,0:T(8,128)(2,1)} %teacher_ref.1) | copy-start | bytes 3145732
  35.6 10.3 %collective-permute-start.8 = (f32[160,128]{1,0:T(8,128)S(1)}, f32[160,128]{1,0:T(8,128)S(1)}, u32[]{:S(2)}, u32[]{:S(2)}) collective-permute-start(f32[160,128]{1,0:T(8,128)S(1)} %get-tuple-element.21), channel_id=1, source_target_pairs={{0,24},{8,16},{16,8},{24,0},{1,25},{9,17},{17,9},{25,1},{2,26},{10... | collective-permute-start | bytes 245768 | tf_op jit(solution)/shard_map/ppermute | solution.py:336
  39.6 6.4 %copy-start.12 = (f32[128,16]{1,0:T(8,128)S(1)}, f32[128,16]{1,0:T(8,128)}, u32[]{:S(2)}) copy-start(f32[128,16]{1,0:T(8,128)} %copy.17.wq_ref) | copy-start | bytes 24580
  39.6 6.4 %copy-start.20 = (bf16[16,256]{1,0:T(8,128)(2,1)S(1)}, bf16[16,256]{1,0:T(8,128)(2,1)}, u32[]{:S(2)}) copy-start(bf16[16,256]{1,0:T(8,128)(2,1)} %constant.36.clone.sela_ref) | copy-start | bytes 24580
  39.6 6.4 %copy-start.21 = (bf16[16,256]{1,0:T(8,128)(2,1)S(1)}, bf16[16,256]{1,0:T(8,128)(2,1)}, u32[]{:S(2)}) copy-start(bf16[16,256]{1,0:T(8,128)(2,1)} %constant.37.clone.selb_ref) | copy-start | bytes 24580
  39.6 6.4 %copy-start.22 = (f32[8,256]{1,0:T(8,128)S(1)}, f32[8,256]{1,0:T(8,128)}, u32[]{:S(2)}) copy-start(f32[8,256]{1,0:T(8,128)} %constant.40.clone.table_ref) | copy-start | bytes 24580
  45.9 6.9 %copy-start.14 = (f32[160,128]{1,0:T(8,128)}, f32[160,128]{1,0:T(8,128)S(1)}, u32[]{:S(2)}) copy-start(f32[160,128]{1,0:T(8,128)S(1)} %collective-permute-done.6.rest_1_) | copy-start | bytes 245764
  45.9 6.9 %copy-start.16 = (f32[160,128]{1,0:T(8,128)}, f32[160,128]{1,0:T(8,128)S(1)}, u32[]{:S(2)}) copy-start(f32[160,128]{1,0:T(8,128)S(1)} %collective-permute-done.7.rest_2_) | copy-start | bytes 245764
  45.9 6.9 %copy-start.18 = (f32[160,128]{1,0:T(8,128)}, f32[160,128]{1,0:T(8,128)S(1)}, u32[]{:S(2)}) copy-start(f32[160,128]{1,0:T(8,128)S(1)} %collective-permute-done.8.rest_3_) | copy-start | bytes 245764
  52.9 1.3 %copy-start.23 = (f32[4,1024,128]{2,1,0:T(8,128)}, f32[4,1024,128]{2,1,0:T(8,128)S(1)}, u32[]{:S(2)}) copy-start(f32[4,1024,128]{2,1,0:T(8,128)S(1)} %get-tuple-element.14.g_ref) | copy-start | bytes 6291460
  54.2 1.4 %copy-start.25 = (f32[4,1024,128]{2,1,0:T(8,128)}, f32[4,1024,128]{2,1,0:T(8,128)S(1)}, u32[]{:S(2)}) copy-start(f32[4,1024,128]{2,1,0:T(8,128)S(1)} %get-tuple-element.15.gd_ref) | copy-start | bytes 6291460
  55.6 4.5 %collective-permute-start.10 = (f32[160,128]{1,0:T(8,128)S(1)}, f32[160,128]{1,0:T(8,128)S(1)}, u32[]{:S(2)}, u32[]{:S(2)}) collective-permute-start(f32[160,128]{1,0:T(8,128)S(1)} %get-tuple-element.30), channel_id=1, source_target_pairs={{0,16},{8,24},{16,0},{24,8},{1,17},{9,25},{17,1},{25,9},{2,18},{10... | collective-permute-start | bytes 245768 | tf_op jit(solution)/shard_map/ppermute | solution.py:336
  56.2 5.3 %collective-permute-start.11 = (f32[160,128]{1,0:T(8,128)S(1)}, f32[160,128]{1,0:T(8,128)S(1)}, u32[]{:S(2)}, u32[]{:S(2)}) collective-permute-start(f32[160,128]{1,0:T(8,128)S(1)} %get-tuple-element.29), channel_id=1, source_target_pairs={{0,24},{8,16},{16,8},{24,0},{1,25},{9,17},{17,9},{25,1},{2,26},{10... | collective-permute-start | bytes 245768 | tf_op jit(solution)/shard_map/ppermute | solution.py:336
  57.6 4.8 %collective-permute-start.9 = (f32[160,128]{1,0:T(8,128)S(1)}, f32[160,128]{1,0:T(8,128)S(1)}, u32[]{:S(2)}, u32[]{:S(2)}) collective-permute-start(f32[160,128]{1,0:T(8,128)S(1)} %get-tuple-element.31), channel_id=1, source_target_pairs={{0,8},{8,0},{16,24},{24,16},{1,9},{9,1},{17,25},{25,17},{2,10},{10... | collective-permute-start | bytes 245768 | tf_op jit(solution)/shard_map/ppermute | solution.py:336
  60.1 2.3 %copy-start.28 = (f32[160,128]{1,0:T(8,128)}, f32[160,128]{1,0:T(8,128)S(1)}, u32[]{:S(2)}) copy-start(f32[160,128]{1,0:T(8,128)S(1)} %collective-permute-done.10) | copy-start | bytes 245764
  61.5 2.9 %copy-start.30 = (f32[160,128]{1,0:T(8,128)}, f32[160,128]{1,0:T(8,128)S(1)}, u32[]{:S(2)}) copy-start(f32[160,128]{1,0:T(8,128)S(1)} %collective-permute-done.11) | copy-start | bytes 245764
  63.1 7.4 %collective-permute-start.12 = (f32[160,128]{1,0:T(8,128)}, f32[160,128]{1,0:T(8,128)}, u32[]{:S(2)}, u32[]{:S(2)}) collective-permute-start(f32[160,128]{1,0:T(8,128)} %add_add_fusion.4), channel_id=1, source_target_pairs={{2,0},{4,2},{6,4},{3,1},{5,3},{7,5},{10,8},{12,10},{14,12},{11,9},... | collective-permute-start | bytes 245768 | tf_op jit(solution)/shard_map/ppermute | solution.py:336
  64.4 7.6 %collective-permute-start.13 = (f32[160,128]{1,0:T(8,128)}, f32[160,128]{1,0:T(8,128)}, u32[]{:S(2)}, u32[]{:S(2)}) collective-permute-start(f32[160,128]{1,0:T(8,128)} %add_add_fusion.4), channel_id=1, source_target_pairs={{4,0},{6,2},{5,1},{7,3},{12,8},{14,10},{13,9},{15,11},{20,16},{22,... | collective-permute-start | bytes 245768 | tf_op jit(solution)/shard_map/ppermute | solution.py:336
  65.7 10.2 %collective-permute-start.14 = (f32[160,128]{1,0:T(8,128)}, f32[160,128]{1,0:T(8,128)}, u32[]{:S(2)}, u32[]{:S(2)}) collective-permute-start(f32[160,128]{1,0:T(8,128)} %add_add_fusion.4), channel_id=1, source_target_pairs={{6,0},{7,1},{14,8},{15,9},{22,16},{23,17},{30,24},{31,25}} | collective-permute-start | bytes 245768 | tf_op jit(solution)/shard_map/ppermute | solution.py:336
  78.0 27.1 %collective-permute-start.15 = (f32[160,128]{1,0:T(8,128)S(1)}, f32[160,128]{1,0:T(8,128)S(1)}, u32[]{:S(2)}, u32[]{:S(2)}) collective-permute-start(f32[160,128]{1,0:T(8,128)S(1)} %get-tuple-element.24), channel_id=1, source_target_pairs={{0,8},{8,0},{16,24},{24,16},{1,9},{9,1},{17,25},{25,17},{2,10},{10... | collective-permute-start | bytes 245768 | tf_op jit(solution)/shard_map/ppermute | solution.py:336
  79.3 25.8 %collective-permute-start.16 = (f32[160,128]{1,0:T(8,128)S(1)}, f32[160,128]{1,0:T(8,128)S(1)}, u32[]{:S(2)}, u32[]{:S(2)}) collective-permute-start(f32[160,128]{1,0:T(8,128)S(1)} %get-tuple-element.23), channel_id=1, source_target_pairs={{0,16},{8,24},{16,0},{24,8},{1,17},{9,25},{17,1},{25,9},{2,18},{10... | collective-permute-start | bytes 245768 | tf_op jit(solution)/shard_map/ppermute | solution.py:336
  79.8 25.3 %collective-permute-start.17 = (f32[160,128]{1,0:T(8,128)S(1)}, f32[160,128]{1,0:T(8,128)S(1)}, u32[]{:S(2)}, u32[]{:S(2)}) collective-permute-start(f32[160,128]{1,0:T(8,128)S(1)} %get-tuple-element.19), channel_id=1, source_target_pairs={{0,24},{8,16},{16,8},{24,0},{1,25},{9,17},{17,9},{25,1},{2,26},{10... | collective-permute-start | bytes 245768 | tf_op jit(solution)/shard_map/ppermute | solution.py:336
  81.6 0.9 copy-start.7
  86.7 1.6 %copy-start.24 = (f32[4,1024,128]{2,1,0:T(8,128)S(1)}, f32[4,1024,128]{2,1,0:T(8,128)}, u32[]{:S(2)}) copy-start(f32[4,1024,128]{2,1,0:T(8,128)} %copy-done.23) | copy-start | bytes 6291460
  88.3 1.6 %copy-start.26 = (f32[4,1024,128]{2,1,0:T(8,128)S(1)}, f32[4,1024,128]{2,1,0:T(8,128)}, u32[]{:S(2)}) copy-start(f32[4,1024,128]{2,1,0:T(8,128)} %copy-done.25) | copy-start | bytes 6291460
  107.7 1.2 %collective-permute-start.18 = (f32[32,128]{1,0:T(8,128)S(1)}, f32[32,128]{1,0:T(8,128)S(1)}, u32[]{:S(2)}, u32[]{:S(2)}) collective-permute-start(f32[32,128]{1,0:T(8,128)S(1)} %pad_maximum_fusion), channel_id=1, source_target_pairs={{0,1},{1,0},{2,3},{3,2},{4,5},{5,4},{6,7},{7,6},{8,9},{9,8},{10,11... | collective-permute-start | bytes 49160 | tf_op jit(solution)/shard_map/ppermute | solution.py:336
  108.9 3.7 %collective-permute-start.19 = (f32[32,128]{1,0:T(8,128)S(1)}, f32[32,128]{1,0:T(8,128)S(1)}, u32[]{:S(2)}, u32[]{:S(2)}) collective-permute-start(f32[32,128]{1,0:T(8,128)S(1)} %fusion), channel_id=1, source_target_pairs={{0,8},{8,0},{16,24},{24,16},{1,9},{9,1},{17,25},{25,17},{2,10},{10... | collective-permute-start | bytes 49160 | tf_op jit(solution)/shard_map/ppermute | solution.py:336
  110.1 3.8 %collective-permute-start.20 = (f32[32,128]{1,0:T(8,128)S(1)}, f32[32,128]{1,0:T(8,128)S(1)}, u32[]{:S(2)}, u32[]{:S(2)}) collective-permute-start(f32[32,128]{1,0:T(8,128)S(1)} %fusion), channel_id=1, source_target_pairs={{0,16},{8,24},{16,0},{24,8},{1,17},{9,25},{17,1},{25,9},{2,18},{10... | collective-permute-start | bytes 49160 | tf_op jit(solution)/shard_map/ppermute | solution.py:336
  110.7 4.6 %collective-permute-start.21 = (f32[32,128]{1,0:T(8,128)S(1)}, f32[32,128]{1,0:T(8,128)S(1)}, u32[]{:S(2)}, u32[]{:S(2)}) collective-permute-start(f32[32,128]{1,0:T(8,128)S(1)} %fusion), channel_id=1, source_target_pairs={{0,24},{8,16},{16,8},{24,0},{1,25},{9,17},{17,9},{25,1},{2,26},{10... | collective-permute-start | bytes 49160 | tf_op jit(solution)/shard_map/ppermute | solution.py:336
  115.3 4.4 %collective-permute-start.22 = (f32[32,128]{1,0:T(8,128)S(1)}, f32[32,128]{1,0:T(8,128)S(1)}, u32[]{:S(2)}, u32[]{:S(2)}) collective-permute-start(f32[32,128]{1,0:T(8,128)S(1)} %add_add_fusion.13), channel_id=1, source_target_pairs={{0,2},{2,0},{4,6},{6,4},{1,3},{3,1},{5,7},{7,5},{8,10},{10,8},{12,... | collective-permute-start | bytes 49160 | tf_op jit(solution)/shard_map/ppermute | solution.py:336
  115.3 4.7 %collective-permute-start.23 = (f32[32,128]{1,0:T(8,128)S(1)}, f32[32,128]{1,0:T(8,128)S(1)}, u32[]{:S(2)}, u32[]{:S(2)}) collective-permute-start(f32[32,128]{1,0:T(8,128)S(1)} %add_add_fusion.13), channel_id=1, source_target_pairs={{0,4},{2,6},{4,0},{6,2},{1,5},{3,7},{5,1},{7,3},{8,12},{10,14},{12... | collective-permute-start | bytes 49160 | tf_op jit(solution)/shard_map/ppermute | solution.py:336
  115.5 6.1 %collective-permute-start.24 = (f32[32,128]{1,0:T(8,128)S(1)}, f32[32,128]{1,0:T(8,128)S(1)}, u32[]{:S(2)}, u32[]{:S(2)}) collective-permute-start(f32[32,128]{1,0:T(8,128)S(1)} %add_add_fusion.13), channel_id=1, source_target_pairs={{0,6},{2,4},{4,2},{6,0},{1,7},{3,5},{5,3},{7,1},{8,14},{10,12},{12... | collective-permute-start | bytes 49160 | tf_op jit(solution)/shard_map/ppermute | solution.py:336
  (9 other events, 7.3 us)

commit v2 on v1

v2 whole, which is shorter than its diff:
```python
import functools
import math

import jax
import jax.numpy as jnp
from jax import lax
from jax.experimental import pallas as pl
from jax.experimental.pallas import tpu as pltpu
from jax.sharding import PartitionSpec as P

f32 = jnp.float32
bf16 = jnp.bfloat16
HALF = 0.5**0.5
LANES = 128
NT = (((1,), (1,)), ((), ()))


class Dims:
    def __init__(self, width):
        self.width = width
        self.half = width // 2
        self.shift = width.bit_length() - 1
        assert width == 1 << self.shift
        self.quad = width * (width + 1) // 2
        self.lin = self.quad
        self.const = self.quad + width
        self.feats = self.const + 1
        self.lanes = -(-self.feats // LANES) * LANES
        self.count_rows = self.lanes // LANES
        self.rows = -(-(self.feats + self.count_rows) // 8) * 8


def positions(shape, dim):
    return lax.broadcasted_iota(jnp.int32, shape, dim)


def one_hot(hit):
    return jnp.where(hit, 1.0, 0.0).astype(bf16)


def first_of(dm, f):
    return jnp.where(f < dm.quad, f & (dm.width - 1), f - dm.lin)


def second_of(dm, f):
    return (f + (f >> dm.shift)) & (dm.width - 1)


def dot(a, b, dims=(((1,), (0,)), ((), ()))):
    return lax.dot_general(a, b, dims, preferred_element_type=f32)


def split2(x):
    hi = x.astype(bf16)
    return hi, (x - hi.astype(f32)).astype(bf16)


def split3(x):
    hi = x.astype(bf16)
    rest = x - hi.astype(f32)
    mid = rest.astype(bf16)
    return hi, mid, (rest - mid.astype(f32)).astype(bf16)


def rolled(w_t, dm):
    shape = (dm.quad, dm.width)
    return dot(one_hot(second_of(dm, positions(shape, 0)) == positions(shape, 1)), w_t).astype(bf16)


def repeated(w_t, dm):
    shape = (LANES, dm.width)
    return dot(one_hot((positions(shape, 0) & (dm.width - 1)) == positions(shape, 1)), w_t).astype(bf16)


def sides(w_t, dm):
    shape = (dm.lanes, dm.width)
    f, j = positions(shape, 0), positions(shape, 1)
    left = dot(one_hot(first_of(dm, f) == j), w_t).astype(bf16)
    right = dot(one_hot((f < dm.quad) & (second_of(dm, f) == j)), w_t).astype(bf16)
    return left, right


def features_t(ext, dm):
    w = dm.width
    base = ext[:w]
    parts = [HALF * base * base]
    for d in range(1, dm.half):
        parts.append(ext[d * w : (d + 1) * w] * base)
    parts.append(ext[dm.half * w : dm.quad] * base[: dm.half])
    parts.append(base)
    tail = dm.rows - dm.const
    rows = lax.broadcasted_iota(jnp.int32, (tail, ext.shape[1]), 0)
    parts.append(jnp.where(rows == 0, 1.0, 0.0).astype(f32))
    return jnp.concatenate(parts, 0)


def features_rows(rows, w_t, dm):
    left, right = sides(w_t, dm)
    f = positions((1, dm.lanes), 1)
    left = dot(rows, left, NT) + jnp.where(f == dm.const, 1.0, 0.0)
    right = dot(rows, right, NT) + jnp.where((f >= dm.lin) & (f < dm.feats), 1.0, 0.0)
    return jnp.where(f < dm.width, HALF, 1.0) * left * right


def feature_grad_t(ext, g, dm):
    w, half = dm.width, dm.half
    base = ext[:w]
    total = g[dm.lin : dm.lin + w] + (2.0 * HALF) * g[:w] * base
    for d in range(1, half):
        quad = g[d * w : (d + 1) * w]
        total = total + quad * ext[d * w : (d + 1) * w]
        back = quad * base
        total = total + jnp.concatenate([back[w - d :], back[: w - d]], 0)
    quad = g[half * w : dm.quad]
    return total + jnp.concatenate([quad * base[half:], quad * base[:half]], 0)


def with_count(state, count, dm):
    rows = lax.broadcasted_iota(jnp.int32, state.shape, 0)
    for c in range(dm.count_rows):
        state = jnp.where(rows == dm.feats + c, count[:, c * LANES : (c + 1) * LANES], state)
    return state


def count_of(state, dm):
    return jnp.concatenate([state[dm.feats + c : dm.feats + c + 1] for c in range(dm.count_rows)], 1)


def state_kernel(dm, n, me_ref, *rest):
    sources, slots, kept, scr, sems, last = rest[:6], rest[6 : 6 + n], rest[6 + n : 12 + n], *rest[12 + n :]
    k_hbm, v_hbm, q_hbm, t_hbm, wk_hbm, wq_hbm = sources
    k_ref, v_ref, q_ref, t_ref, wk_ref, wq_ref = kept
    heads = k_ref.shape[0]
    first = pltpu.make_async_copy(wk_hbm, wk_ref, last.at[0])
    keys = [pltpu.make_async_copy(k_hbm.at[h], k_ref.at[h], sems.at[h]) for h in range(heads)]
    values = [pltpu.make_async_copy(v_hbm.at[h], v_ref.at[h], sems.at[heads + h]) for h in range(heads)]
    others = [
        pltpu.make_async_copy(wq_hbm, wq_ref, last.at[1]),
        pltpu.make_async_copy(q_hbm, q_ref, last.at[2]),
        pltpu.make_async_copy(t_hbm, t_ref, last.at[3]),
    ]
    first.start()
    for h in range(heads):
        keys[h].start()
        values[h].start()
    for copy in others:
        copy.start()
    first.wait()
    w_ext = rolled(wk_ref[...].astype(bf16), dm)
    for h in range(heads):
        keys[h].wait()
        phi = features_t(dot(w_ext, k_ref[h], NT), dm)
        values[h].wait()
        state = dot(phi.astype(bf16), v_ref[h])
        part = phi[:, :LANES]
        for c in range(1, phi.shape[1] // LANES):
            part = part + phi[:, c * LANES : (c + 1) * LANES]
        count = lax.dot_general(
            jnp.ones((8, LANES), f32), part, NT, precision=lax.Precision.HIGHEST, preferred_element_type=f32
        )[0:1]
        count = jnp.concatenate([count, jnp.zeros((1, dm.lanes - dm.rows), f32)], 1)
        scr[h * dm.rows : (h + 1) * dm.rows, :] = with_count(state, count, dm)
    scatter_slots(me_ref, slots, scr)
    for copy in others:
        copy.wait()


def packs(q, k, wq, wk, dm):
    w = dm.width
    q1, q2, q3 = split3(dot(q, repeated(wq, dm), NT))
    group = positions((1, LANES), 1)
    zero = jnp.zeros((), bf16)

    def at(lo, hi):
        return (group >= lo * w) & (group < hi * w)

    q_pack = jnp.where(at(0, 3), q1, jnp.where(at(3, 5), q2, jnp.where(at(5, 6), q3, zero)))
    q_pack = jnp.where(group == 6 * w, jnp.ones((), bf16), q_pack)
    k_t = dot(wk, k, NT)
    k1, k2, k3 = split3(k_t)
    last = one_hot(positions((LANES - 6 * w, k_t.shape[1]), 0) == 0)
    return q_pack, jnp.concatenate([k1, k2, k3, k1, k2, k1, last], 0), k1, k2


def intra_kernel(dm, tile, h0, q_ref, k_ref, v_ref, wq_ref, wk_ref, numer_ref, denom_ref, phi_ref, phi_t_ref):
    h = pl.program_id(0)
    q, k, v = q_ref[h0 + h], k_ref[h0 + h], v_ref.at[h0 + h]
    wq = wq_ref[...].astype(bf16)
    phi_ref[h] = features_rows(q, wq, dm)
    phi_t_ref[h] = features_t(dot(rolled(wq, dm), q, NT), dm)
    q_pack, k_pack, _, _ = packs(q, k, wq, wk_ref[...].astype(bf16), dm)
    tokens = q_pack.shape[0]
    below = positions((tile, tile), 0) >= positions((tile, tile), 1)
    for i in range(tokens // tile):
        rows = slice(i * tile, (i + 1) * tile)
        numer = jnp.zeros((tile, v.shape[1]), f32)
        denom = jnp.zeros((tile, LANES), f32)
        for j in range(i + 1):
            cols = slice(j * tile, (j + 1) * tile)
            t = dot(q_pack[rows], k_pack[:, cols])
            weight = (0.5 * t) * t + 0.5
            if j == i:
                weight = jnp.where(below, weight, 0.0)
            for c in range(tile // LANES):
                denom = denom + weight[:, c * LANES : (c + 1) * LANES]
            numer = numer + dot(weight.astype(bf16), v[cols])
        numer_ref[h, rows, :] = numer
        denom_ref[h, rows, :] = denom


def gather_slots(me_ref, slots, scr):
    me = me_ref[0]
    size = slots[0].shape[0]
    for d, slot in enumerate(slots):
        scr[pl.ds(pl.multiple_of((me ^ d) * size, 8), size), :] = slot[...]


def scatter_slots(me_ref, slots, scr):
    size = slots[0].shape[0]
    for d, slot in enumerate(slots):
        slot[...] = scr[pl.ds(pl.multiple_of((me_ref[0] ^ d) * size, 8), size), :]


def join_kernel(n, backward, me_ref, *refs):
    far, got, outs = refs[: -2 * n], refs[-2 * n : -n], refs[-n:]

    def before(a, b):
        return a > b if backward else a < b

    me, mine = me_ref[0], me_ref[1]
    outer = jnp.zeros(outs[0].shape, f32)
    for d, piece in enumerate(far, 1):
        outer = outer + jnp.where(before(mine ^ d, mine), piece[...], 0.0)
    for d, out in enumerate(outs):
        total = outer
        for e, piece in enumerate(got):
            if e != d:
                total = total + jnp.where(before(me ^ e, me ^ d), piece[...], 0.0)
        out[...] = total


def head_rows(scr, dm, h):
    start = h * dm.rows
    return scr[pl.ds(start if isinstance(h, int) else pl.multiple_of(start, 8), dm.rows), :]


def forward_kernel(dm, scale, n, parts, me_ref, t_ref, *rest):
    intra, rest = rest[: 4 * len(parts)], rest[4 * len(parts) :]
    slots, (student_ref, g_ref, gd_ref), backs = rest[:n], rest[n : n + 3], rest[n + 3 : 2 * n + 3]
    scr, back_scr = rest[2 * n + 3 :]
    gather_slots(me_ref, slots, scr)
    for p, (h0, count) in enumerate(parts):
        for i in range(count):
            numer, denom, phi, phi_t = [ref[i] for ref in intra[4 * p : 4 * p + 4]]
            outs = forward_head(dm, scale, head_rows(scr, dm, h0 + i), t_ref[h0 + i], numer, denom, phi, phi_t)
            for ref, value in zip((student_ref, g_ref, gd_ref), outs):
                ref[h0 + i] = value
            back_scr[(h0 + i) * dm.rows : (h0 + i + 1) * dm.rows, :] = outs[3]
    scatter_slots(me_ref, backs, back_scr)


def forward_head(dm, scale, state, teacher, numer, part, phi, phi_t):
    hd = state.shape[1]
    s_pack = jnp.concatenate(split2(state), 1)
    s_pack = jnp.concatenate([s_pack, jnp.zeros((dm.lanes - dm.rows, 2 * hd), bf16)], 0)
    p1, p2 = split2(phi)
    prod = dot(p1, s_pack) + dot(p2, s_pack)
    numer = numer + (prod[:, :hd] + prod[:, hd:])
    weighted = phi * count_of(state, dm)
    for c in range(dm.lanes // LANES):
        part = part + weighted[:, c * LANES : (c + 1) * LANES]
    inv = 1.0 / jnp.sum(part, 1, keepdims=True)
    y = numer * inv
    g_out = scale * (y - teacher.astype(f32))
    g_numer = g_out * inv
    g_denom = -jnp.sum(g_out * y, 1, keepdims=True) * inv
    t1, t2 = split2(phi_t)
    g_pack = jnp.concatenate(split2(g_numer), 1)
    prod = dot(t1, g_pack) + dot(t2, g_pack)
    back = with_count(prod[:, :hd] + prod[:, hd:], jnp.sum(phi * g_denom, 0, keepdims=True), dm)
    return y.astype(bf16), g_numer, jnp.broadcast_to(g_denom, part.shape), back


def count_column(state, dm):
    row, lane = positions((dm.rows, dm.lanes), 0), positions((dm.rows, dm.lanes), 1)
    return jnp.sum(jnp.where(row == lane, count_of(state, dm), 0.0), 1, keepdims=True)


def backward_kernel(dm, tile, n, h0, me_ref, q_ref, k_ref, v_ref, wq_ref, wk_ref, g_ref, gd_ref, *rest):
    slots, (gk_ref, wgrad_ref, scr) = rest[:n], rest[n:]
    h = h0 + pl.program_id(0)
    q, k, v = q_ref[h], k_ref[h], v_ref.at[h]

    @pl.when(pl.program_id(0) == 0)
    def _():
        gather_slots(me_ref, slots, scr)
        wgrad_ref[...] = jnp.zeros_like(wgrad_ref)

    state = head_rows(scr, dm, h)
    wq = wq_ref[...].astype(bf16)
    q_pack, k_pack, k1, k2 = packs(q, k, wq, wk_ref[...].astype(bf16), dm)
    k_two = jnp.concatenate([k1, k2], 0)
    ext = dot(rolled(wq, dm), q, NT)
    w = dm.width
    q1, q2 = split2(ext[:w])
    q_two = jnp.concatenate([q1, q2], 0)
    g_numer = g_ref[h]
    g_hi = g_numer.astype(bf16)
    tokens = q.shape[0]
    below = positions((tile, tile), 0) >= positions((tile, tile), 1)
    count = tokens // tile
    g_k = [jnp.zeros((w, tile), f32) for _ in range(count)]
    g_q = []
    for i in range(count):
        rows = slice(i * tile, (i + 1) * tile)
        gd = gd_ref[h, rows, :]
        gd = jnp.concatenate([gd] * (tile // LANES), 1)
        total = jnp.zeros((w, tile), f32)
        for j in range(i + 1):
            cols = slice(j * tile, (j + 1) * tile)
            t = dot(q_pack[rows], k_pack[:, cols])
            score = (dot(g_hi[rows], v[cols], NT) + gd) * t
            if j == i:
                score = jnp.where(below, score, 0.0)
            hi, lo = split2(score)
            both = dot(k_two[:, cols], hi, NT)
            total = total + (both[:w] + both[w:]) + dot(k1[:, cols], lo, NT)
            both = dot(q_two[:, rows], hi)
            g_k[j] = g_k[j] + (both[:w] + both[w:]) + dot(q1[:, rows], lo)
        g_q.append(total)
    gk_ref[pl.program_id(0)] = jnp.concatenate(g_k, 1)
    first = positions((1, LANES), 1) == 0
    s_aug = jnp.concatenate([state, jnp.where(first, count_column(state, dm), 0.0)], 1)
    g_aug = jnp.concatenate([g_numer, jnp.where(first, gd_ref[h], 0.0)], 1)
    s1, s2 = split2(s_aug)
    a1, a2 = split2(g_aug)
    both = dot(jnp.concatenate([s1, s2], 0), a1, NT)
    g_phi = both[: dm.rows] + both[dm.rows :] + dot(s1, a2, NT)
    total = jnp.concatenate(g_q, 1) + feature_grad_t(ext, g_phi, dm)
    wgrad_ref[...] += dot(total.astype(bf16), q)


def key_kernel(dm, n, parts, me_ref, k_ref, v_ref, wk_ref, *rest):
    slots, backs, (out_ref, scr) = rest[:n], rest[n:-2], rest[-2:]
    gather_slots(me_ref, slots, scr)
    w = dm.width
    out_ref[:w] = functools.reduce(jnp.add, [g[...] for g in backs[1::2]])
    w_ext = rolled(wk_ref[...].astype(bf16), dm)
    grad = jnp.zeros((w, out_ref.shape[1]), f32)
    for (h0, count), gk_ref in zip(parts, backs[::2]):
        for i in range(count):
            k, v = k_ref[h0 + i], v_ref[h0 + i]
            state = head_rows(scr, dm, h0 + i)
            g_phi = dot(state.astype(bf16), v, NT) + count_column(state, dm)
            total = gk_ref[i] + feature_grad_t(dot(w_ext, k, NT), g_phi, dm)
            grad = grad + dot(total.astype(bf16), k)
    out_ref[w:] = grad


VMEM_LIMIT = 20 * 1024 * 1024
HBM = pl.BlockSpec(memory_space=pltpu.HBM)
VMEM = pl.BlockSpec(memory_space=pltpu.VMEM)
SMEM = pl.BlockSpec(memory_space=pltpu.SMEM)


def placed(args, specs):
    spaces = {id(HBM): pltpu.HBM, id(VMEM): pltpu.VMEM}
    return [
        pltpu.with_memory_space_constraint(a, spaces[id(s)]) if id(s) in spaces else a
        for a, s in zip(args, specs)
    ]


def call(body, grid, args, specs, outs, out_specs, scratch, flops):
    return pl.pallas_call(
        body,
        grid=grid,
        in_specs=specs,
        out_specs=out_specs,
        out_shape=outs,
        scratch_shapes=scratch,
        compiler_params=pltpu.CompilerParams(
            dimension_semantics=("arbitrary",) * len(grid), vmem_limit_bytes=VMEM_LIMIT
        ),
        cost_estimate=pl.CostEstimate(flops=flops, bytes_accessed=0, transcendentals=0),
    )(*placed(args, specs))


def shifted(array, axis, pairs):
    return lax.ppermute(array, axis, pairs)


def exchange(parts, axis):
    n = lax.axis_size(axis)
    got = []
    for d, part in enumerate(parts):
        got.append(part if d == 0 else shifted(part, axis, [(i, i ^ d) for i in range(n)]))
    return got


def carried(me, parts, backward):
    n, m = lax.axis_size("seq"), lax.axis_size("seg")
    got = exchange(parts, "seq")
    total = functools.reduce(jnp.add, got)
    far = exchange([total] * m, "seg")[1:]
    shape = pltpu.VMEM(parts[0].shape, f32)
    before = call(
        functools.partial(join_kernel, n, backward),
        (),
        (me, *far, *got),
        [SMEM] + [VMEM] * (n + m - 1),
        [shape] * n,
        [VMEM] * n,
        [],
        parts[0].size * n * n,
    )
    return exchange(before, "seq")


def summed(array):
    for axis in ("head", "seq", "seg"):
        n = lax.axis_size(axis)
        got = [shifted(array, axis, [(i, i ^ d) for i in range(n)]) for d in range(1, n)]
        array = functools.reduce(jnp.add, [array] + got)
    return array


INTRA_SPLIT = (2, 2)
BACK_SPLIT = (1, 2, 1)


def split_heads(heads, split):
    if heads % sum(split):
        return [(0, heads)]
    unit, at, out = heads // sum(split), 0, []
    for part in split:
        out.append((at, part * unit))
        at += part * unit
    return out


def shards(queries, keys, values, teacher, query_proj, key_proj):
    heads, tokens, hd = queries.shape
    dm = Dims(query_proj.shape[1])
    n = lax.axis_size("seq")
    heads_all = heads * lax.axis_size("head")
    tokens_all = tokens * n * lax.axis_size("seg")
    scale = 1.0 / math.sqrt(heads_all * tokens_all)
    tile = min(256, tokens)
    wq, wk = query_proj.T, key_proj.T
    me = jnp.stack([lax.axis_index("seq"), lax.axis_index("seg")]).astype(jnp.int32)
    slot_shape = pltpu.VMEM((heads * dm.rows // n, hd), f32)
    tok_shape = pltpu.VMEM((heads, tokens, hd), f32)
    lane_shape = pltpu.VMEM((heads, tokens, LANES), f32)
    grad_shape = pltpu.VMEM((dm.width, hd), f32)
    slots = [pltpu.VMEM((heads * dm.rows, hd), f32)]

    sources = (keys, values, queries, teacher, wk, wq)
    called = call(
        functools.partial(state_kernel, dm, n),
        (),
        (me, *sources),
        [SMEM] + [HBM] * len(sources),
        [slot_shape] * n + [pltpu.VMEM(a.shape, a.dtype) for a in sources],
        [VMEM] * (n + len(sources)),
        slots + [pltpu.SemaphoreType.DMA((2 * heads,)), pltpu.SemaphoreType.DMA((4,))],
        4 * heads * tokens * dm.rows * hd,
    )
    states, (keys, values, queries, teacher, wk, wq) = called[:n], called[n:]
    intra = []
    intra_parts = split_heads(heads, INTRA_SPLIT)
    for h0, count in intra_parts:
        shapes = [
            pltpu.VMEM((count, tokens, hd), f32),
            pltpu.VMEM((count, tokens, LANES), f32),
            pltpu.VMEM((count, tokens, dm.lanes), f32),
            pltpu.VMEM((count, dm.rows, tokens), f32),
        ]
        intra += call(
            functools.partial(intra_kernel, dm, tile, h0),
            (count,),
            (queries, keys, values, wq, wk),
            [VMEM] * 5,
            shapes,
            [VMEM] * len(shapes),
            [],
            4 * count * tokens * tokens * hd,
        )
    prev = carried(me, states, False)
    student, g_numer, g_denom, *back = call(
        functools.partial(forward_kernel, dm, scale, n, intra_parts),
        (),
        (me, teacher, *intra, *prev),
        [SMEM] + [VMEM] * (1 + len(intra) + n),
        [pltpu.VMEM((heads, tokens, hd), bf16), tok_shape, lane_shape] + [slot_shape] * n,
        [VMEM] * (3 + n),
        2 * slots,
        8 * heads * tokens * dm.lanes * hd,
    )
    backs = []
    back_parts = split_heads(heads, BACK_SPLIT)
    for h0, count in back_parts:
        backs += call(
            functools.partial(backward_kernel, dm, tile, n, h0),
            (count,),
            (me, queries, keys, values, wq, wk, g_numer, g_denom, *prev),
            [SMEM] + [VMEM] * (7 + n),
            [pltpu.VMEM((count, dm.width, tokens), f32), grad_shape],
            [VMEM, VMEM],
            slots,
            8 * count * tokens * tokens * hd,
        )
    later = carried(me, back, True)
    grads = call(
        functools.partial(key_kernel, dm, n, back_parts),
        (),
        (me, keys, values, wk, *later, *backs),
        [SMEM] + [VMEM] * (3 + n + len(backs)),
        [pltpu.VMEM((2 * dm.width, hd), f32)],
        [VMEM],
        slots,
        4 * heads * tokens * dm.rows * hd,
    )[0]
    grads = summed(grads)
    return student, grads[: dm.width].T, grads[dm.width :].T


def solution(mesh):
    in_specs = (
        P("head", ("seg", "seq"), None),
        P("head", ("seg", "seq"), None),
        P("head", ("seg", "seq"), None),
        P("head", ("seg", "seq"), None),
        P(),
        P(),
    )
    out_specs = (P("head", ("seg", "seq"), None), P(), P())
    return jax.shard_map(shards, mesh=mesh, in_specs=in_specs, out_specs=out_specs, check_vma=False)
```

time: 123 us -> 84.9 us (0.69)
  local copies, waits for them, and re-layouts: 18.7 us -> 1.58 us
  waiting for transfers between devices: 24.8 us -> 11.7 us
  other arithmetic: 6.49 us -> 0.13 us
  starting transfers between devices: 37.5 us -> 32 us
  Pallas kernels: 33.7 us -> 38.5 us
    unnamed x66 -> x1, local copies, waits for them, and re-layouts: 17.4 us -> 0.97 us
    ppermute x25, waiting for transfers between devices: 24.8 us -> 11.7 us  [shifted(): return lax.ppermute(array, axis, pairs)]
    ppermute x25, starting transfers between devices: 37.5 us -> 32 us  [shifted(): return lax.ppermute(array, axis, pairs)]
    pallas_call x5 -> x10, Pallas kernels: 33.7 us -> 38.5 us  [call(): pl.pallas_call(body, grid=grid, in_specs=specs, out_specs=out_specs, out_...]
    add x4 -> x0, other arithmetic: 4.17 us -> none  [carried(): before = [b + far for b in before]]
    add x2, other arithmetic: 2.3 us -> 0.04 us  [carried(): total = functools.reduce(jnp.add, got)]
  transfers between devices with their start and end apart: 25 -> 25, of which waited for: 16 -> 10; matrix products, arithmetic and copies ran while one was open for 1% -> 1% of each run, Pallas kernels for 18% -> 30%
where the time goes in v2:
time: 84.9 us; the launch traced here: 84.8 us
  Pallas kernels  38.5 us (45%)
  starting transfers between devices  32 us (38%)
  waiting for transfers between devices  11.7 us (14%)
  local copies, waits for them, and re-layouts  1.58 us (2%)
    pallas_call x10, Pallas kernels, call(): pl.pallas_call(body, grid=grid, in_specs=specs, out_specs=out_specs, out_...  38.5 us
    ppermute x25, starting transfers between devices, shifted(): return lax.ppermute(array, axis, pairs)  32 us
    ppermute x25, waiting for transfers between devices, shifted(): return lax.ppermute(array, axis, pairs)  11.7 us
  transfers between devices with their start and end apart: 25, of which 10 were waited for; matrix products, arithmetic and copies ran while one was open for 1% of the time, Pallas kernels for 30%

profile of v2, /device:TPU:0, one launch (start us, length us, event | category | flops | bytes accessed | tf_op | source)
XLA Modules:
  0.0 84.8 jit_solution(10100625712653663908)
XLA Ops:
  0.6 0.1 pad_add_fusion.me_ref
  0.7 4.6 %shard_map.85 = (f32[160,128]{1,0:T(8,128)S(1)}, f32[160,128]{1,0:T(8,128)S(1)}, f32[160,128]{1,0:T(8,128)S(1)}, f32[160,128]{1,0:T(8,128)S(1)}, bf16[4,1024,128...) custom-call(s32[2]{0:T(128)S(1)} %pad_add_fusion.me_ref, ...), custom_call_target="tpu_custom_call" | custom-call | flops 335544320 | tf_op jit(solution)/shard_map/pallas_call | solution.py:375
  5.3 3.0 %collective-permute-start = (f32[160,128]{1,0:T(8,128)S(1)}, f32[160,128]{1,0:T(8,128)S(1)}, u32[]{:S(2)}, u32[]{:S(2)}) collective-permute-start(f32[160,128]{1,0:T(8,128)S(1)} %get-tuple-element.57), channel_id=1, source_target_pairs={{0,8},{8,0},{16,24},{24,16},{1,9},{9,1},{17,25},{25,17},{2,10},{10... | collective-permute-start | bytes 245768 | tf_op jit(solution)/shard_map/ppermute | solution.py:390
  8.4 1.5 %collective-permute-start.1 = (f32[160,128]{1,0:T(8,128)S(1)}, f32[160,128]{1,0:T(8,128)S(1)}, u32[]{:S(2)}, u32[]{:S(2)}) collective-permute-start(f32[160,128]{1,0:T(8,128)S(1)} %get-tuple-element.58), channel_id=1, source_target_pairs={{0,16},{8,24},{16,0},{24,8},{1,17},{9,25},{17,1},{25,9},{2,18},{10... | collective-permute-start | bytes 245768 | tf_op jit(solution)/shard_map/ppermute | solution.py:390
  9.9 0.0 collective-permute-start.2
  9.9 1.2 %collective-permute-done.refs_4_ = f32[160,128]{1,0:T(8,128)S(1)} collective-permute-done((f32[160,128]{1,0:T(8,128)S(1)}, f32[160,128]{1,0:T(8,128)S(1)}, u32[]{:S(2)}, u32[]{:S(2)}) %collective-permute-start) | collective-permute-done | bytes 81952 | tf_op jit(solution)/shard_map/ppermute | solution.py:390
  11.1 2.6 %collective-permute-done.1.refs_5_ = f32[160,128]{1,0:T(8,128)S(1)} collective-permute-done((f32[160,128]{1,0:T(8,128)S(1)}, f32[160,128]{1,0:T(8,128)S(1)}, u32[]{:S(2)}, u32[]{:S(2)}) %collective-permute-start.1) | collective-permute-done | bytes 81952 | tf_op jit(solution)/shard_map/ppermute | solution.py:390
  13.7 1.5 %collective-permute-done.2.refs_6_ = f32[160,128]{1,0:T(8,128)S(1)} collective-permute-done((f32[160,128]{1,0:T(8,128)S(1)}, f32[160,128]{1,0:T(8,128)S(1)}, u32[]{:S(2)}, u32[]{:S(2)}) %collective-permute-start.2) | collective-permute-done | bytes 81952 | tf_op jit(solution)/shard_map/ppermute | solution.py:390
  15.2 3.7 %collective-permute-start.5 = (f32[160,128]{1,0:T(8,128)S(1)}, f32[160,128]{1,0:T(8,128)S(1)}, u32[]{:S(2)}, u32[]{:S(2)}) collective-permute-start(f32[160,128]{1,0:T(8,128)S(1)} %add_add_fusion.1), channel_id=1, source_target_pairs={{0,6},{2,4},{4,2},{6,0},{1,7},{3,5},{5,3},{7,1},{8,14},{10,12},{12... | collective-permute-start | bytes 245768 | tf_op jit(solution)/shard_map/ppermute | solution.py:390
  18.9 0.0 collective-permute-start.4
  18.9 0.8 collective-permute-start.3
  19.7 4.5 %shard_map.87 = (f32[2,1024,128]{2,1,0:T(8,128)S(1)}, f32[2,1024,128]{2,1,0:T(8,128)S(1)}, f32[2,1024,256]{2,1,0:T(8,128)S(1)}, f32[2,160,1024]{2,1,0:T(8,128)S(1)}) custom-call(bf16[4,1024,128]{2,1,0:T(8,128)(2,1)S(1)} %get-tuple-element.43.q_ref, bf16[4,1024,128]{2,1,0:T(8,128)(2,1)S(1)} %get-tuple-element.44.k_ref, ...), custom_call_target="tpu_custom_call" | custom-call | flops 1073741824 | tf_op jit(solution)/shard_map/pallas_call | solution.py:375
  24.2 0.4 collective-permute-done.4.refs_1_
  24.6 0.6 shard_map.88
  25.2 1.1 %collective-permute-start.6 = (f32[160,128]{1,0:T(8,128)S(1)}, f32[160,128]{1,0:T(8,128)S(1)}, u32[]{:S(2)}, u32[]{:S(2)}) collective-permute-start(f32[160,128]{1,0:T(8,128)S(1)} %get-tuple-element.61), channel_id=1, source_target_pairs={{0,8},{8,0},{16,24},{24,16},{1,9},{9,1},{17,25},{25,17},{2,10},{10... | collective-permute-start | bytes 245768 | tf_op jit(solution)/shard_map/ppermute | solution.py:390
  26.3 0.6 collective-permute-start.7
  26.9 1.9 %collective-permute-start.8 = (f32[160,128]{1,0:T(8,128)S(1)}, f32[160,128]{1,0:T(8,128)S(1)}, u32[]{:S(2)}, u32[]{:S(2)}) collective-permute-start(f32[160,128]{1,0:T(8,128)S(1)} %get-tuple-element.63), channel_id=1, source_target_pairs={{0,24},{8,16},{16,8},{24,0},{1,25},{9,17},{17,9},{25,1},{2,26},{10... | collective-permute-start | bytes 245768 | tf_op jit(solution)/shard_map/ppermute | solution.py:390
  28.8 4.5 %shard_map.86 = (f32[2,1024,128]{2,1,0:T(8,128)S(1)}, f32[2,1024,128]{2,1,0:T(8,128)S(1)}, f32[2,1024,256]{2,1,0:T(8,128)S(1)}, f32[2,160,1024]{2,1,0:T(8,128)S(1)}) custom-call(bf16[4,1024,128]{2,1,0:T(8,128)(2,1)S(1)} %get-tuple-element.43.q_ref, bf16[4,1024,128]{2,1,0:T(8,128)(2,1)S(1)} %get-tuple-element.44.k_ref, ...), custom_call_target="tpu_custom_call" | custom-call | flops 1073741824 | tf_op jit(solution)/shard_map/pallas_call | solution.py:375
  33.4 4.8 %shard_map.89 = (bf16[4,1024,128]{2,1,0:T(8,128)(2,1)S(1)}, f32[4,1024,128]{2,1,0:T(8,128)S(1)}, f32[4,1024,128]{2,1,0:T(8,128)S(1)}, f32[160,128]{1,0:T(8,128)S...) custom-call(s32[2]{0:T(128)S(1)} %pad_add_fusion.me_ref, ...), custom_call_target="tpu_custom_call" | custom-call | flops 1073741824 | tf_op jit(solution)/shard_map/pallas_call | solution.py:375
  38.2 1.1 %collective-permute-start.9 = (f32[160,128]{1,0:T(8,128)S(1)}, f32[160,128]{1,0:T(8,128)S(1)}, u32[]{:S(2)}, u32[]{:S(2)}) collective-permute-start(f32[160,128]{1,0:T(8,128)S(1)} %get-tuple-element.66), channel_id=1, source_target_pairs={{0,8},{8,0},{16,24},{24,16},{1,9},{9,1},{17,25},{25,17},{2,10},{10... | collective-permute-start | bytes 245768 | tf_op jit(solution)/shard_map/ppermute | solution.py:390
  39.3 0.6 collective-permute-start.10
  39.9 1.9 %collective-permute-start.11 = (f32[160,128]{1,0:T(8,128)S(1)}, f32[160,128]{1,0:T(8,128)S(1)}, u32[]{:S(2)}, u32[]{:S(2)}) collective-permute-start(f32[160,128]{1,0:T(8,128)S(1)} %get-tuple-element.68), channel_id=1, source_target_pairs={{0,24},{8,16},{16,8},{24,0},{1,25},{9,17},{17,9},{25,1},{2,26},{10... | collective-permute-start | bytes 245768 | tf_op jit(solution)/shard_map/ppermute | solution.py:390
  41.8 8.3 %shard_map.92 = (f32[2,16,1024]{2,1,0:T(8,128)S(1)}, f32[16,128]{1,0:T(8,128)S(1)}) custom-call(s32[2]{0:T(128)S(1)} %pad_add_fusion.me_ref, bf16[4,1024,128]{2,1,0:T(8,128)(2,1)S(1)} %get-tuple-element.43.q_ref, bf16[4,1024,128]{2,1,0:T(8,128)(2,1)S(1)} %get-tuple-element.44.k_ref, bf16[4,1024,128]{2,1,0:T(8,128)(2,1)S(1)} %get-tuple-element.45.v_ref, ...), custom_call_target="tpu_custom_call" | custom-call | flops 2147483648 | tf_op jit(solution)/shard_map/pallas_call | solution.py:375
  50.1 3.3 %collective-permute-start.14 = (f32[160,128]{1,0:T(8,128)S(1)}, f32[160,128]{1,0:T(8,128)S(1)}, u32[]{:S(2)}, u32[]{:S(2)}) collective-permute-start(f32[160,128]{1,0:T(8,128)S(1)} %add_add_fusion), channel_id=1, source_target_pairs={{0,6},{2,4},{4,2},{6,0},{1,7},{3,5},{5,3},{7,1},{8,14},{10,12},{12... | collective-permute-start | bytes 245768 | tf_op jit(solution)/shard_map/ppermute | solution.py:390
  53.4 1.1 %collective-permute-start.12 = (f32[160,128]{1,0:T(8,128)S(1)}, f32[160,128]{1,0:T(8,128)S(1)}, u32[]{:S(2)}, u32[]{:S(2)}) collective-permute-start(f32[160,128]{1,0:T(8,128)S(1)} %add_add_fusion), channel_id=1, source_target_pairs={{0,2},{2,0},{4,6},{6,4},{1,3},{3,1},{5,7},{7,5},{8,10},{10,8},{12,... | collective-permute-start | bytes 245768 | tf_op jit(solution)/shard_map/ppermute | solution.py:390
  54.5 4.2 %shard_map.93 = (f32[1,16,1024]{2,1,0:T(8,128)S(1)}, f32[16,128]{1,0:T(8,128)S(1)}) custom-call(s32[2]{0:T(128)S(1)} %pad_add_fusion.me_ref, bf16[4,1024,128]{2,1,0:T(8,128)(2,1)S(1)} %get-tuple-element.43.q_ref, bf16[4,1024,128]{2,1,0:T(8,128)(2,1)S(1)} %get-tuple-element.44.k_ref, bf16[4,1024,128]{2,1,0:T(8,128)(2,1)S(1)} %get-tuple-element.45.v_ref, ...), custom_call_target="tpu_custom_call" | custom-call | flops 1073741824 | tf_op jit(solution)/shard_map/pallas_call | solution.py:375
  58.8 0.0 collective-permute-done.13.refs_1_
  58.8 0.6 shard_map.90
  59.4 1.1 %collective-permute-start.15 = (f32[160,128]{1,0:T(8,128)S(1)}, f32[160,128]{1,0:T(8,128)S(1)}, u32[]{:S(2)}, u32[]{:S(2)}) collective-permute-start(f32[160,128]{1,0:T(8,128)S(1)} %get-tuple-element.70), channel_id=1, source_target_pairs={{0,8},{8,0},{16,24},{24,16},{1,9},{9,1},{17,25},{25,17},{2,10},{10... | collective-permute-start | bytes 245768 | tf_op jit(solution)/shard_map/ppermute | solution.py:390
  60.5 0.6 collective-permute-start.16
  61.1 1.9 %collective-permute-start.17 = (f32[160,128]{1,0:T(8,128)S(1)}, f32[160,128]{1,0:T(8,128)S(1)}, u32[]{:S(2)}, u32[]{:S(2)}) collective-permute-start(f32[160,128]{1,0:T(8,128)S(1)} %get-tuple-element.72), channel_id=1, source_target_pairs={{0,24},{8,16},{16,8},{24,0},{1,25},{9,17},{17,9},{25,1},{2,26},{10... | collective-permute-start | bytes 245768 | tf_op jit(solution)/shard_map/ppermute | solution.py:390
  63.0 4.2 %shard_map.91 = (f32[1,16,1024]{2,1,0:T(8,128)S(1)}, f32[16,128]{1,0:T(8,128)S(1)}) custom-call(s32[2]{0:T(128)S(1)} %pad_add_fusion.me_ref, bf16[4,1024,128]{2,1,0:T(8,128)(2,1)S(1)} %get-tuple-element.43.q_ref, bf16[4,1024,128]{2,1,0:T(8,128)(2,1)S(1)} %get-tuple-element.44.k_ref, bf16[4,1024,128]{2,1,0:T(8,128)(2,1)S(1)} %get-tuple-element.45.v_ref, ...), custom_call_target="tpu_custom_call" | custom-call | flops 1073741824 | tf_op jit(solution)/shard_map/pallas_call | solution.py:375
  67.2 0.0 collective-permute-done.16.rest_2_
  67.3 2.0 %shard_map.94 = f32[32,128]{1,0:T(8,128)S(1)} custom-call(s32[2]{0:T(128)S(1)} %pad_add_fusion.me_ref, bf16[4,1024,128]{2,1,0:T(8,128)(2,1)S(1)} %get-tuple-element.44.k_ref, bf16[4,1024,128]{2,1,0:T(8,128)(2,1)S(1)} %get-tuple-element.45.v_ref, f32[16,128]{1,0:T(8,128)S(1)} %get-tuple-element.47.wk_ref, f32[160,128]{1,0:T(8,128)S(1)} %get-tuple-element.69.rest_0_, ...), custom_call_target="tpu_custom_call" | custom-call | flops 335544320 | tf_op jit(solution)/shard_map/pallas_call | solution.py:375
  69.3 0.0 collective-permute-start.18
  69.3 1.2 %collective-permute-done.18 = f32[32,128]{1,0:T(8,128)S(1)} collective-permute-done((f32[32,128]{1,0:T(8,128)S(1)}, f32[32,128]{1,0:T(8,128)S(1)}, u32[]{:S(2)}, u32[]{:S(2)}) %collective-permute-start.18) | collective-permute-done | bytes 16416 | tf_op jit(solution)/shard_map/ppermute | solution.py:390
  70.5 1.1 %collective-permute-start.21 = (f32[32,128]{1,0:T(8,128)S(1)}, f32[32,128]{1,0:T(8,128)S(1)}, u32[]{:S(2)}, u32[]{:S(2)}) collective-permute-start(f32[32,128]{1,0:T(8,128)S(1)} %add.45), channel_id=1, source_target_pairs={{0,24},{8,16},{16,8},{24,0},{1,25},{9,17},{17,9},{25,1},{2,26},{10... | collective-permute-start | bytes 49160 | tf_op jit(solution)/shard_map/ppermute | solution.py:390
  71.6 1.4 %collective-permute-start.20 = (f32[32,128]{1,0:T(8,128)S(1)}, f32[32,128]{1,0:T(8,128)S(1)}, u32[]{:S(2)}, u32[]{:S(2)}) collective-permute-start(f32[32,128]{1,0:T(8,128)S(1)} %add.45), channel_id=1, source_target_pairs={{0,16},{8,24},{16,0},{24,8},{1,17},{9,25},{17,1},{25,9},{2,18},{10... | collective-permute-start | bytes 49160 | tf_op jit(solution)/shard_map/ppermute | solution.py:390
  73.0 1.0 %collective-permute-start.19 = (f32[32,128]{1,0:T(8,128)S(1)}, f32[32,128]{1,0:T(8,128)S(1)}, u32[]{:S(2)}, u32[]{:S(2)}) collective-permute-start(f32[32,128]{1,0:T(8,128)S(1)} %add.45), channel_id=1, source_target_pairs={{0,8},{8,0},{16,24},{24,16},{1,9},{9,1},{17,25},{25,17},{2,10},{10... | collective-permute-start | bytes 49160 | tf_op jit(solution)/shard_map/ppermute | solution.py:390
  74.0 1.1 %collective-permute-done.21 = f32[32,128]{1,0:T(8,128)S(1)} collective-permute-done((f32[32,128]{1,0:T(8,128)S(1)}, f32[32,128]{1,0:T(8,128)S(1)}, u32[]{:S(2)}, u32[]{:S(2)}) %collective-permute-start.21) | collective-permute-done | bytes 16416 | tf_op jit(solution)/shard_map/ppermute | solution.py:390
  75.1 0.2 collective-permute-done.20
  75.3 1.4 %collective-permute-done.19 = f32[32,128]{1,0:T(8,128)S(1)} collective-permute-done((f32[32,128]{1,0:T(8,128)S(1)}, f32[32,128]{1,0:T(8,128)S(1)}, u32[]{:S(2)}, u32[]{:S(2)}) %collective-permute-start.19) | collective-permute-done | bytes 16416 | tf_op jit(solution)/shard_map/ppermute | solution.py:390
  76.7 2.8 %collective-permute-start.24 = (f32[32,128]{1,0:T(8,128)S(1)}, f32[32,128]{1,0:T(8,128)S(1)}, u32[]{:S(2)}, u32[]{:S(2)}) collective-permute-start(f32[32,128]{1,0:T(8,128)S(1)} %add_add_fusion.3), channel_id=1, source_target_pairs={{0,6},{2,4},{4,2},{6,0},{1,7},{3,5},{5,3},{7,1},{8,14},{10,12},{12... | collective-permute-start | bytes 49160 | tf_op jit(solution)/shard_map/ppermute | solution.py:390
  79.5 1.6 %collective-permute-start.22 = (f32[32,128]{1,0:T(8,128)S(1)}, f32[32,128]{1,0:T(8,128)S(1)}, u32[]{:S(2)}, u32[]{:S(2)}) collective-permute-start(f32[32,128]{1,0:T(8,128)S(1)} %add_add_fusion.3), channel_id=1, source_target_pairs={{0,2},{2,0},{4,6},{6,4},{1,3},{3,1},{5,7},{7,5},{8,10},{10,8},{12,... | collective-permute-start | bytes 49160 | tf_op jit(solution)/shard_map/ppermute | solution.py:390
  81.1 1.0 %copy.9 = bf16[4,1024,128]{2,1,0:T(8,128)(2,1)} copy(bf16[4,1024,128]{2,1,0:T(8,128)(2,1)S(1)} %get-tuple-element.83) | data formatting | bytes 2097152
  82.1 0.2 collective-permute-done.24
  82.2 1.9 %collective-permute-done.23 = f32[32,128]{1,0:T(8,128)S(1)} collective-permute-done((f32[32,128]{1,0:T(8,128)S(1)}, f32[32,128]{1,0:T(8,128)S(1)}, u32[]{:S(2)}, u32[]{:S(2)}) %collective-permute-start.23) | collective-permute-done | bytes 16416 | tf_op jit(solution)/shard_map/ppermute | solution.py:390
  84.2 0.6 slice_bitcast_fusion
  (20 shorter events, 0.1 us)
Async XLA Ops:
  5.3 5.7 %collective-permute-start = (f32[160,128]{1,0:T(8,128)S(1)}, f32[160,128]{1,0:T(8,128)S(1)}, u32[]{:S(2)}, u32[]{:S(2)}) collective-permute-start(f32[160,128]{1,0:T(8,128)S(1)} %get-tuple-element.57), channel_id=1, source_target_pairs={{0,8},{8,0},{16,24},{24,16},{1,9},{9,1},{17,25},{25,17},{2,10},{10... | collective-permute-start | bytes 245768 | tf_op jit(solution)/shard_map/ppermute | solution.py:390
  8.4 5.3 %collective-permute-start.1 = (f32[160,128]{1,0:T(8,128)S(1)}, f32[160,128]{1,0:T(8,128)S(1)}, u32[]{:S(2)}, u32[]{:S(2)}) collective-permute-start(f32[160,128]{1,0:T(8,128)S(1)} %get-tuple-element.58), channel_id=1, source_target_pairs={{0,16},{8,24},{16,0},{24,8},{1,17},{9,25},{17,1},{25,9},{2,18},{10... | collective-permute-start | bytes 245768 | tf_op jit(solution)/shard_map/ppermute | solution.py:390
  9.9 5.3 %collective-permute-start.2 = (f32[160,128]{1,0:T(8,128)S(1)}, f32[160,128]{1,0:T(8,128)S(1)}, u32[]{:S(2)}, u32[]{:S(2)}) collective-permute-start(f32[160,128]{1,0:T(8,128)S(1)} %get-tuple-element.59), channel_id=1, source_target_pairs={{0,24},{8,16},{16,8},{24,0},{1,25},{9,17},{17,9},{25,1},{2,26},{10... | collective-permute-start | bytes 245768 | tf_op jit(solution)/shard_map/ppermute | solution.py:390
  15.2 9.0 %collective-permute-start.5 = (f32[160,128]{1,0:T(8,128)S(1)}, f32[160,128]{1,0:T(8,128)S(1)}, u32[]{:S(2)}, u32[]{:S(2)}) collective-permute-start(f32[160,128]{1,0:T(8,128)S(1)} %add_add_fusion.1), channel_id=1, source_target_pairs={{0,6},{2,4},{4,2},{6,0},{1,7},{3,5},{5,3},{7,1},{8,14},{10,12},{12... | collective-permute-start | bytes 245768 | tf_op jit(solution)/shard_map/ppermute | solution.py:390
  18.9 5.7 %collective-permute-start.4 = (f32[160,128]{1,0:T(8,128)S(1)}, f32[160,128]{1,0:T(8,128)S(1)}, u32[]{:S(2)}, u32[]{:S(2)}) collective-permute-start(f32[160,128]{1,0:T(8,128)S(1)} %add_add_fusion.1), channel_id=1, source_target_pairs={{0,4},{2,6},{4,0},{6,2},{1,5},{3,7},{5,1},{7,3},{8,12},{10,14},{12... | collective-permute-start | bytes 245768 | tf_op jit(solution)/shard_map/ppermute | solution.py:390
  18.9 5.7 %collective-permute-start.3 = (f32[160,128]{1,0:T(8,128)S(1)}, f32[160,128]{1,0:T(8,128)S(1)}, u32[]{:S(2)}, u32[]{:S(2)}) collective-permute-start(f32[160,128]{1,0:T(8,128)S(1)} %add_add_fusion.1), channel_id=1, source_target_pairs={{0,2},{2,0},{4,6},{6,4},{1,3},{3,1},{5,7},{7,5},{8,10},{10,8},{12,... | collective-permute-start | bytes 245768 | tf_op jit(solution)/shard_map/ppermute | solution.py:390
  25.2 8.1 %collective-permute-start.6 = (f32[160,128]{1,0:T(8,128)S(1)}, f32[160,128]{1,0:T(8,128)S(1)}, u32[]{:S(2)}, u32[]{:S(2)}) collective-permute-start(f32[160,128]{1,0:T(8,128)S(1)} %get-tuple-element.61), channel_id=1, source_target_pairs={{0,8},{8,0},{16,24},{24,16},{1,9},{9,1},{17,25},{25,17},{2,10},{10... | collective-permute-start | bytes 245768 | tf_op jit(solution)/shard_map/ppermute | solution.py:390
  26.3 7.0 %collective-permute-start.7 = (f32[160,128]{1,0:T(8,128)S(1)}, f32[160,128]{1,0:T(8,128)S(1)}, u32[]{:S(2)}, u32[]{:S(2)}) collective-permute-start(f32[160,128]{1,0:T(8,128)S(1)} %get-tuple-element.62), channel_id=1, source_target_pairs={{0,16},{8,24},{16,0},{24,8},{1,17},{9,25},{17,1},{25,9},{2,18},{10... | collective-permute-start | bytes 245768 | tf_op jit(solution)/shard_map/ppermute | solution.py:390
  26.9 6.4 %collective-permute-start.8 = (f32[160,128]{1,0:T(8,128)S(1)}, f32[160,128]{1,0:T(8,128)S(1)}, u32[]{:S(2)}, u32[]{:S(2)}) collective-permute-start(f32[160,128]{1,0:T(8,128)S(1)} %get-tuple-element.63), channel_id=1, source_target_pairs={{0,24},{8,16},{16,8},{24,0},{1,25},{9,17},{17,9},{25,1},{2,26},{10... | collective-permute-start | bytes 245768 | tf_op jit(solution)/shard_map/ppermute | solution.py:390
  38.2 11.8 %collective-permute-start.9 = (f32[160,128]{1,0:T(8,128)S(1)}, f32[160,128]{1,0:T(8,128)S(1)}, u32[]{:S(2)}, u32[]{:S(2)}) collective-permute-start(f32[160,128]{1,0:T(8,128)S(1)} %get-tuple-element.66), channel_id=1, source_target_pairs={{0,8},{8,0},{16,24},{24,16},{1,9},{9,1},{17,25},{25,17},{2,10},{10... | collective-permute-start | bytes 245768 | tf_op jit(solution)/shard_map/ppermute | solution.py:390
  39.3 10.8 %collective-permute-start.10 = (f32[160,128]{1,0:T(8,128)S(1)}, f32[160,128]{1,0:T(8,128)S(1)}, u32[]{:S(2)}, u32[]{:S(2)}) collective-permute-start(f32[160,128]{1,0:T(8,128)S(1)} %get-tuple-element.67), channel_id=1, source_target_pairs={{0,16},{8,24},{16,0},{24,8},{1,17},{9,25},{17,1},{25,9},{2,18},{10... | collective-permute-start | bytes 245768 | tf_op jit(solution)/shard_map/ppermute | solution.py:390
  39.9 10.2 %collective-permute-start.11 = (f32[160,128]{1,0:T(8,128)S(1)}, f32[160,128]{1,0:T(8,128)S(1)}, u32[]{:S(2)}, u32[]{:S(2)}) collective-permute-start(f32[160,128]{1,0:T(8,128)S(1)} %get-tuple-element.68), channel_id=1, source_target_pairs={{0,24},{8,16},{16,8},{24,0},{1,25},{9,17},{17,9},{25,1},{2,26},{10... | collective-permute-start | bytes 245768 | tf_op jit(solution)/shard_map/ppermute | solution.py:390
  50.1 8.7 %collective-permute-start.14 = (f32[160,128]{1,0:T(8,128)S(1)}, f32[160,128]{1,0:T(8,128)S(1)}, u32[]{:S(2)}, u32[]{:S(2)}) collective-permute-start(f32[160,128]{1,0:T(8,128)S(1)} %add_add_fusion), channel_id=1, source_target_pairs={{0,6},{2,4},{4,2},{6,0},{1,7},{3,5},{5,3},{7,1},{8,14},{10,12},{12... | collective-permute-start | bytes 245768 | tf_op jit(solution)/shard_map/ppermute | solution.py:390
  53.4 5.4 %collective-permute-start.13 = (f32[160,128]{1,0:T(8,128)S(1)}, f32[160,128]{1,0:T(8,128)S(1)}, u32[]{:S(2)}, u32[]{:S(2)}) collective-permute-start(f32[160,128]{1,0:T(8,128)S(1)} %add_add_fusion), channel_id=1, source_target_pairs={{0,4},{2,6},{4,0},{6,2},{1,5},{3,7},{5,1},{7,3},{8,12},{10,14},{12... | collective-permute-start | bytes 245768 | tf_op jit(solution)/shard_map/ppermute | solution.py:390
  53.4 5.4 %collective-permute-start.12 = (f32[160,128]{1,0:T(8,128)S(1)}, f32[160,128]{1,0:T(8,128)S(1)}, u32[]{:S(2)}, u32[]{:S(2)}) collective-permute-start(f32[160,128]{1,0:T(8,128)S(1)} %add_add_fusion), channel_id=1, source_target_pairs={{0,2},{2,0},{4,6},{6,4},{1,3},{3,1},{5,7},{7,5},{8,10},{10,8},{12,... | collective-permute-start | bytes 245768 | tf_op jit(solution)/shard_map/ppermute | solution.py:390
  59.4 7.8 %collective-permute-start.15 = (f32[160,128]{1,0:T(8,128)S(1)}, f32[160,128]{1,0:T(8,128)S(1)}, u32[]{:S(2)}, u32[]{:S(2)}) collective-permute-start(f32[160,128]{1,0:T(8,128)S(1)} %get-tuple-element.70), channel_id=1, source_target_pairs={{0,8},{8,0},{16,24},{24,16},{1,9},{9,1},{17,25},{25,17},{2,10},{10... | collective-permute-start | bytes 245768 | tf_op jit(solution)/shard_map/ppermute | solution.py:390
  60.5 6.7 %collective-permute-start.16 = (f32[160,128]{1,0:T(8,128)S(1)}, f32[160,128]{1,0:T(8,128)S(1)}, u32[]{:S(2)}, u32[]{:S(2)}) collective-permute-start(f32[160,128]{1,0:T(8,128)S(1)} %get-tuple-element.71), channel_id=1, source_target_pairs={{0,16},{8,24},{16,0},{24,8},{1,17},{9,25},{17,1},{25,9},{2,18},{10... | collective-permute-start | bytes 245768 | tf_op jit(solution)/shard_map/ppermute | solution.py:390
  61.1 6.1 %collective-permute-start.17 = (f32[160,128]{1,0:T(8,128)S(1)}, f32[160,128]{1,0:T(8,128)S(1)}, u32[]{:S(2)}, u32[]{:S(2)}) collective-permute-start(f32[160,128]{1,0:T(8,128)S(1)} %get-tuple-element.72), channel_id=1, source_target_pairs={{0,24},{8,16},{16,8},{24,0},{1,25},{9,17},{17,9},{25,1},{2,26},{10... | collective-permute-start | bytes 245768 | tf_op jit(solution)/shard_map/ppermute | solution.py:390
  69.3 1.2 %collective-permute-start.18 = (f32[32,128]{1,0:T(8,128)S(1)}, f32[32,128]{1,0:T(8,128)S(1)}, u32[]{:S(2)}, u32[]{:S(2)}) collective-permute-start(f32[32,128]{1,0:T(8,128)S(1)} %shard_map.94), channel_id=1, source_target_pairs={{0,1},{1,0},{2,3},{3,2},{4,5},{5,4},{6,7},{7,6},{8,9},{9,8},{10,11... | collective-permute-start | bytes 49160 | tf_op jit(solution)/shard_map/ppermute | solution.py:390
  70.5 4.6 %collective-permute-start.21 = (f32[32,128]{1,0:T(8,128)S(1)}, f32[32,128]{1,0:T(8,128)S(1)}, u32[]{:S(2)}, u32[]{:S(2)}) collective-permute-start(f32[32,128]{1,0:T(8,128)S(1)} %add.45), channel_id=1, source_target_pairs={{0,24},{8,16},{16,8},{24,0},{1,25},{9,17},{17,9},{25,1},{2,26},{10... | collective-permute-start | bytes 49160 | tf_op jit(solution)/shard_map/ppermute | solution.py:390
  71.6 3.7 %collective-permute-start.20 = (f32[32,128]{1,0:T(8,128)S(1)}, f32[32,128]{1,0:T(8,128)S(1)}, u32[]{:S(2)}, u32[]{:S(2)}) collective-permute-start(f32[32,128]{1,0:T(8,128)S(1)} %add.45), channel_id=1, source_target_pairs={{0,16},{8,24},{16,0},{24,8},{1,17},{9,25},{17,1},{25,9},{2,18},{10... | collective-permute-start | bytes 49160 | tf_op jit(solution)/shard_map/ppermute | solution.py:390
  73.0 3.7 %collective-permute-start.19 = (f32[32,128]{1,0:T(8,128)S(1)}, f32[32,128]{1,0:T(8,128)S(1)}, u32[]{:S(2)}, u32[]{:S(2)}) collective-permute-start(f32[32,128]{1,0:T(8,128)S(1)} %add.45), channel_id=1, source_target_pairs={{0,8},{8,0},{16,24},{24,16},{1,9},{9,1},{17,25},{25,17},{2,10},{10... | collective-permute-start | bytes 49160 | tf_op jit(solution)/shard_map/ppermute | solution.py:390
  76.7 5.5 %collective-permute-start.24 = (f32[32,128]{1,0:T(8,128)S(1)}, f32[32,128]{1,0:T(8,128)S(1)}, u32[]{:S(2)}, u32[]{:S(2)}) collective-permute-start(f32[32,128]{1,0:T(8,128)S(1)} %add_add_fusion.3), channel_id=1, source_target_pairs={{0,6},{2,4},{4,2},{6,0},{1,7},{3,5},{5,3},{7,1},{8,14},{10,12},{12... | collective-permute-start | bytes 49160 | tf_op jit(solution)/shard_map/ppermute | solution.py:390
  79.5 4.6 %collective-permute-start.23 = (f32[32,128]{1,0:T(8,128)S(1)}, f32[32,128]{1,0:T(8,128)S(1)}, u32[]{:S(2)}, u32[]{:S(2)}) collective-permute-start(f32[32,128]{1,0:T(8,128)S(1)} %add_add_fusion.3), channel_id=1, source_target_pairs={{0,4},{2,6},{4,0},{6,2},{1,5},{3,7},{5,1},{7,3},{8,12},{10,14},{12... | collective-permute-start | bytes 49160 | tf_op jit(solution)/shard_map/ppermute | solution.py:390
  79.5 4.6 %collective-permute-start.22 = (f32[32,128]{1,0:T(8,128)S(1)}, f32[32,128]{1,0:T(8,128)S(1)}, u32[]{:S(2)}, u32[]{:S(2)}) collective-permute-start(f32[32,128]{1,0:T(8,128)S(1)} %add_add_fusion.3), channel_id=1, source_target_pairs={{0,2},{2,0},{4,6},{6,4},{1,3},{3,1},{5,7},{7,5},{8,10},{10,8},{12,... | collective-permute-start | bytes 49160 | tf_op jit(solution)/shard_map/ppermute | solution.py:390

commit v3 on v2

--- a/solution.py
+++ b/solution.py
@@ -46,6 +46,11 @@
     return (f + (f >> dm.shift)) & (dm.width - 1)
 
 
+def tiles(tokens, size=256):
+    size = min(size, tokens)
+    return [slice(i, i + size) for i in range(0, tokens, size)]
+
+
 def dot(a, b, dims=(((1,), (0,)), ((), ()))):
     return lax.dot_general(a, b, dims, preferred_element_type=f32)
 
@@ -94,8 +99,8 @@
     return jnp.concatenate(parts, 0)
 
 
-def features_rows(rows, w_t, dm):
-    left, right = sides(w_t, dm)
+def features_rows(rows, side, dm):
+    left, right = side
     f = positions((1, dm.lanes), 1)
     left = dot(rows, left, NT) + jnp.where(f == dm.const, 1.0, 0.0)
     right = dot(rows, right, NT) + jnp.where((f >= dm.lin) & (f < dm.feats), 1.0, 0.0)
@@ -126,42 +131,42 @@
     return jnp.concatenate([state[dm.feats + c : dm.feats + c + 1] for c in range(dm.count_rows)], 1)
 
 
+def column_row(part, dm):
+    column = jnp.sum(part, 1, keepdims=True)
+    row, lane = positions((dm.rows, dm.lanes), 0), positions((dm.rows, dm.lanes), 1)
+    return jnp.sum(jnp.where(row == lane, column, 0.0), 0, keepdims=True)
+
+
 def state_kernel(dm, n, me_ref, *rest):
-    sources, slots, kept, scr, sems, last = rest[:6], rest[6 : 6 + n], rest[6 + n : 12 + n], *rest[12 + n :]
-    k_hbm, v_hbm, q_hbm, t_hbm, wk_hbm, wq_hbm = sources
-    k_ref, v_ref, q_ref, t_ref, wk_ref, wq_ref = kept
+    sources, slots, kept, at_ref, scr, sems = rest[:4], rest[4 : 4 + n], rest[4 + n : 8 + n], *rest[8 + n :]
+    at_ref[0] = me_ref[0]
+    at_ref[1] = me_ref[1]
+    wk_ref, k_ref, v_ref = kept[:3]
     heads = k_ref.shape[0]
-    first = pltpu.make_async_copy(wk_hbm, wk_ref, last.at[0])
-    keys = [pltpu.make_async_copy(k_hbm.at[h], k_ref.at[h], sems.at[h]) for h in range(heads)]
-    values = [pltpu.make_async_copy(v_hbm.at[h], v_ref.at[h], sems.at[heads + h]) for h in range(heads)]
-    others = [
-        pltpu.make_async_copy(wq_hbm, wq_ref, last.at[1]),
-        pltpu.make_async_copy(q_hbm, q_ref, last.at[2]),
-        pltpu.make_async_copy(t_hbm, t_ref, last.at[3]),
-    ]
-    first.start()
+    copies = [pltpu.make_async_copy(a, b, sems.at[i]) for i, (a, b) in enumerate(zip(sources, kept))]
+    for copy in copies:
+        copy.start()
+    copies[0].wait()
+    w_ext = rolled(wk_ref[...].astype(bf16), dm)
+    for copy in copies[1:]:
+        copy.wait()
     for h in range(heads):
-        keys[h].start()
-        values[h].start()
-    for copy in others:
+        phi = features_t(dot(w_ext, k_ref[h], NT), dm)
+        part = phi[:, :LANES]
+        for c in range(LANES, phi.shape[1], LANES):
+            part = part + phi[:, c : c + LANES]
+        state = dot(phi.astype(bf16), v_ref[h])
+        scr[h * dm.rows : (h + 1) * dm.rows, :] = with_count(state, column_row(part, dm), dm)
+    scatter_slots(me_ref, slots, scr)
+
+
+def turn_kernel(v_ref, q_hbm, t_hbm, vt_ref, q_ref, t_ref, sems):
+    copies = [pltpu.make_async_copy(a, b, sems.at[i]) for i, (a, b) in enumerate(((q_hbm, q_ref), (t_hbm, t_ref)))]
+    for copy in copies:
         copy.start()
-    first.wait()
-    w_ext = rolled(wk_ref[...].astype(bf16), dm)
-    for h in range(heads):
-        keys[h].wait()
-        phi = features_t(dot(w_ext, k_ref[h], NT), dm)
-        values[h].wait()
-        state = dot(phi.astype(bf16), v_ref[h])
-        part = phi[:, :LANES]
-        for c in range(1, phi.shape[1] // LANES):
-            part = part + phi[:, c * LANES : (c + 1) * LANES]
-        count = lax.dot_general(
-            jnp.ones((8, LANES), f32), part, NT, precision=lax.Precision.HIGHEST, preferred_element_type=f32
-        )[0:1]
-        count = jnp.concatenate([count, jnp.zeros((1, dm.lanes - dm.rows), f32)], 1)
-        scr[h * dm.rows : (h + 1) * dm.rows, :] = with_count(state, count, dm)
-    scatter_slots(me_ref, slots, scr)
-    for copy in others:
+    for h in range(v_ref.shape[0]):
+        vt_ref[h] = v_ref[h].T
+    for copy in copies:
         copy.wait()
 
 
@@ -179,16 +184,20 @@
     k_t = dot(wk, k, NT)
     k1, k2, k3 = split3(k_t)
     last = one_hot(positions((LANES - 6 * w, k_t.shape[1]), 0) == 0)
-    return q_pack, jnp.concatenate([k1, k2, k3, k1, k2, k1, last], 0), k1, k2
-
-
-def intra_kernel(dm, tile, h0, q_ref, k_ref, v_ref, wq_ref, wk_ref, numer_ref, denom_ref, phi_ref, phi_t_ref):
+    return q_pack, jnp.concatenate([k1, k2, k3, k1, k2, k1, last], 0)
+
+
+def intra_kernel(dm, tile, h0, q_ref, k_ref, v_ref, wq_ref, wk_ref, *outs):
+    numer_ref, denom_ref, q_pack_ref, k_pack_ref, q_two_ref, ext_ref = outs
     h = pl.program_id(0)
     q, k, v = q_ref[h0 + h], k_ref[h0 + h], v_ref.at[h0 + h]
     wq = wq_ref[...].astype(bf16)
-    phi_ref[h] = features_rows(q, wq, dm)
-    phi_t_ref[h] = features_t(dot(rolled(wq, dm), q, NT), dm)
-    q_pack, k_pack, _, _ = packs(q, k, wq, wk_ref[...].astype(bf16), dm)
+    ext = dot(rolled(wq, dm), q, NT)
+    ext_ref[h] = ext
+    q_two_ref[h] = jnp.concatenate(split2(ext[: dm.width]), 0)
+    q_pack, k_pack = packs(q, k, wq, wk_ref[...].astype(bf16), dm)
+    q_pack_ref[h] = q_pack
+    k_pack_ref[h] = k_pack
     tokens = q_pack.shape[0]
     below = positions((tile, tile), 0) >= positions((tile, tile), 1)
     for i in range(tokens // tile):
@@ -208,6 +217,17 @@
         denom_ref[h, rows, :] = denom
 
 
+def feature_kernel(dm, h0, q_ref, wq_ref, ext_ref, phi_ref, p1_ref, p2_ref, t_ref):
+    h = pl.program_id(0)
+    wq = wq_ref[...].astype(bf16)
+    side = sides(wq, dm)
+    for cols in tiles(q_ref.shape[1]):
+        phi = features_rows(q_ref[h0 + h, cols, :], side, dm)
+        phi_ref[h, cols, :] = phi
+        p1_ref[h, cols, :], p2_ref[h, cols, :] = split2(phi)
+        t_ref[h, :, cols] = jnp.concatenate(split2(features_t(ext_ref[h, :, cols], dm)), 0)
+
+
 def gather_slots(me_ref, slots, scr):
     me = me_ref[0]
     size = slots[0].shape[0]
@@ -245,40 +265,47 @@
 
 
 def forward_kernel(dm, scale, n, parts, me_ref, t_ref, *rest):
-    intra, rest = rest[: 4 * len(parts)], rest[4 * len(parts) :]
-    slots, (student_ref, g_ref, gd_ref), backs = rest[:n], rest[n : n + 3], rest[n + 3 : 2 * n + 3]
+    used, rest = rest[: 6 * len(parts)], rest[6 * len(parts) :]
+    slots, outs, backs = rest[:n], rest[n : n + 3], rest[n + 3 : 2 * n + 3]
     scr, back_scr = rest[2 * n + 3 :]
     gather_slots(me_ref, slots, scr)
     for p, (h0, count) in enumerate(parts):
         for i in range(count):
-            numer, denom, phi, phi_t = [ref[i] for ref in intra[4 * p : 4 * p + 4]]
-            outs = forward_head(dm, scale, head_rows(scr, dm, h0 + i), t_ref[h0 + i], numer, denom, phi, phi_t)
-            for ref, value in zip((student_ref, g_ref, gd_ref), outs):
-                ref[h0 + i] = value
-            back_scr[(h0 + i) * dm.rows : (h0 + i + 1) * dm.rows, :] = outs[3]
+            h = h0 + i
+            refs = [ref.at[i] for ref in used[6 * p : 6 * p + 6]]
+            back = forward_head(dm, scale, head_rows(scr, dm, h), t_ref.at[h], *refs, *[ref.at[h] for ref in outs])
+            back_scr[h * dm.rows : (h + 1) * dm.rows, :] = back
     scatter_slots(me_ref, backs, back_scr)
 
 
-def forward_head(dm, scale, state, teacher, numer, part, phi, phi_t):
+def forward_head(
+    dm, scale, state, teacher, numer_ref, denom_ref, phi_ref, p1_ref, p2_ref, phi_t_ref, student_ref, g_ref, gd_ref
+):
     hd = state.shape[1]
     s_pack = jnp.concatenate(split2(state), 1)
     s_pack = jnp.concatenate([s_pack, jnp.zeros((dm.lanes - dm.rows, 2 * hd), bf16)], 0)
-    p1, p2 = split2(phi)
-    prod = dot(p1, s_pack) + dot(p2, s_pack)
-    numer = numer + (prod[:, :hd] + prod[:, hd:])
-    weighted = phi * count_of(state, dm)
-    for c in range(dm.lanes // LANES):
-        part = part + weighted[:, c * LANES : (c + 1) * LANES]
-    inv = 1.0 / jnp.sum(part, 1, keepdims=True)
-    y = numer * inv
-    g_out = scale * (y - teacher.astype(f32))
-    g_numer = g_out * inv
-    g_denom = -jnp.sum(g_out * y, 1, keepdims=True) * inv
-    t1, t2 = split2(phi_t)
-    g_pack = jnp.concatenate(split2(g_numer), 1)
-    prod = dot(t1, g_pack) + dot(t2, g_pack)
-    back = with_count(prod[:, :hd] + prod[:, hd:], jnp.sum(phi * g_denom, 0, keepdims=True), dm)
-    return y.astype(bf16), g_numer, jnp.broadcast_to(g_denom, part.shape), back
+    before = count_of(state, dm)
+    back, count = 0.0, 0.0
+    for rows in tiles(teacher.shape[0]):
+        phi = phi_ref[rows]
+        prod = dot(p1_ref[rows], s_pack) + dot(p2_ref[rows], s_pack)
+        numer = numer_ref[rows] + (prod[:, :hd] + prod[:, hd:])
+        weighted = phi * before
+        part = denom_ref[rows]
+        for c in range(0, dm.lanes, LANES):
+            part = part + weighted[:, c : c + LANES]
+        inv = 1.0 / jnp.sum(part, 1, keepdims=True)
+        y = numer * inv
+        student_ref[rows] = y.astype(bf16)
+        g_out = scale * (y - teacher[rows].astype(f32))
+        g_numer = g_out * inv
+        g_denom = -jnp.sum(g_out * y, 1, keepdims=True) * inv
+        g_ref[rows] = g_numer
+        gd_ref[rows] = jnp.broadcast_to(g_denom, part.shape)
+        count = count + jnp.sum(phi * g_denom, 0, keepdims=True)
+        back = back + dot(phi_t_ref[:, rows], jnp.concatenate(split2(g_numer), 1))
+    back = back[: dm.rows] + back[dm.rows :]
+    return with_count(back[:, :hd] + back[:, hd:], count, dm)
 
 
 def count_column(state, dm):
@@ -286,61 +313,60 @@
     return jnp.sum(jnp.where(row == lane, count_of(state, dm), 0.0), 1, keepdims=True)
 
 
-def backward_kernel(dm, tile, n, h0, me_ref, q_ref, k_ref, v_ref, wq_ref, wk_ref, g_ref, gd_ref, *rest):
-    slots, (gk_ref, wgrad_ref, scr) = rest[:n], rest[n:]
-    h = h0 + pl.program_id(0)
-    q, k, v = q_ref[h], k_ref[h], v_ref.at[h]
-
-    @pl.when(pl.program_id(0) == 0)
+def backward_kernel(dm, tile, n, h0, me_ref, q_ref, vt_ref, g_ref, gd_ref, q_pack_ref, k_pack_ref, q_two_ref, ext_ref, *rest):
+    slots, (gk_ref, wgrad_ref, scr) = rest[:n], rest[n : n + 3]
+    i0 = pl.program_id(0)
+    h = h0 + i0
+
+    @pl.when(i0 == 0)
     def _():
         gather_slots(me_ref, slots, scr)
         wgrad_ref[...] = jnp.zeros_like(wgrad_ref)
 
     state = head_rows(scr, dm, h)
-    wq = wq_ref[...].astype(bf16)
-    q_pack, k_pack, k1, k2 = packs(q, k, wq, wk_ref[...].astype(bf16), dm)
-    k_two = jnp.concatenate([k1, k2], 0)
-    ext = dot(rolled(wq, dm), q, NT)
     w = dm.width
-    q1, q2 = split2(ext[:w])
-    q_two = jnp.concatenate([q1, q2], 0)
-    g_numer = g_ref[h]
-    g_hi = g_numer.astype(bf16)
-    tokens = q.shape[0]
+    q_pack, k_pack, q_two, vt = q_pack_ref.at[i0], k_pack_ref.at[i0], q_two_ref.at[i0], vt_ref.at[h]
+    g_numer, g_denom, ext = g_ref.at[h], gd_ref.at[h], ext_ref.at[i0]
+    s_aug = jnp.concatenate(
+        [state, jnp.where(positions((1, LANES), 1) == 0, count_column(state, dm), 0.0)], 1
+    )
+    s1, s2 = split2(s_aug)
+    s_two = jnp.concatenate([s1, s2], 0)
+    count = q_pack.shape[0] // tile
     below = positions((tile, tile), 0) >= positions((tile, tile), 1)
-    count = tokens // tile
-    g_k = [jnp.zeros((w, tile), f32) for _ in range(count)]
-    g_q = []
+    g_q, g_k = [], 0.0
     for i in range(count):
         rows = slice(i * tile, (i + 1) * tile)
-        gd = gd_ref[h, rows, :]
-        gd = jnp.concatenate([gd] * (tile // LANES), 1)
-        total = jnp.zeros((w, tile), f32)
-        for j in range(i + 1):
-            cols = slice(j * tile, (j + 1) * tile)
-            t = dot(q_pack[rows], k_pack[:, cols])
-            score = (dot(g_hi[rows], v[cols], NT) + gd) * t
-            if j == i:
-                score = jnp.where(below, score, 0.0)
-            hi, lo = split2(score)
-            both = dot(k_two[:, cols], hi, NT)
-            total = total + (both[:w] + both[w:]) + dot(k1[:, cols], lo, NT)
-            both = dot(q_two[:, rows], hi)
-            g_k[j] = g_k[j] + (both[:w] + both[w:]) + dot(q1[:, rows], lo)
-        g_q.append(total)
-    gk_ref[pl.program_id(0)] = jnp.concatenate(g_k, 1)
+        width = (i + 1) * tile
+        t = dot(q_pack[rows], k_pack[:, :width])
+        g_weight = dot(g_numer[rows].astype(bf16), vt[:, :width]) + jnp.concatenate([g_denom[rows]] * (width // LANES), 1)
+        score = g_weight * t
+        last = jnp.where(below, score[:, width - tile :], 0.0)
+        hi, lo = split2(jnp.concatenate([score[:, : width - tile], last], 1) if i else last)
+        both = dot(k_pack[: 2 * w, :width], hi, NT)
+        g_q.append(both[:w] + both[w:] + dot(k_pack[:w, :width], lo, NT))
+        both = dot(q_two[:, rows], hi)
+        part = both[:w] + both[w:] + dot(q_two[:w, rows], lo)
+        rest = count * tile - width
+        g_k = g_k + (jnp.concatenate([part, jnp.zeros((w, rest), f32)], 1) if rest else part)
+    gk_ref[i0] = g_k
     first = positions((1, LANES), 1) == 0
-    s_aug = jnp.concatenate([state, jnp.where(first, count_column(state, dm), 0.0)], 1)
-    g_aug = jnp.concatenate([g_numer, jnp.where(first, gd_ref[h], 0.0)], 1)
-    s1, s2 = split2(s_aug)
-    a1, a2 = split2(g_aug)
-    both = dot(jnp.concatenate([s1, s2], 0), a1, NT)
+    a1, a2 = split2(jnp.concatenate([g_numer[...], jnp.where(first, g_denom[...], 0.0)], 1))
+    both = dot(s_two, a1, NT)
     g_phi = both[: dm.rows] + both[dm.rows :] + dot(s1, a2, NT)
-    total = jnp.concatenate(g_q, 1) + feature_grad_t(ext, g_phi, dm)
-    wgrad_ref[...] += dot(total.astype(bf16), q)
-
-
-def key_kernel(dm, n, parts, me_ref, k_ref, v_ref, wk_ref, *rest):
+    total = jnp.concatenate(g_q, 1) + feature_grad_t(ext[...], g_phi, dm)
+    wgrad_ref[...] += dot(total.astype(bf16), q_ref[h])
+
+
+def saving_kernel(body, n_in, *refs):
+    src, dst, sem = refs[n_in - 1], refs[-3], refs[-1]
+    copy = pltpu.make_async_copy(src, dst, sem.at[0])
+    pl.when(pl.program_id(0) == 0)(copy.start)
+    body(*refs[: n_in - 1], *refs[n_in:-3], refs[-2])
+    pl.when(pl.program_id(0) == pl.num_programs(0) - 1)(copy.wait)
+
+
+def key_kernel(dm, n, parts, me_ref, k_ref, vt_ref, wk_ref, *rest):
     slots, backs, (out_ref, scr) = rest[:n], rest[n:-2], rest[-2:]
     gather_slots(me_ref, slots, scr)
     w = dm.width
@@ -349,9 +375,10 @@
     grad = jnp.zeros((w, out_ref.shape[1]), f32)
     for (h0, count), gk_ref in zip(parts, backs[::2]):
         for i in range(count):
-            k, v = k_ref[h0 + i], v_ref[h0 + i]
             state = head_rows(scr, dm, h0 + i)
-            g_phi = dot(state.astype(bf16), v, NT) + count_column(state, dm)
+            column, state = count_column(state, dm), state.astype(bf16)
+            k = k_ref[h0 + i]
+            g_phi = dot(state, vt_ref[h0 + i]) + column
             total = gk_ref[i] + feature_grad_t(dot(w_ext, k, NT), g_phi, dm)
             grad = grad + dot(total.astype(bf16), k)
     out_ref[w:] = grad
@@ -364,7 +391,7 @@
 
 
 def placed(args, specs):
-    spaces = {id(HBM): pltpu.HBM, id(VMEM): pltpu.VMEM}
+    spaces = {id(HBM): pltpu.HBM, id(VMEM): pltpu.VMEM, id(SMEM): pltpu.SMEM}
     return [
         pltpu.with_memory_space_constraint(a, spaces[id(s)]) if id(s) in spaces else a
         for a, s in zip(args, specs)
@@ -419,14 +446,11 @@
 
 def summed(array):
     for axis in ("head", "seq", "seg"):
-        n = lax.axis_size(axis)
-        got = [shifted(array, axis, [(i, i ^ d) for i in range(n)]) for d in range(1, n)]
-        array = functools.reduce(jnp.add, [array] + got)
+        array = functools.reduce(jnp.add, exchange([array] * lax.axis_size(axis), axis))
     return array
 
 
-INTRA_SPLIT = (2, 2)
-BACK_SPLIT = (1, 2, 1)
+SPLIT = (1, 2, 1)
 
 
 def split_heads(heads, split):
@@ -455,37 +479,64 @@
     grad_shape = pltpu.VMEM((dm.width, hd), f32)
     slots = [pltpu.VMEM((heads * dm.rows, hd), f32)]
 
-    sources = (keys, values, queries, teacher, wk, wq)
+    sources = (wk, keys, values, wq)
     called = call(
         functools.partial(state_kernel, dm, n),
         (),
         (me, *sources),
         [SMEM] + [HBM] * len(sources),
-        [slot_shape] * n + [pltpu.VMEM(a.shape, a.dtype) for a in sources],
-        [VMEM] * (n + len(sources)),
-        slots + [pltpu.SemaphoreType.DMA((2 * heads,)), pltpu.SemaphoreType.DMA((4,))],
+        [slot_shape] * n + [pltpu.VMEM(a.shape, a.dtype) for a in sources] + [pltpu.SMEM((2,), jnp.int32)],
+        [VMEM] * (n + len(sources)) + [SMEM],
+        slots + [pltpu.SemaphoreType.DMA((len(sources),))],
         4 * heads * tokens * dm.rows * hd,
     )
-    states, (keys, values, queries, teacher, wk, wq) = called[:n], called[n:]
-    intra = []
-    intra_parts = split_heads(heads, INTRA_SPLIT)
+    states, (wk, keys, values, wq, me) = called[:n], called[n:]
+    vt, queries, teacher = call(
+        turn_kernel,
+        (),
+        (values, queries, teacher),
+        [VMEM, HBM, HBM],
+        [pltpu.VMEM((heads, hd, tokens), bf16)] + [pltpu.VMEM(a.shape, bf16) for a in (queries, teacher)],
+        [VMEM] * 3,
+        [pltpu.SemaphoreType.DMA((2,))],
+        heads * tokens * hd * hd,
+    )
+    intra, packed, intra_parts = [], [], split_heads(heads, SPLIT)
     for h0, count in intra_parts:
-        shapes = [
-            pltpu.VMEM((count, tokens, hd), f32),
-            pltpu.VMEM((count, tokens, LANES), f32),
-            pltpu.VMEM((count, tokens, dm.lanes), f32),
-            pltpu.VMEM((count, dm.rows, tokens), f32),
-        ]
-        intra += call(
+        outs = call(
             functools.partial(intra_kernel, dm, tile, h0),
             (count,),
             (queries, keys, values, wq, wk),
             [VMEM] * 5,
-            shapes,
-            [VMEM] * len(shapes),
+            [
+                pltpu.VMEM((count, tokens, hd), f32),
+                pltpu.VMEM((count, tokens, LANES), f32),
+                pltpu.VMEM((count, tokens, LANES), bf16),
+                pltpu.VMEM((count, LANES, tokens), bf16),
+                pltpu.VMEM((count, 2 * dm.width, tokens), bf16),
+                pltpu.VMEM((count, dm.quad, tokens), f32),
+            ],
+            [VMEM] * 6,
             [],
             4 * count * tokens * tokens * hd,
         )
+        outs += call(
+            functools.partial(feature_kernel, dm, h0),
+            (count,),
+            (queries, wq, outs[5]),
+            [VMEM] * 3,
+            [
+                pltpu.VMEM((count, tokens, dm.lanes), f32),
+                pltpu.VMEM((count, tokens, dm.lanes), bf16),
+                pltpu.VMEM((count, tokens, dm.lanes), bf16),
+                pltpu.VMEM((count, 2 * dm.rows, tokens), bf16),
+            ],
+            [VMEM] * 4,
+            [],
+            4 * count * tokens * dm.lanes * hd,
+        )
+        intra += outs[:2] + outs[6:]
+        packed.append(outs[2:6])
     prev = carried(me, states, False)
     student, g_numer, g_denom, *back = call(
         functools.partial(forward_kernel, dm, scale, n, intra_parts),
@@ -498,23 +549,34 @@
         8 * heads * tokens * dm.lanes * hd,
     )
     backs = []
-    back_parts = split_heads(heads, BACK_SPLIT)
-    for h0, count in back_parts:
-        backs += call(
-            functools.partial(backward_kernel, dm, tile, n, h0),
+    for part, (h0, count) in enumerate(intra_parts):
+        body = functools.partial(backward_kernel, dm, tile, n, h0)
+        args = (me, queries, vt, g_numer, g_denom, *packed[part], *prev)
+        outs = [pltpu.VMEM((count, dm.width, tokens), f32), grad_shape]
+        specs, scratch = [VMEM] * len(outs), slots
+        if part == 0:
+            args += (student,)
+            body = functools.partial(saving_kernel, body, len(args))
+            outs, specs = outs + [pltpu.HBM(student.shape, bf16)], specs + [HBM]
+            scratch = slots + [pltpu.SemaphoreType.DMA((1,))]
+        outs = call(
+            body,
             (count,),
-            (me, queries, keys, values, wq, wk, g_numer, g_denom, *prev),
-            [SMEM] + [VMEM] * (7 + n),
-            [pltpu.VMEM((count, dm.width, tokens), f32), grad_shape],
-            [VMEM, VMEM],
-            slots,
+            args,
+            [SMEM] + [VMEM] * (len(args) - 1),
+            outs,
+            specs,
+            scratch,
             8 * count * tokens * tokens * hd,
         )
+        if part == 0:
+            student = outs[2]
+        backs += outs[:2]
     later = carried(me, back, True)
     grads = call(
-        functools.partial(key_kernel, dm, n, back_parts),
+        functools.partial(key_kernel, dm, n, intra_parts),
         (),
-        (me, keys, values, wk, *later, *backs),
+        (me, keys, vt, wk, *later, *backs),
         [SMEM] + [VMEM] * (3 + n + len(backs)),
         [pltpu.VMEM((2 * dm.width, hd), f32)],
         [VMEM],

time: 84.9 us -> 75.4 us (0.89)
  Pallas kernels: 38.5 us -> 30 us
  local copies, waits for them, and re-layouts: 1.58 us -> 0.61 us
    pallas_call x10 -> x15, Pallas kernels: 38.5 us -> 30 us  [call(): pl.pallas_call(body, grid=grid, in_specs=specs, out_specs=out_specs, out_...]
    unnamed x1 -> x0, local copies, waits for them, and re-layouts: 0.97 us -> none
  transfers between devices with their start and end apart: 25 -> 25, of which waited for: 10 -> 11; matrix products, arithmetic and copies ran while one was open for 1% -> 0% of each run, Pallas kernels for 30% -> 30%
where the time goes in v3:
time: 75.4 us; the launch traced here: 75.2 us
  starting transfers between devices  32.1 us (43%)
  Pallas kernels  30 us (40%)
  waiting for transfers between devices  11.6 us (15%)
  between operations  0.85 us (1%)
    ppermute x25, starting transfers between devices, shifted(): return lax.ppermute(array, axis, pairs)  32.1 us
    pallas_call x15, Pallas kernels, call(): pl.pallas_call(body, grid=grid, in_specs=specs, out_specs=out_specs, out_...  30 us
    ppermute x25, waiting for transfers between devices, shifted(): return lax.ppermute(array, axis, pairs)  11.6 us
  transfers between devices with their start and end apart: 25, of which 11 were waited for; matrix products, arithmetic and copies ran while one was open for 0% of the time, Pallas kernels for 30%

profile of v3, /device:TPU:0, one launch (start us, length us, event | category | flops | bytes accessed | tf_op | source)
XLA Modules:
  0.0 75.2 jit_solution(14903243845912316822)
XLA Ops:
  0.6 0.1 pad_add_fusion.me_ref
  0.7 3.2 %shard_map.85 = (f32[160,128]{1,0:T(8,128)S(1)}, f32[160,128]{1,0:T(8,128)S(1)}, f32[160,128]{1,0:T(8,128)S(1)}, f32[160,128]{1,0:T(8,128)S(1)}, f32[16,128]{1,0...) custom-call(s32[2]{0:T(128)S(1)} %pad_add_fusion.me_ref, ...), custom_call_target="tpu_custom_call" | custom-call | flops 335544320 | tf_op jit(solution)/shard_map/pallas_call | solution.py:402
  3.9 3.0 %collective-permute-start = (f32[160,128]{1,0:T(8,128)S(1)}, f32[160,128]{1,0:T(8,128)S(1)}, u32[]{:S(2)}, u32[]{:S(2)}) collective-permute-start(f32[160,128]{1,0:T(8,128)S(1)} %get-tuple-element.97), channel_id=1, source_target_pairs={{0,8},{8,0},{16,24},{24,16},{1,9},{9,1},{17,25},{25,17},{2,10},{10... | collective-permute-start | bytes 245768 | tf_op jit(solution)/shard_map/ppermute | solution.py:417
  7.0 1.5 %collective-permute-start.1 = (f32[160,128]{1,0:T(8,128)S(1)}, f32[160,128]{1,0:T(8,128)S(1)}, u32[]{:S(2)}, u32[]{:S(2)}) collective-permute-start(f32[160,128]{1,0:T(8,128)S(1)} %get-tuple-element.98), channel_id=1, source_target_pairs={{0,16},{8,24},{16,0},{24,8},{1,17},{9,25},{17,1},{25,9},{2,18},{10... | collective-permute-start | bytes 245768 | tf_op jit(solution)/shard_map/ppermute | solution.py:417
  8.5 1.6 %shard_map.86 = (bf16[4,128,1024]{2,1,0:T(8,128)(2,1)S(1)}, bf16[4,1024,128]{2,1,0:T(8,128)(2,1)S(1)}, bf16[4,1024,128]{2,1,0:T(8,128)(2,1)S(1)}) custom-call(bf16[4,1024,128]{2,1,0:T(8,128)(2,1)S(1)} %get-tuple-element.68.v_ref, bf16[4,1024,128]{2,1,0:T(8,128)(2,1)} %q_hbm.1, bf16[4,1024,128]{2,1,0:T(8,128)(2,1)} %t_hbm.1), custom_call_target="tpu_custom_call" | custom-call | flops 67108864 | tf_op jit(solution)/shard_map/pallas_call | solution.py:402
  10.1 1.8 %shard_map.87 = (f32[1,1024,128]{2,1,0:T(8,128)S(1)}, f32[1,1024,128]{2,1,0:T(8,128)S(1)}, bf16[1,1024,128]{2,1,0:T(8,128)(2,1)S(1)}, bf16[1,128,1024]{2,1,0:T(8...) custom-call(bf16[4,1024,128]{2,1,0:T(8,128)(2,1)S(1)} %get-tuple-element.69.q_ref.refs_1_, ...), custom_call_target="tpu_custom_call" | custom-call | flops 536870912 | tf_op jit(solution)/shard_map/pallas_call | solution.py:402
  11.9 0.6 shard_map.88
  12.6 1.3 %collective-permute-done.2.refs_6_ = f32[160,128]{1,0:T(8,128)S(1)} collective-permute-done((f32[160,128]{1,0:T(8,128)S(1)}, f32[160,128]{1,0:T(8,128)S(1)}, u32[]{:S(2)}, u32[]{:S(2)}) %collective-permute-start.2) | collective-permute-done | bytes 81952 | tf_op jit(solution)/shard_map/ppermute | solution.py:417
  13.9 3.7 %collective-permute-start.5 = (f32[160,128]{1,0:T(8,128)S(1)}, f32[160,128]{1,0:T(8,128)S(1)}, u32[]{:S(2)}, u32[]{:S(2)}) collective-permute-start(f32[160,128]{1,0:T(8,128)S(1)} %add_add_fusion.1), channel_id=1, source_target_pairs={{0,6},{2,4},{4,2},{6,0},{1,7},{3,5},{5,3},{7,1},{8,14},{10,12},{12... | collective-permute-start | bytes 245768 | tf_op jit(solution)/shard_map/ppermute | solution.py:417
  17.5 0.8 %collective-permute-start.3 = (f32[160,128]{1,0:T(8,128)S(1)}, f32[160,128]{1,0:T(8,128)S(1)}, u32[]{:S(2)}, u32[]{:S(2)}) collective-permute-start(f32[160,128]{1,0:T(8,128)S(1)} %add_add_fusion.1), channel_id=1, source_target_pairs={{0,2},{2,0},{4,6},{6,4},{1,3},{3,1},{5,7},{7,5},{8,10},{10,8},{12,... | collective-permute-start | bytes 245768 | tf_op jit(solution)/shard_map/ppermute | solution.py:417
  18.3 3.6 %shard_map.89 = (f32[2,1024,128]{2,1,0:T(8,128)S(1)}, f32[2,1024,128]{2,1,0:T(8,128)S(1)}, bf16[2,1024,128]{2,1,0:T(8,128)(2,1)S(1)}, bf16[2,128,1024]{2,1,0:T(8...) custom-call(bf16[4,1024,128]{2,1,0:T(8,128)(2,1)S(1)} %get-tuple-element.69.q_ref.refs_1_, ...), custom_call_target="tpu_custom_call" | custom-call | flops 1073741824 | tf_op jit(solution)/shard_map/pallas_call | solution.py:402
  21.9 1.3 %collective-permute-done.4.refs_1_ = f32[160,128]{1,0:T(8,128)S(1)} collective-permute-done((f32[160,128]{1,0:T(8,128)S(1)}, f32[160,128]{1,0:T(8,128)S(1)}, u32[]{:S(2)}, u32[]{:S(2)}) %collective-permute-start.4) | collective-permute-done | bytes 81952 | tf_op jit(solution)/shard_map/ppermute | solution.py:417
  23.2 0.1 shard_map.93
  23.3 1.3 %collective-permute-start.6 = (f32[160,128]{1,0:T(8,128)S(1)}, f32[160,128]{1,0:T(8,128)S(1)}, u32[]{:S(2)}, u32[]{:S(2)}) collective-permute-start(f32[160,128]{1,0:T(8,128)S(1)} %get-tuple-element.101), channel_id=1, source_target_pairs={{0,8},{8,0},{16,24},{24,16},{1,9},{9,1},{17,25},{25,17},{2,10},{10... | collective-permute-start | bytes 245768 | tf_op jit(solution)/shard_map/ppermute | solution.py:417
  24.6 1.5 %collective-permute-start.7 = (f32[160,128]{1,0:T(8,128)S(1)}, f32[160,128]{1,0:T(8,128)S(1)}, u32[]{:S(2)}, u32[]{:S(2)}) collective-permute-start(f32[160,128]{1,0:T(8,128)S(1)} %get-tuple-element.102), channel_id=1, source_target_pairs={{0,16},{8,24},{16,0},{24,8},{1,17},{9,25},{17,1},{25,9},{2,18},{10... | collective-permute-start | bytes 245768 | tf_op jit(solution)/shard_map/ppermute | solution.py:417
  26.1 0.7 collective-permute-start.8
  26.9 1.8 %shard_map.91 = (f32[1,1024,128]{2,1,0:T(8,128)S(1)}, f32[1,1024,128]{2,1,0:T(8,128)S(1)}, bf16[1,1024,128]{2,1,0:T(8,128)(2,1)S(1)}, bf16[1,128,1024]{2,1,0:T(8...) custom-call(bf16[4,1024,128]{2,1,0:T(8,128)(2,1)S(1)} %get-tuple-element.69.q_ref.refs_1_, ...), custom_call_target="tpu_custom_call" | custom-call | flops 536870912 | tf_op jit(solution)/shard_map/pallas_call | solution.py:402
  28.7 0.6 shard_map.92
  29.3 1.3 %shard_map.90 = (f32[2,1024,256]{2,1,0:T(8,128)S(1)}, bf16[2,1024,256]{2,1,0:T(8,128)(2,1)S(1)}, bf16[2,1024,256]{2,1,0:T(8,128)(2,1)S(1)}, bf16[2,320,1024]{2,1,0:T(8,128)(2,1)S(1)}) custom-call(bf16[4,1024,128]{2,1,0:T(8,128)(2,1)S(1)} %get-tuple-element.69.q_ref.refs_1_, f32[16,128]{1,0:T(8,128)S(1)} %get-tuple-element.73.wq_ref, ...), custom_call_target="tpu_custom_call" | custom-call | flops 268435456 | tf_op jit(solution)/shard_map/pallas_call | solution.py:402
  30.7 0.8 %collective-permute-done.8.rest_21_.refs_12_.rest_3_ = f32[160,128]{1,0:T(8,128)S(1)} collective-permute-done((f32[160,128]{1,0:T(8,128)S(1)}, f32[160,128]{1,0:T(8,128)S(1)}, u32[]{:S(2)}, u32[]{:S(2)}) %collective-permute-start.8) | collective-permute-done | bytes 81952 | tf_op jit(solution)/shard_map/ppermute | solution.py:417
  31.5 2.9 %shard_map.94 = (bf16[4,1024,128]{2,1,0:T(8,128)(2,1)S(1)}, f32[4,1024,128]{2,1,0:T(8,128)S(1)}, f32[4,1024,128]{2,1,0:T(8,128)S(1)}, f32[160,128]{1,0:T(8,128)S...) custom-call(s32[2]{0:T(128)S(4)} %get-tuple-element.67.me_ref.refs_0_, ...), custom_call_target="tpu_custom_call" | custom-call | flops 1073741824 | tf_op jit(solution)/shard_map/pallas_call | solution.py:402
  34.4 0.6 collective-permute-start.9
  34.9 1.5 %collective-permute-start.10 = (f32[160,128]{1,0:T(8,128)S(1)}, f32[160,128]{1,0:T(8,128)S(1)}, u32[]{:S(2)}, u32[]{:S(2)}) collective-permute-start(f32[160,128]{1,0:T(8,128)S(1)} %get-tuple-element.113), channel_id=1, source_target_pairs={{0,16},{8,24},{16,0},{24,8},{1,17},{9,25},{17,1},{25,9},{2,18},{10... | collective-permute-start | bytes 245768 | tf_op jit(solution)/shard_map/ppermute | solution.py:417
  36.4 1.5 %collective-permute-start.11 = (f32[160,128]{1,0:T(8,128)S(1)}, f32[160,128]{1,0:T(8,128)S(1)}, u32[]{:S(2)}, u32[]{:S(2)}) collective-permute-start(f32[160,128]{1,0:T(8,128)S(1)} %get-tuple-element.114), channel_id=1, source_target_pairs={{0,24},{8,16},{16,8},{24,0},{1,25},{9,17},{17,9},{25,1},{2,26},{10... | collective-permute-start | bytes 245768 | tf_op jit(solution)/shard_map/ppermute | solution.py:417
  37.9 5.6 %shard_map.97 = (f32[2,16,1024]{2,1,0:T(8,128)S(1)}, f32[16,128]{1,0:T(8,128)S(1)}) custom-call(s32[2]{0:T(128)S(4)} %get-tuple-element.67.me_ref.refs_0_, bf16[4,1024,128]{2,1,0:T(8,128)(2,1)S(1)} %get-tuple-element.69.q_ref.refs_1_, bf16[4,128,1024]{2,1,0:T(8,128)(2,1)S(1)} %get-tuple-element.70.refs_2_.vt_ref, ...), custom_call_target="tpu_custom_call" | custom-call | flops 2147483648 | tf_op jit(solution)/shard_map/pallas_call | solution.py:402
  43.6 2.5 %collective-permute-start.14 = (f32[160,128]{1,0:T(8,128)S(1)}, f32[160,128]{1,0:T(8,128)S(1)}, u32[]{:S(2)}, u32[]{:S(2)}) collective-permute-start(f32[160,128]{1,0:T(8,128)S(1)} %add_add_fusion), channel_id=1, source_target_pairs={{0,6},{2,4},{4,2},{6,0},{1,7},{3,5},{5,3},{7,1},{8,14},{10,12},{12... | collective-permute-start | bytes 245768 | tf_op jit(solution)/shard_map/ppermute | solution.py:417
  46.1 1.9 %collective-permute-start.12 = (f32[160,128]{1,0:T(8,128)S(1)}, f32[160,128]{1,0:T(8,128)S(1)}, u32[]{:S(2)}, u32[]{:S(2)}) collective-permute-start(f32[160,128]{1,0:T(8,128)S(1)} %add_add_fusion), channel_id=1, source_target_pairs={{0,2},{2,0},{4,6},{6,4},{1,3},{3,1},{5,7},{7,5},{8,10},{10,8},{12,... | collective-permute-start | bytes 245768 | tf_op jit(solution)/shard_map/ppermute | solution.py:417
  48.0 2.7 %shard_map.98 = (f32[1,16,1024]{2,1,0:T(8,128)S(1)}, f32[16,128]{1,0:T(8,128)S(1)}) custom-call(s32[2]{0:T(128)S(4)} %get-tuple-element.67.me_ref.refs_0_, bf16[4,1024,128]{2,1,0:T(8,128)(2,1)S(1)} %get-tuple-element.69.q_ref.refs_1_, bf16[4,128,1024]{2,1,0:T(8,128)(2,1)S(1)} %get-tuple-element.70.refs_2_.vt_ref, ...), custom_call_target="tpu_custom_call" | custom-call | flops 1073741824 | tf_op jit(solution)/shard_map/pallas_call | solution.py:402
  50.7 0.9 %collective-permute-done.13.refs_1_ = f32[160,128]{1,0:T(8,128)S(1)} collective-permute-done((f32[160,128]{1,0:T(8,128)S(1)}, f32[160,128]{1,0:T(8,128)S(1)}, u32[]{:S(2)}, u32[]{:S(2)}) %collective-permute-start.13) | collective-permute-done | bytes 81952 | tf_op jit(solution)/shard_map/ppermute | solution.py:417
  51.6 0.1 shard_map.96
  51.7 0.6 collective-permute-start.15
  52.3 1.5 %collective-permute-start.16 = (f32[160,128]{1,0:T(8,128)S(1)}, f32[160,128]{1,0:T(8,128)S(1)}, u32[]{:S(2)}, u32[]{:S(2)}) collective-permute-start(f32[160,128]{1,0:T(8,128)S(1)} %get-tuple-element.117), channel_id=1, source_target_pairs={{0,16},{8,24},{16,0},{24,8},{1,17},{9,25},{17,1},{25,9},{2,18},{10... | collective-permute-start | bytes 245768 | tf_op jit(solution)/shard_map/ppermute | solution.py:417
  53.8 1.5 %collective-permute-start.17 = (f32[160,128]{1,0:T(8,128)S(1)}, f32[160,128]{1,0:T(8,128)S(1)}, u32[]{:S(2)}, u32[]{:S(2)}) collective-permute-start(f32[160,128]{1,0:T(8,128)S(1)} %get-tuple-element.118), channel_id=1, source_target_pairs={{0,24},{8,16},{16,8},{24,0},{1,25},{9,17},{17,9},{25,1},{2,26},{10... | collective-permute-start | bytes 245768 | tf_op jit(solution)/shard_map/ppermute | solution.py:417
  55.3 2.7 %shard_map.95 = (f32[1,16,1024]{2,1,0:T(8,128)S(1)}, f32[16,128]{1,0:T(8,128)S(1)}, bf16[4,1024,128]{2,1,0:T(8,128)(2,1)}) custom-call(s32[2]{0:T(128)S(4)} %get-tuple-element.67.me_ref.refs_0_, bf16[4,1024,128]{2,1,0:T(8,128)(2,1)S(1)} %get-tuple-element.69.q_ref.refs_1_, bf16[4,128,1024]{2,1,0:T(8,128)(2,1)S(1)} %get-tuple-element.70.refs_2_.vt_ref, ...), custom_call_target="tpu_custom_call" | custom-call | flops 1073741824 | tf_op jit(solution)/shard_map/pallas_call | solution.py:402
  58.0 1.1 %collective-permute-done.17.rest_3_ = f32[160,128]{1,0:T(8,128)S(1)} collective-permute-done((f32[160,128]{1,0:T(8,128)S(1)}, f32[160,128]{1,0:T(8,128)S(1)}, u32[]{:S(2)}, u32[]{:S(2)}) %collective-permute-start.17) | collective-permute-done | bytes 81952 | tf_op jit(solution)/shard_map/ppermute | solution.py:417
  59.1 1.4 %shard_map.99 = f32[32,128]{1,0:T(8,128)S(1)} custom-call(s32[2]{0:T(128)S(4)} %get-tuple-element.67.me_ref.refs_0_, bf16[4,1024,128]{2,1,0:T(8,128)(2,1)S(1)} %get-tuple-element.72.k_ref, bf16[4,128,1024]{2,1,0:T(8,128)(2,1)S(1)} %get-tuple-element.70.refs_2_.vt_ref, f32[16,128]{1,0:T(8,128)S(1)} %get-tuple-element.74.wk_ref, ...), custom_call_target="tpu_custom_call" | custom-call | flops 335544320 | tf_op jit(solution)/shard_map/pallas_call | solution.py:402
  60.5 1.2 %collective-permute-done.18 = f32[32,128]{1,0:T(8,128)S(1)} collective-permute-done((f32[32,128]{1,0:T(8,128)S(1)}, f32[32,128]{1,0:T(8,128)S(1)}, u32[]{:S(2)}, u32[]{:S(2)}) %collective-permute-start.18) | collective-permute-done | bytes 16416 | tf_op jit(solution)/shard_map/ppermute | solution.py:417
  61.7 1.5 %collective-permute-start.21 = (f32[32,128]{1,0:T(8,128)S(1)}, f32[32,128]{1,0:T(8,128)S(1)}, u32[]{:S(2)}, u32[]{:S(2)}) collective-permute-start(f32[32,128]{1,0:T(8,128)S(1)} %add.45), channel_id=1, source_target_pairs={{0,24},{8,16},{16,8},{24,0},{1,25},{9,17},{17,9},{25,1},{2,26},{10... | collective-permute-start | bytes 49160 | tf_op jit(solution)/shard_map/ppermute | solution.py:417
  63.2 0.5 collective-permute-start.20
  63.7 1.5 %collective-permute-start.19 = (f32[32,128]{1,0:T(8,128)S(1)}, f32[32,128]{1,0:T(8,128)S(1)}, u32[]{:S(2)}, u32[]{:S(2)}) collective-permute-start(f32[32,128]{1,0:T(8,128)S(1)} %add.45), channel_id=1, source_target_pairs={{0,8},{8,0},{16,24},{24,16},{1,9},{9,1},{17,25},{25,17},{2,10},{10... | collective-permute-start | bytes 49160 | tf_op jit(solution)/shard_map/ppermute | solution.py:417
  65.2 1.1 %collective-permute-done.21 = f32[32,128]{1,0:T(8,128)S(1)} collective-permute-done((f32[32,128]{1,0:T(8,128)S(1)}, f32[32,128]{1,0:T(8,128)S(1)}, u32[]{:S(2)}, u32[]{:S(2)}) %collective-permute-start.21) | collective-permute-done | bytes 16416 | tf_op jit(solution)/shard_map/ppermute | solution.py:417
  66.4 0.6 collective-permute-done.20
  67.0 0.5 collective-permute-done.19
  67.5 2.5 %collective-permute-start.24 = (f32[32,128]{1,0:T(8,128)S(1)}, f32[32,128]{1,0:T(8,128)S(1)}, u32[]{:S(2)}, u32[]{:S(2)}) collective-permute-start(f32[32,128]{1,0:T(8,128)S(1)} %add_add_fusion.3), channel_id=1, source_target_pairs={{0,6},{2,4},{4,2},{6,0},{1,7},{3,5},{5,3},{7,1},{8,14},{10,12},{12... | collective-permute-start | bytes 49160 | tf_op jit(solution)/shard_map/ppermute | solution.py:417
  69.9 1.9 %collective-permute-start.22 = (f32[32,128]{1,0:T(8,128)S(1)}, f32[32,128]{1,0:T(8,128)S(1)}, u32[]{:S(2)}, u32[]{:S(2)}) collective-permute-start(f32[32,128]{1,0:T(8,128)S(1)} %add_add_fusion.3), channel_id=1, source_target_pairs={{0,2},{2,0},{4,6},{6,4},{1,3},{3,1},{5,7},{7,5},{8,10},{10,8},{12,... | collective-permute-start | bytes 49160 | tf_op jit(solution)/shard_map/ppermute | solution.py:417
  71.9 1.1 %collective-permute-done.24 = f32[32,128]{1,0:T(8,128)S(1)} collective-permute-done((f32[32,128]{1,0:T(8,128)S(1)}, f32[32,128]{1,0:T(8,128)S(1)}, u32[]{:S(2)}, u32[]{:S(2)}) %collective-permute-start.24) | collective-permute-done | bytes 16416 | tf_op jit(solution)/shard_map/ppermute | solution.py:417
  73.0 1.6 %collective-permute-done.23 = f32[32,128]{1,0:T(8,128)S(1)} collective-permute-done((f32[32,128]{1,0:T(8,128)S(1)}, f32[32,128]{1,0:T(8,128)S(1)}, u32[]{:S(2)}, u32[]{:S(2)}) %collective-permute-start.23) | collective-permute-done | bytes 16416 | tf_op jit(solution)/shard_map/ppermute | solution.py:417
  74.6 0.6 slice_bitcast_fusion
  (24 shorter events, 0.2 us)
Async XLA Ops:
  3.9 8.6 %collective-permute-start = (f32[160,128]{1,0:T(8,128)S(1)}, f32[160,128]{1,0:T(8,128)S(1)}, u32[]{:S(2)}, u32[]{:S(2)}) collective-permute-start(f32[160,128]{1,0:T(8,128)S(1)} %get-tuple-element.97), channel_id=1, source_target_pairs={{0,8},{8,0},{16,24},{24,16},{1,9},{9,1},{17,25},{25,17},{2,10},{10... | collective-permute-start | bytes 245768 | tf_op jit(solution)/shard_map/ppermute | solution.py:417
  7.0 5.6 %collective-permute-start.1 = (f32[160,128]{1,0:T(8,128)S(1)}, f32[160,128]{1,0:T(8,128)S(1)}, u32[]{:S(2)}, u32[]{:S(2)}) collective-permute-start(f32[160,128]{1,0:T(8,128)S(1)} %get-tuple-element.98), channel_id=1, source_target_pairs={{0,16},{8,24},{16,0},{24,8},{1,17},{9,25},{17,1},{25,9},{2,18},{10... | collective-permute-start | bytes 245768 | tf_op jit(solution)/shard_map/ppermute | solution.py:417
  8.5 5.3 %collective-permute-start.2 = (f32[160,128]{1,0:T(8,128)S(1)}, f32[160,128]{1,0:T(8,128)S(1)}, u32[]{:S(2)}, u32[]{:S(2)}) collective-permute-start(f32[160,128]{1,0:T(8,128)S(1)} %get-tuple-element.99), channel_id=1, source_target_pairs={{0,24},{8,16},{16,8},{24,0},{1,25},{9,17},{17,9},{25,1},{2,26},{10... | collective-permute-start | bytes 245768 | tf_op jit(solution)/shard_map/ppermute | solution.py:417
  13.9 8.1 %collective-permute-start.5 = (f32[160,128]{1,0:T(8,128)S(1)}, f32[160,128]{1,0:T(8,128)S(1)}, u32[]{:S(2)}, u32[]{:S(2)}) collective-permute-start(f32[160,128]{1,0:T(8,128)S(1)} %add_add_fusion.1), channel_id=1, source_target_pairs={{0,6},{2,4},{4,2},{6,0},{1,7},{3,5},{5,3},{7,1},{8,14},{10,12},{12... | collective-permute-start | bytes 245768 | tf_op jit(solution)/shard_map/ppermute | solution.py:417
  17.5 5.7 %collective-permute-start.4 = (f32[160,128]{1,0:T(8,128)S(1)}, f32[160,128]{1,0:T(8,128)S(1)}, u32[]{:S(2)}, u32[]{:S(2)}) collective-permute-start(f32[160,128]{1,0:T(8,128)S(1)} %add_add_fusion.1), channel_id=1, source_target_pairs={{0,4},{2,6},{4,0},{6,2},{1,5},{3,7},{5,1},{7,3},{8,12},{10,14},{12... | collective-permute-start | bytes 245768 | tf_op jit(solution)/shard_map/ppermute | solution.py:417
  17.5 5.7 %collective-permute-start.3 = (f32[160,128]{1,0:T(8,128)S(1)}, f32[160,128]{1,0:T(8,128)S(1)}, u32[]{:S(2)}, u32[]{:S(2)}) collective-permute-start(f32[160,128]{1,0:T(8,128)S(1)} %add_add_fusion.1), channel_id=1, source_target_pairs={{0,2},{2,0},{4,6},{6,4},{1,3},{3,1},{5,7},{7,5},{8,10},{10,8},{12,... | collective-permute-start | bytes 245768 | tf_op jit(solution)/shard_map/ppermute | solution.py:417
  23.3 7.3 %collective-permute-start.6 = (f32[160,128]{1,0:T(8,128)S(1)}, f32[160,128]{1,0:T(8,128)S(1)}, u32[]{:S(2)}, u32[]{:S(2)}) collective-permute-start(f32[160,128]{1,0:T(8,128)S(1)} %get-tuple-element.101), channel_id=1, source_target_pairs={{0,8},{8,0},{16,24},{24,16},{1,9},{9,1},{17,25},{25,17},{2,10},{10... | collective-permute-start | bytes 245768 | tf_op jit(solution)/shard_map/ppermute | solution.py:417
  24.6 6.1 %collective-permute-start.7 = (f32[160,128]{1,0:T(8,128)S(1)}, f32[160,128]{1,0:T(8,128)S(1)}, u32[]{:S(2)}, u32[]{:S(2)}) collective-permute-start(f32[160,128]{1,0:T(8,128)S(1)} %get-tuple-element.102), channel_id=1, source_target_pairs={{0,16},{8,24},{16,0},{24,8},{1,17},{9,25},{17,1},{25,9},{2,18},{10... | collective-permute-start | bytes 245768 | tf_op jit(solution)/shard_map/ppermute | solution.py:417
  26.1 5.3 %collective-permute-start.8 = (f32[160,128]{1,0:T(8,128)S(1)}, f32[160,128]{1,0:T(8,128)S(1)}, u32[]{:S(2)}, u32[]{:S(2)}) collective-permute-start(f32[160,128]{1,0:T(8,128)S(1)} %get-tuple-element.103), channel_id=1, source_target_pairs={{0,24},{8,16},{16,8},{24,0},{1,25},{9,17},{17,9},{25,1},{2,26},{10... | collective-permute-start | bytes 245768 | tf_op jit(solution)/shard_map/ppermute | solution.py:417
  34.4 9.2 %collective-permute-start.9 = (f32[160,128]{1,0:T(8,128)S(1)}, f32[160,128]{1,0:T(8,128)S(1)}, u32[]{:S(2)}, u32[]{:S(2)}) collective-permute-start(f32[160,128]{1,0:T(8,128)S(1)} %get-tuple-element.112), channel_id=1, source_target_pairs={{0,8},{8,0},{16,24},{24,16},{1,9},{9,1},{17,25},{25,17},{2,10},{10... | collective-permute-start | bytes 245768 | tf_op jit(solution)/shard_map/ppermute | solution.py:417
  34.9 8.6 %collective-permute-start.10 = (f32[160,128]{1,0:T(8,128)S(1)}, f32[160,128]{1,0:T(8,128)S(1)}, u32[]{:S(2)}, u32[]{:S(2)}) collective-permute-start(f32[160,128]{1,0:T(8,128)S(1)} %get-tuple-element.113), channel_id=1, source_target_pairs={{0,16},{8,24},{16,0},{24,8},{1,17},{9,25},{17,1},{25,9},{2,18},{10... | collective-permute-start | bytes 245768 | tf_op jit(solution)/shard_map/ppermute | solution.py:417
  36.4 7.1 %collective-permute-start.11 = (f32[160,128]{1,0:T(8,128)S(1)}, f32[160,128]{1,0:T(8,128)S(1)}, u32[]{:S(2)}, u32[]{:S(2)}) collective-permute-start(f32[160,128]{1,0:T(8,128)S(1)} %get-tuple-element.114), channel_id=1, source_target_pairs={{0,24},{8,16},{16,8},{24,0},{1,25},{9,17},{17,9},{25,1},{2,26},{10... | collective-permute-start | bytes 245768 | tf_op jit(solution)/shard_map/ppermute | solution.py:417
  43.6 7.1 %collective-permute-start.14 = (f32[160,128]{1,0:T(8,128)S(1)}, f32[160,128]{1,0:T(8,128)S(1)}, u32[]{:S(2)}, u32[]{:S(2)}) collective-permute-start(f32[160,128]{1,0:T(8,128)S(1)} %add_add_fusion), channel_id=1, source_target_pairs={{0,6},{2,4},{4,2},{6,0},{1,7},{3,5},{5,3},{7,1},{8,14},{10,12},{12... | collective-permute-start | bytes 245768 | tf_op jit(solution)/shard_map/ppermute | solution.py:417
  46.1 5.5 %collective-permute-start.13 = (f32[160,128]{1,0:T(8,128)S(1)}, f32[160,128]{1,0:T(8,128)S(1)}, u32[]{:S(2)}, u32[]{:S(2)}) collective-permute-start(f32[160,128]{1,0:T(8,128)S(1)} %add_add_fusion), channel_id=1, source_target_pairs={{0,4},{2,6},{4,0},{6,2},{1,5},{3,7},{5,1},{7,3},{8,12},{10,14},{12... | collective-permute-start | bytes 245768 | tf_op jit(solution)/shard_map/ppermute | solution.py:417
  46.1 5.5 %collective-permute-start.12 = (f32[160,128]{1,0:T(8,128)S(1)}, f32[160,128]{1,0:T(8,128)S(1)}, u32[]{:S(2)}, u32[]{:S(2)}) collective-permute-start(f32[160,128]{1,0:T(8,128)S(1)} %add_add_fusion), channel_id=1, source_target_pairs={{0,2},{2,0},{4,6},{6,4},{1,3},{3,1},{5,7},{7,5},{8,10},{10,8},{12,... | collective-permute-start | bytes 245768 | tf_op jit(solution)/shard_map/ppermute | solution.py:417
  51.7 6.3 %collective-permute-start.15 = (f32[160,128]{1,0:T(8,128)S(1)}, f32[160,128]{1,0:T(8,128)S(1)}, u32[]{:S(2)}, u32[]{:S(2)}) collective-permute-start(f32[160,128]{1,0:T(8,128)S(1)} %get-tuple-element.116), channel_id=1, source_target_pairs={{0,8},{8,0},{16,24},{24,16},{1,9},{9,1},{17,25},{25,17},{2,10},{10... | collective-permute-start | bytes 245768 | tf_op jit(solution)/shard_map/ppermute | solution.py:417
  52.3 5.7 %collective-permute-start.16 = (f32[160,128]{1,0:T(8,128)S(1)}, f32[160,128]{1,0:T(8,128)S(1)}, u32[]{:S(2)}, u32[]{:S(2)}) collective-permute-start(f32[160,128]{1,0:T(8,128)S(1)} %get-tuple-element.117), channel_id=1, source_target_pairs={{0,16},{8,24},{16,0},{24,8},{1,17},{9,25},{17,1},{25,9},{2,18},{10... | collective-permute-start | bytes 245768 | tf_op jit(solution)/shard_map/ppermute | solution.py:417
  53.8 5.3 %collective-permute-start.17 = (f32[160,128]{1,0:T(8,128)S(1)}, f32[160,128]{1,0:T(8,128)S(1)}, u32[]{:S(2)}, u32[]{:S(2)}) collective-permute-start(f32[160,128]{1,0:T(8,128)S(1)} %get-tuple-element.118), channel_id=1, source_target_pairs={{0,24},{8,16},{16,8},{24,0},{1,25},{9,17},{17,9},{25,1},{2,26},{10... | collective-permute-start | bytes 245768 | tf_op jit(solution)/shard_map/ppermute | solution.py:417
  60.5 1.2 %collective-permute-start.18 = (f32[32,128]{1,0:T(8,128)S(1)}, f32[32,128]{1,0:T(8,128)S(1)}, u32[]{:S(2)}, u32[]{:S(2)}) collective-permute-start(f32[32,128]{1,0:T(8,128)S(1)} %shard_map.99), channel_id=1, source_target_pairs={{0,1},{1,0},{2,3},{3,2},{4,5},{5,4},{6,7},{7,6},{8,9},{9,8},{10,11... | collective-permute-start | bytes 49160 | tf_op jit(solution)/shard_map/ppermute | solution.py:417
  61.7 4.6 %collective-permute-start.21 = (f32[32,128]{1,0:T(8,128)S(1)}, f32[32,128]{1,0:T(8,128)S(1)}, u32[]{:S(2)}, u32[]{:S(2)}) collective-permute-start(f32[32,128]{1,0:T(8,128)S(1)} %add.45), channel_id=1, source_target_pairs={{0,24},{8,16},{16,8},{24,0},{1,25},{9,17},{17,9},{25,1},{2,26},{10... | collective-permute-start | bytes 49160 | tf_op jit(solution)/shard_map/ppermute | solution.py:417
  63.2 3.7 %collective-permute-start.20 = (f32[32,128]{1,0:T(8,128)S(1)}, f32[32,128]{1,0:T(8,128)S(1)}, u32[]{:S(2)}, u32[]{:S(2)}) collective-permute-start(f32[32,128]{1,0:T(8,128)S(1)} %add.45), channel_id=1, source_target_pairs={{0,16},{8,24},{16,0},{24,8},{1,17},{9,25},{17,1},{25,9},{2,18},{10... | collective-permute-start | bytes 49160 | tf_op jit(solution)/shard_map/ppermute | solution.py:417
  63.7 3.7 %collective-permute-start.19 = (f32[32,128]{1,0:T(8,128)S(1)}, f32[32,128]{1,0:T(8,128)S(1)}, u32[]{:S(2)}, u32[]{:S(2)}) collective-permute-start(f32[32,128]{1,0:T(8,128)S(1)} %add.45), channel_id=1, source_target_pairs={{0,8},{8,0},{16,24},{24,16},{1,9},{9,1},{17,25},{25,17},{2,10},{10... | collective-permute-start | bytes 49160 | tf_op jit(solution)/shard_map/ppermute | solution.py:417
  67.5 5.5 %collective-permute-start.24 = (f32[32,128]{1,0:T(8,128)S(1)}, f32[32,128]{1,0:T(8,128)S(1)}, u32[]{:S(2)}, u32[]{:S(2)}) collective-permute-start(f32[32,128]{1,0:T(8,128)S(1)} %add_add_fusion.3), channel_id=1, source_target_pairs={{0,6},{2,4},{4,2},{6,0},{1,7},{3,5},{5,3},{7,1},{8,14},{10,12},{12... | collective-permute-start | bytes 49160 | tf_op jit(solution)/shard_map/ppermute | solution.py:417
  69.9 4.6 %collective-permute-start.23 = (f32[32,128]{1,0:T(8,128)S(1)}, f32[32,128]{1,0:T(8,128)S(1)}, u32[]{:S(2)}, u32[]{:S(2)}) collective-permute-start(f32[32,128]{1,0:T(8,128)S(1)} %add_add_fusion.3), channel_id=1, source_target_pairs={{0,4},{2,6},{4,0},{6,2},{1,5},{3,7},{5,1},{7,3},{8,12},{10,14},{12... | collective-permute-start | bytes 49160 | tf_op jit(solution)/shard_map/ppermute | solution.py:417
  69.9 4.6 %collective-permute-start.22 = (f32[32,128]{1,0:T(8,128)S(1)}, f32[32,128]{1,0:T(8,128)S(1)}, u32[]{:S(2)}, u32[]{:S(2)}) collective-permute-start(f32[32,128]{1,0:T(8,128)S(1)} %add_add_fusion.3), channel_id=1, source_target_pairs={{0,2},{2,0},{4,6},{6,4},{1,3},{3,1},{5,7},{7,5},{8,10},{10,8},{12,... | collective-permute-start | bytes 49160 | tf_op jit(solution)/shard_map/ppermute | solution.py:417

commit v4 on v3

--- a/solution.py
+++ b/solution.py
@@ -7,6 +7,7 @@
 from jax.experimental import pallas as pl
 from jax.experimental.pallas import tpu as pltpu
 from jax.sharding import PartitionSpec as P
+
 
 f32 = jnp.float32
 bf16 = jnp.bfloat16
@@ -137,27 +138,55 @@
     return jnp.sum(jnp.where(row == lane, column, 0.0), 0, keepdims=True)
 
 
+def head_at(me_ref, per, p):
+    return (me_ref[0] >> (per.bit_length() - 1)) ^ p
+
+
+def put_slots(me_ref, slots, scr, value):
+    if len(slots) == 1:
+        slots[0][...] = value
+        return
+    scr[...] = value
+    size = slots[0].shape[0]
+    for c, slot in enumerate(slots):
+        slot[...] = scr[pl.ds(pl.multiple_of(((me_ref[0] & (len(slots) - 1)) ^ c) * size, 8), size), :]
+
+
+def get_slots(me_ref, slots, scr):
+    if len(slots) == 1:
+        return slots[0][...]
+    size = slots[0].shape[0]
+    for c, slot in enumerate(slots):
+        scr[pl.ds(pl.multiple_of(((me_ref[0] & (len(slots) - 1)) ^ c) * size, 8), size), :] = slot[...]
+    return scr[...]
+
+
 def state_kernel(dm, n, me_ref, *rest):
     sources, slots, kept, at_ref, scr, sems = rest[:4], rest[4 : 4 + n], rest[4 + n : 8 + n], *rest[8 + n :]
     at_ref[0] = me_ref[0]
     at_ref[1] = me_ref[1]
     wk_ref, k_ref, v_ref = kept[:3]
     heads = k_ref.shape[0]
+    per = n // heads
     copies = [pltpu.make_async_copy(a, b, sems.at[i]) for i, (a, b) in enumerate(zip(sources, kept))]
     for copy in copies:
         copy.start()
     copies[0].wait()
     w_ext = rolled(wk_ref[...].astype(bf16), dm)
-    for copy in copies[1:]:
-        copy.wait()
-    for h in range(heads):
-        phi = features_t(dot(w_ext, k_ref[h], NT), dm)
+    copies[1].wait()
+    phis, parts = [], []
+    for p in range(heads):
+        phi = features_t(dot(w_ext, k_ref[head_at(me_ref, per, p)], NT), dm)
         part = phi[:, :LANES]
         for c in range(LANES, phi.shape[1], LANES):
             part = part + phi[:, c : c + LANES]
-        state = dot(phi.astype(bf16), v_ref[h])
-        scr[h * dm.rows : (h + 1) * dm.rows, :] = with_count(state, column_row(part, dm), dm)
-    scatter_slots(me_ref, slots, scr)
+        phis.append(phi.astype(bf16))
+        parts.append(part)
+    for copy in copies[2:]:
+        copy.wait()
+    for p in range(heads):
+        state = with_count(dot(phis[p], v_ref[head_at(me_ref, per, p)]), column_row(parts[p], dm), dm)
+        put_slots(me_ref, slots[p * per : (p + 1) * per], scr, state)
 
 
 def turn_kernel(v_ref, q_hbm, t_hbm, vt_ref, q_ref, t_ref, sems):
@@ -187,10 +216,11 @@
     return q_pack, jnp.concatenate([k1, k2, k3, k1, k2, k1, last], 0)
 
 
-def intra_kernel(dm, tile, h0, q_ref, k_ref, v_ref, wq_ref, wk_ref, *outs):
+def intra_kernel(dm, tile, per, p0, me_ref, q_ref, k_ref, v_ref, wq_ref, wk_ref, *outs):
     numer_ref, denom_ref, q_pack_ref, k_pack_ref, q_two_ref, ext_ref = outs
     h = pl.program_id(0)
-    q, k, v = q_ref[h0 + h], k_ref[h0 + h], v_ref.at[h0 + h]
+    at = head_at(me_ref, per, p0 + h)
+    q, k, v = q_ref[at], k_ref[at], v_ref.at[at]
     wq = wq_ref[...].astype(bf16)
     ext = dot(rolled(wq, dm), q, NT)
     ext_ref[h] = ext
@@ -217,28 +247,16 @@
         denom_ref[h, rows, :] = denom
 
 
-def feature_kernel(dm, h0, q_ref, wq_ref, ext_ref, phi_ref, p1_ref, p2_ref, t_ref):
+def feature_kernel(dm, per, p0, me_ref, q_ref, wq_ref, ext_ref, phi_ref, p1_ref, p2_ref, t_ref):
     h = pl.program_id(0)
+    at = head_at(me_ref, per, p0 + h)
     wq = wq_ref[...].astype(bf16)
     side = sides(wq, dm)
     for cols in tiles(q_ref.shape[1]):
-        phi = features_rows(q_ref[h0 + h, cols, :], side, dm)
+        phi = features_rows(q_ref[at, cols, :], side, dm)
         phi_ref[h, cols, :] = phi
         p1_ref[h, cols, :], p2_ref[h, cols, :] = split2(phi)
         t_ref[h, :, cols] = jnp.concatenate(split2(features_t(ext_ref[h, :, cols], dm)), 0)
-
-
-def gather_slots(me_ref, slots, scr):
-    me = me_ref[0]
-    size = slots[0].shape[0]
-    for d, slot in enumerate(slots):
-        scr[pl.ds(pl.multiple_of((me ^ d) * size, 8), size), :] = slot[...]
-
-
-def scatter_slots(me_ref, slots, scr):
-    size = slots[0].shape[0]
-    for d, slot in enumerate(slots):
-        slot[...] = scr[pl.ds(pl.multiple_of((me_ref[0] ^ d) * size, 8), size), :]
 
 
 def join_kernel(n, backward, me_ref, *refs):
@@ -259,23 +277,12 @@
         out[...] = total
 
 
-def head_rows(scr, dm, h):
-    start = h * dm.rows
-    return scr[pl.ds(start if isinstance(h, int) else pl.multiple_of(start, 8), dm.rows), :]
-
-
-def forward_kernel(dm, scale, n, parts, me_ref, t_ref, *rest):
-    used, rest = rest[: 6 * len(parts)], rest[6 * len(parts) :]
-    slots, outs, backs = rest[:n], rest[n : n + 3], rest[n + 3 : 2 * n + 3]
-    scr, back_scr = rest[2 * n + 3 :]
-    gather_slots(me_ref, slots, scr)
-    for p, (h0, count) in enumerate(parts):
-        for i in range(count):
-            h = h0 + i
-            refs = [ref.at[i] for ref in used[6 * p : 6 * p + 6]]
-            back = forward_head(dm, scale, head_rows(scr, dm, h), t_ref.at[h], *refs, *[ref.at[h] for ref in outs])
-            back_scr[h * dm.rows : (h + 1) * dm.rows, :] = back
-    scatter_slots(me_ref, backs, back_scr)
+def forward_kernel(dm, scale, per, p, i, me_ref, t_ref, *rest):
+    used, slots, outs = rest[:6], rest[6 : 6 + per], rest[6 + per : 9 + per]
+    backs, (scr,) = rest[9 + per : 9 + 2 * per], rest[9 + 2 * per :]
+    state = get_slots(me_ref, slots, scr)
+    teacher = t_ref.at[head_at(me_ref, per, p)]
+    put_slots(me_ref, backs, scr, forward_head(dm, scale, state, teacher, *[ref.at[i] for ref in used], *outs))
 
 
 def forward_head(
@@ -313,25 +320,26 @@
     return jnp.sum(jnp.where(row == lane, count_of(state, dm), 0.0), 1, keepdims=True)
 
 
-def backward_kernel(dm, tile, n, h0, me_ref, q_ref, vt_ref, g_ref, gd_ref, q_pack_ref, k_pack_ref, q_two_ref, ext_ref, *rest):
-    slots, (gk_ref, wgrad_ref, scr) = rest[:n], rest[n : n + 3]
-    i0 = pl.program_id(0)
-    h = h0 + i0
-
-    @pl.when(i0 == 0)
-    def _():
-        gather_slots(me_ref, slots, scr)
-        wgrad_ref[...] = jnp.zeros_like(wgrad_ref)
-
-    state = head_rows(scr, dm, h)
+def backward_kernel(dm, tile, per, p0, count, me_ref, q_ref, vt_ref, *rest):
+    packed, rest = rest[:4], rest[4:]
+    grads, rest = rest[: 2 * count], rest[2 * count :]
+    slots, (gk_ref, wgrad_ref, scr) = rest[: per * count], rest[per * count :]
+    grad = 0.0
+    for i in range(count):
+        state = get_slots(me_ref, slots[i * per : (i + 1) * per], scr)
+        at = head_at(me_ref, per, p0 + i)
+        refs = [ref.at[i] for ref in packed]
+        gk_ref[i], head_grad = backward_head(dm, tile, state, q_ref.at[at], vt_ref.at[at], *grads[2 * i : 2 * i + 2], *refs)
+        grad = grad + head_grad
+    wgrad_ref[...] = grad
+
+
+def backward_head(dm, tile, state, q, vt, g_numer, g_denom, q_pack, k_pack, q_two, ext):
     w = dm.width
-    q_pack, k_pack, q_two, vt = q_pack_ref.at[i0], k_pack_ref.at[i0], q_two_ref.at[i0], vt_ref.at[h]
-    g_numer, g_denom, ext = g_ref.at[h], gd_ref.at[h], ext_ref.at[i0]
     s_aug = jnp.concatenate(
         [state, jnp.where(positions((1, LANES), 1) == 0, count_column(state, dm), 0.0)], 1
     )
     s1, s2 = split2(s_aug)
-    s_two = jnp.concatenate([s1, s2], 0)
     count = q_pack.shape[0] // tile
     below = positions((tile, tile), 0) >= positions((tile, tile), 1)
     g_q, g_k = [], 0.0
@@ -349,36 +357,41 @@
         part = both[:w] + both[w:] + dot(q_two[:w, rows], lo)
         rest = count * tile - width
         g_k = g_k + (jnp.concatenate([part, jnp.zeros((w, rest), f32)], 1) if rest else part)
-    gk_ref[i0] = g_k
     first = positions((1, LANES), 1) == 0
     a1, a2 = split2(jnp.concatenate([g_numer[...], jnp.where(first, g_denom[...], 0.0)], 1))
-    both = dot(s_two, a1, NT)
+    both = dot(jnp.concatenate([s1, s2], 0), a1, NT)
     g_phi = both[: dm.rows] + both[dm.rows :] + dot(s1, a2, NT)
     total = jnp.concatenate(g_q, 1) + feature_grad_t(ext[...], g_phi, dm)
-    wgrad_ref[...] += dot(total.astype(bf16), q_ref[h])
-
-
-def saving_kernel(body, n_in, *refs):
-    src, dst, sem = refs[n_in - 1], refs[-3], refs[-1]
-    copy = pltpu.make_async_copy(src, dst, sem.at[0])
-    pl.when(pl.program_id(0) == 0)(copy.start)
-    body(*refs[: n_in - 1], *refs[n_in:-3], refs[-2])
-    pl.when(pl.program_id(0) == pl.num_programs(0) - 1)(copy.wait)
+    return g_k, dot(total.astype(bf16), q[...])
+
+
+def saving_kernel(body, per, n_in, heads, me_ref, *refs):
+    used, pieces, outs = refs[: n_in - 1], refs[n_in - 1 : n_in - 1 + heads], refs[n_in - 1 + heads :]
+    gk_ref, wgrad_ref, dst, scr, sems = outs
+    copies = [
+        pltpu.make_async_copy(piece, dst.at[head_at(me_ref, per, p)], sems.at[p]) for p, piece in enumerate(pieces)
+    ]
+    for copy in copies:
+        copy.start()
+    body(me_ref, *used, gk_ref, wgrad_ref, scr)
+    for copy in copies:
+        copy.wait()
 
 
 def key_kernel(dm, n, parts, me_ref, k_ref, vt_ref, wk_ref, *rest):
     slots, backs, (out_ref, scr) = rest[:n], rest[n:-2], rest[-2:]
-    gather_slots(me_ref, slots, scr)
+    per = n // k_ref.shape[0]
     w = dm.width
     out_ref[:w] = functools.reduce(jnp.add, [g[...] for g in backs[1::2]])
     w_ext = rolled(wk_ref[...].astype(bf16), dm)
     grad = jnp.zeros((w, out_ref.shape[1]), f32)
-    for (h0, count), gk_ref in zip(parts, backs[::2]):
+    for (p0, count), gk_ref in zip(parts, backs[::2]):
         for i in range(count):
-            state = head_rows(scr, dm, h0 + i)
-            column, state = count_column(state, dm), state.astype(bf16)
-            k = k_ref[h0 + i]
-            g_phi = dot(state, vt_ref[h0 + i]) + column
+            p = p0 + i
+            state = get_slots(me_ref, slots[p * per : (p + 1) * per], scr)
+            at = head_at(me_ref, per, p)
+            k = k_ref[at]
+            g_phi = dot(state.astype(bf16), vt_ref[at]) + count_column(state, dm)
             total = gk_ref[i] + feature_grad_t(dot(w_ext, k, NT), g_phi, dm)
             grad = grad + dot(total.astype(bf16), k)
     out_ref[w:] = grad
@@ -467,6 +480,8 @@
     heads, tokens, hd = queries.shape
     dm = Dims(query_proj.shape[1])
     n = lax.axis_size("seq")
+    assert n % heads == 0
+    per = n // heads
     heads_all = heads * lax.axis_size("head")
     tokens_all = tokens * n * lax.axis_size("seg")
     scale = 1.0 / math.sqrt(heads_all * tokens_all)
@@ -474,10 +489,8 @@
     wq, wk = query_proj.T, key_proj.T
     me = jnp.stack([lax.axis_index("seq"), lax.axis_index("seg")]).astype(jnp.int32)
     slot_shape = pltpu.VMEM((heads * dm.rows // n, hd), f32)
-    tok_shape = pltpu.VMEM((heads, tokens, hd), f32)
-    lane_shape = pltpu.VMEM((heads, tokens, LANES), f32)
     grad_shape = pltpu.VMEM((dm.width, hd), f32)
-    slots = [pltpu.VMEM((heads * dm.rows, hd), f32)]
+    scr = [pltpu.VMEM((dm.rows, hd), f32)]
 
     sources = (wk, keys, values, wq)
     called = call(
@@ -487,7 +500,7 @@
         [SMEM] + [HBM] * len(sources),
         [slot_shape] * n + [pltpu.VMEM(a.shape, a.dtype) for a in sources] + [pltpu.SMEM((2,), jnp.int32)],
         [VMEM] * (n + len(sources)) + [SMEM],
-        slots + [pltpu.SemaphoreType.DMA((len(sources),))],
+        scr + [pltpu.SemaphoreType.DMA((len(sources),))],
         4 * heads * tokens * dm.rows * hd,
     )
     states, (wk, keys, values, wq, me) = called[:n], called[n:]
@@ -501,13 +514,13 @@
         [pltpu.SemaphoreType.DMA((2,))],
         heads * tokens * hd * hd,
     )
-    intra, packed, intra_parts = [], [], split_heads(heads, SPLIT)
-    for h0, count in intra_parts:
+    intra, packed, parts = [], [], split_heads(heads, SPLIT)
+    for p0, count in parts:
         outs = call(
-            functools.partial(intra_kernel, dm, tile, h0),
+            functools.partial(intra_kernel, dm, tile, per, p0),
             (count,),
-            (queries, keys, values, wq, wk),
-            [VMEM] * 5,
+            (me, queries, keys, values, wq, wk),
+            [SMEM] + [VMEM] * 5,
             [
                 pltpu.VMEM((count, tokens, hd), f32),
                 pltpu.VMEM((count, tokens, LANES), f32),
@@ -521,10 +534,10 @@
             4 * count * tokens * tokens * hd,
         )
         outs += call(
-            functools.partial(feature_kernel, dm, h0),
+            functools.partial(feature_kernel, dm, per, p0),
             (count,),
-            (queries, wq, outs[5]),
-            [VMEM] * 3,
+            (me, queries, wq, outs[5]),
+            [SMEM] + [VMEM] * 3,
             [
                 pltpu.VMEM((count, tokens, dm.lanes), f32),
                 pltpu.VMEM((count, tokens, dm.lanes), bf16),
@@ -535,52 +548,55 @@
             [],
             4 * count * tokens * dm.lanes * hd,
         )
-        intra += outs[:2] + outs[6:]
+        intra.append(outs[:2] + outs[6:])
         packed.append(outs[2:6])
     prev = carried(me, states, False)
-    student, g_numer, g_denom, *back = call(
-        functools.partial(forward_kernel, dm, scale, n, intra_parts),
-        (),
-        (me, teacher, *intra, *prev),
-        [SMEM] + [VMEM] * (1 + len(intra) + n),
-        [pltpu.VMEM((heads, tokens, hd), bf16), tok_shape, lane_shape] + [slot_shape] * n,
-        [VMEM] * (3 + n),
-        2 * slots,
-        8 * heads * tokens * dm.lanes * hd,
-    )
+    heads_out = {}
+    for p, i, part in reversed([(p0 + i, i, part) for part, (p0, count) in enumerate(parts) for i in range(count)]):
+        heads_out[p] = call(
+            functools.partial(forward_kernel, dm, scale, per, p, i),
+            (),
+            (me, teacher, *intra[part], *prev[p * per : (p + 1) * per]),
+            [SMEM] + [VMEM] * (7 + per),
+            [
+                pltpu.VMEM((tokens, hd), bf16),
+                pltpu.VMEM((tokens, hd), f32),
+                pltpu.VMEM((tokens, LANES), f32),
+            ]
+            + [slot_shape] * per,
+            [VMEM] * (3 + per),
+            scr,
+            8 * tokens * dm.lanes * hd,
+        )
+    later = carried(me, [b for p in range(heads) for b in heads_out[p][3:]], True)
     backs = []
-    for part, (h0, count) in enumerate(intra_parts):
-        body = functools.partial(backward_kernel, dm, tile, n, h0)
-        args = (me, queries, vt, g_numer, g_denom, *packed[part], *prev)
+    for part, (p0, count) in enumerate(parts):
+        body = functools.partial(backward_kernel, dm, tile, per, p0, count)
+        args = (me, queries, vt, *packed[part])
+        for i in range(count):
+            args += tuple(heads_out[p0 + i][1:3])
+        args += tuple(prev[p0 * per : (p0 + count) * per])
         outs = [pltpu.VMEM((count, dm.width, tokens), f32), grad_shape]
-        specs, scratch = [VMEM] * len(outs), slots
+        specs, scratch = [VMEM] * len(outs), scr
         if part == 0:
-            args += (student,)
-            body = functools.partial(saving_kernel, body, len(args))
-            outs, specs = outs + [pltpu.HBM(student.shape, bf16)], specs + [HBM]
-            scratch = slots + [pltpu.SemaphoreType.DMA((1,))]
+            body = functools.partial(saving_kernel, body, per, len(args), heads)
+            args += tuple(heads_out[p][0] for p in range(heads))
+            outs, specs = outs + [pltpu.HBM((heads, tokens, hd), bf16)], specs + [HBM]
+            scratch = scr + [pltpu.SemaphoreType.DMA((heads,))]
         outs = call(
-            body,
-            (count,),
-            args,
-            [SMEM] + [VMEM] * (len(args) - 1),
-            outs,
-            specs,
-            scratch,
-            8 * count * tokens * tokens * hd,
+            body, (), args, [SMEM] + [VMEM] * (len(args) - 1), outs, specs, scratch, 8 * count * tokens * tokens * hd
         )
         if part == 0:
             student = outs[2]
         backs += outs[:2]
-    later = carried(me, back, True)
     grads = call(
-        functools.partial(key_kernel, dm, n, intra_parts),
+        functools.partial(key_kernel, dm, n, parts),
         (),
         (me, keys, vt, wk, *later, *backs),
         [SMEM] + [VMEM] * (3 + n + len(backs)),
         [pltpu.VMEM((2 * dm.width, hd), f32)],
         [VMEM],
-        slots,
+        scr,
         4 * heads * tokens * dm.rows * hd,
     )[0]
     grads = summed(grads)

time: 75.4 us -> 79 us (1.048)
  waiting for transfers between devices: 11.6 us -> 14.3 us
    ppermute x25, waiting for transfers between devices: 11.6 us -> 14.3 us  [shifted(): return lax.ppermute(array, axis, pairs)]
    pallas_call x15 -> x18, Pallas kernels: 30 us -> 30.7 us  [call(): pl.pallas_call(body, grid=grid, in_specs=specs, out_specs=out_specs, out_...]
  transfers between devices with their start and end apart: 25 -> 25, of which waited for: 11 -> 12; matrix products, arithmetic and copies ran while one was open for 0% -> 0% of each run, Pallas kernels for 30% -> 33%
where the time goes in v4:
time: 79 us; the launch traced here: 78.8 us
  starting transfers between devices  32.3 us (41%)
  Pallas kernels  30.7 us (39%)
  waiting for transfers between devices  14.3 us (18%)
  between operations  0.86 us (1%)
    ppermute x25, starting transfers between devices, shifted(): return lax.ppermute(array, axis, pairs)  32.3 us
    pallas_call x18, Pallas kernels, call(): pl.pallas_call(body, grid=grid, in_specs=specs, out_specs=out_specs, out_...  30.7 us
    ppermute x25, waiting for transfers between devices, shifted(): return lax.ppermute(array, axis, pairs)  14.3 us
  transfers between devices with their start and end apart: 25, of which 12 were waited for; matrix products, arithmetic and copies ran while one was open for 0% of the time, Pallas kernels for 33%

profile of v4, /device:TPU:0, one launch (start us, length us, event | category | flops | bytes accessed | tf_op | source)
XLA Modules:
  0.0 78.8 jit_solution(4406893154734422924)
XLA Ops:
  0.7 2.8 %shard_map.85 = (f32[160,128]{1,0:T(8,128)S(1)}, f32[160,128]{1,0:T(8,128)S(1)}, f32[160,128]{1,0:T(8,128)S(1)}, f32[160,128]{1,0:T(8,128)S(1)}, f32[16,128]{1,0...) custom-call(s32[2]{0:T(128)S(1)} %pad_add_fusion.me_ref, ...), custom_call_target="tpu_custom_call" | custom-call | flops 335544320 | tf_op jit(solution)/shard_map/pallas_call | solution.py:415
  3.5 3.0 %collective-permute-start = (f32[160,128]{1,0:T(8,128)S(1)}, f32[160,128]{1,0:T(8,128)S(1)}, u32[]{:S(2)}, u32[]{:S(2)}) collective-permute-start(f32[160,128]{1,0:T(8,128)S(1)} %get-tuple-element.95), channel_id=1, source_target_pairs={{0,8},{8,0},{16,24},{24,16},{1,9},{9,1},{17,25},{25,17},{2,10},{10... | collective-permute-start | bytes 245768 | tf_op jit(solution)/shard_map/ppermute | solution.py:430
  6.6 1.5 %collective-permute-start.1 = (f32[160,128]{1,0:T(8,128)S(1)}, f32[160,128]{1,0:T(8,128)S(1)}, u32[]{:S(2)}, u32[]{:S(2)}) collective-permute-start(f32[160,128]{1,0:T(8,128)S(1)} %get-tuple-element.96), channel_id=1, source_target_pairs={{0,16},{8,24},{16,0},{24,8},{1,17},{9,25},{17,1},{25,9},{2,18},{10... | collective-permute-start | bytes 245768 | tf_op jit(solution)/shard_map/ppermute | solution.py:430
  8.1 1.6 %shard_map.86 = (bf16[4,128,1024]{2,1,0:T(8,128)(2,1)S(1)}, bf16[4,1024,128]{2,1,0:T(8,128)(2,1)S(1)}, bf16[4,1024,128]{2,1,0:T(8,128)(2,1)S(1)}) custom-call(bf16[4,1024,128]{2,1,0:T(8,128)(2,1)S(1)} %get-tuple-element.77.v_ref, bf16[4,1024,128]{2,1,0:T(8,128)(2,1)} %q_hbm.1, bf16[4,1024,128]{2,1,0:T(8,128)(2,1)} %t_hbm.1), custom_call_target="tpu_custom_call" | custom-call | flops 67108864 | tf_op jit(solution)/shard_map/pallas_call | solution.py:415
  9.7 1.8 %shard_map.95 = (f32[1,1024,128]{2,1,0:T(8,128)S(1)}, f32[1,1024,128]{2,1,0:T(8,128)S(1)}, bf16[1,1024,128]{2,1,0:T(8,128)(2,1)S(1)}, bf16[1,128,1024]{2,1,0:T(8...) custom-call(s32[2]{0:T(128)S(4)} %get-tuple-element.76.me_ref, ...), custom_call_target="tpu_custom_call" | custom-call | flops 536870912 | tf_op jit(solution)/shard_map/pallas_call | solution.py:415
  11.5 0.4 collective-permute-done.1.refs_5_
  11.9 1.5 %collective-permute-done.2.refs_6_ = f32[160,128]{1,0:T(8,128)S(1)} collective-permute-done((f32[160,128]{1,0:T(8,128)S(1)}, f32[160,128]{1,0:T(8,128)S(1)}, u32[]{:S(2)}, u32[]{:S(2)}) %collective-permute-start.2) | collective-permute-done | bytes 81952 | tf_op jit(solution)/shard_map/ppermute | solution.py:430
  13.4 1.6 %collective-permute-start.3 = (f32[160,128]{1,0:T(8,128)S(1)}, f32[160,128]{1,0:T(8,128)S(1)}, u32[]{:S(2)}, u32[]{:S(2)}) collective-permute-start(f32[160,128]{1,0:T(8,128)S(1)} %add_add_fusion.1), channel_id=1, source_target_pairs={{0,2},{2,0},{4,6},{6,4},{1,3},{3,1},{5,7},{7,5},{8,10},{10,8},{12,... | collective-permute-start | bytes 245768 | tf_op jit(solution)/shard_map/ppermute | solution.py:430
  15.1 2.6 %collective-permute-start.4 = (f32[160,128]{1,0:T(8,128)S(1)}, f32[160,128]{1,0:T(8,128)S(1)}, u32[]{:S(2)}, u32[]{:S(2)}) collective-permute-start(f32[160,128]{1,0:T(8,128)S(1)} %add_add_fusion.1), channel_id=1, source_target_pairs={{0,4},{2,6},{4,0},{6,2},{1,5},{3,7},{5,1},{7,3},{8,12},{10,14},{12... | collective-permute-start | bytes 245768 | tf_op jit(solution)/shard_map/ppermute | solution.py:430
  17.9 3.6 %shard_map.91 = (f32[2,1024,128]{2,1,0:T(8,128)S(1)}, f32[2,1024,128]{2,1,0:T(8,128)S(1)}, bf16[2,1024,128]{2,1,0:T(8,128)(2,1)S(1)}, bf16[2,128,1024]{2,1,0:T(8...) custom-call(s32[2]{0:T(128)S(4)} %get-tuple-element.76.me_ref, ...), custom_call_target="tpu_custom_call" | custom-call | flops 1073741824 | tf_op jit(solution)/shard_map/pallas_call | solution.py:415
  21.5 0.7 collective-permute-done.4.refs_1_
  22.2 1.8 %collective-permute-done.5.refs_2_ = f32[160,128]{1,0:T(8,128)S(1)} collective-permute-done((f32[160,128]{1,0:T(8,128)S(1)}, f32[160,128]{1,0:T(8,128)S(1)}, u32[]{:S(2)}, u32[]{:S(2)}) %collective-permute-start.5) | collective-permute-done | bytes 81952 | tf_op jit(solution)/shard_map/ppermute | solution.py:430
  24.0 1.1 %collective-permute-start.8 = (f32[160,128]{1,0:T(8,128)S(1)}, f32[160,128]{1,0:T(8,128)S(1)}, u32[]{:S(2)}, u32[]{:S(2)}) collective-permute-start(f32[160,128]{1,0:T(8,128)S(1)} %get-tuple-element.120), channel_id=1, source_target_pairs={{0,24},{8,16},{16,8},{24,0},{1,25},{9,17},{17,9},{25,1},{2,26},{10... | collective-permute-start | bytes 245768 | tf_op jit(solution)/shard_map/ppermute | solution.py:430
  25.1 1.8 %shard_map.87 = (f32[1,1024,128]{2,1,0:T(8,128)S(1)}, f32[1,1024,128]{2,1,0:T(8,128)S(1)}, bf16[1,1024,128]{2,1,0:T(8,128)(2,1)S(1)}, bf16[1,128,1024]{2,1,0:T(8...) custom-call(s32[2]{0:T(128)S(4)} %get-tuple-element.76.me_ref, ...), custom_call_target="tpu_custom_call" | custom-call | flops 536870912 | tf_op jit(solution)/shard_map/pallas_call | solution.py:415
  26.9 1.1 %collective-permute-start.7 = (f32[160,128]{1,0:T(8,128)S(1)}, f32[160,128]{1,0:T(8,128)S(1)}, u32[]{:S(2)}, u32[]{:S(2)}) collective-permute-start(f32[160,128]{1,0:T(8,128)S(1)} %get-tuple-element.111), channel_id=1, source_target_pairs={{0,16},{8,24},{16,0},{24,8},{1,17},{9,25},{17,1},{25,9},{2,18},{10... | collective-permute-start | bytes 245768 | tf_op jit(solution)/shard_map/ppermute | solution.py:430
  28.0 1.5 %shard_map.92 = (f32[2,1024,256]{2,1,0:T(8,128)S(1)}, bf16[2,1024,256]{2,1,0:T(8,128)(2,1)S(1)}, bf16[2,1024,256]{2,1,0:T(8,128)(2,1)S(1)}, bf16[2,320,1024]{2,1,0:T(8,128)(2,1)S(1)}) custom-call(s32[2]{0:T(128)S(4)} %get-tuple-element.76.me_ref, bf16[4,1024,128]{2,1,0:T(8,128)(2,1)S(1)} %get-tuple-element.78.q_ref.refs_0_, ...), custom_call_target="tpu_custom_call" | custom-call | flops 268435456 | tf_op jit(solution)/shard_map/pallas_call | solution.py:415
  29.5 0.6 shard_map.96
  30.2 1.5 %collective-permute-start.6 = (f32[160,128]{1,0:T(8,128)S(1)}, f32[160,128]{1,0:T(8,128)S(1)}, u32[]{:S(2)}, u32[]{:S(2)}) collective-permute-start(f32[160,128]{1,0:T(8,128)S(1)} %get-tuple-element.109), channel_id=1, source_target_pairs={{0,8},{8,0},{16,24},{24,16},{1,9},{9,1},{17,25},{25,17},{2,10},{10... | collective-permute-start | bytes 245768 | tf_op jit(solution)/shard_map/ppermute | solution.py:430
  31.6 0.6 shard_map.88
  32.3 0.9 %shard_map.90 = (bf16[1024,128]{1,0:T(8,128)(2,1)S(1)}, f32[1024,128]{1,0:T(8,128)S(1)}, f32[1024,128]{1,0:T(8,128)S(1)}, f32[160,128]{1,0:T(8,128)S(1)}) custom-call(s32[2]{0:T(128)S(4)} %get-tuple-element.76.me_ref, bf16[4,1024,128]{2,1,0:T(8,128)(2,1)S(1)} %get-tuple-element.87.t_ref, f32[1,1024,128]{2,1,0:T(8,128)S(1)} %get-tuple-element.88.rest_0_, ...), custom_call_target="tpu_custom_call" | custom-call | flops 268435456 | tf_op jit(solution)/shard_map/pallas_call | solution.py:415
  33.2 0.8 %shard_map.97 = (bf16[1024,128]{1,0:T(8,128)(2,1)S(1)}, f32[1024,128]{1,0:T(8,128)S(1)}, f32[1024,128]{1,0:T(8,128)S(1)}, f32[160,128]{1,0:T(8,128)S(1)}) custom-call(s32[2]{0:T(128)S(4)} %get-tuple-element.76.me_ref, bf16[4,1024,128]{2,1,0:T(8,128)(2,1)S(1)} %get-tuple-element.87.t_ref, f32[1,1024,128]{2,1,0:T(8,128)S(1)} %get-tuple-element.113.rest_0_, ...), custom_call_target="tpu_custom_call" | custom-call | flops 268435456 | tf_op jit(solution)/shard_map/pallas_call | solution.py:415
  34.0 1.1 %collective-permute-start.11 = (f32[160,128]{1,0:T(8,128)S(1)}, f32[160,128]{1,0:T(8,128)S(1)}, u32[]{:S(2)}, u32[]{:S(2)}) collective-permute-start(f32[160,128]{1,0:T(8,128)S(1)} %get-tuple-element.126), channel_id=1, source_target_pairs={{0,24},{8,16},{16,8},{24,0},{1,25},{9,17},{17,9},{25,1},{2,26},{10... | collective-permute-start | bytes 245768 | tf_op jit(solution)/shard_map/ppermute | solution.py:430
  35.2 0.8 %shard_map.94 = (bf16[1024,128]{1,0:T(8,128)(2,1)S(1)}, f32[1024,128]{1,0:T(8,128)S(1)}, f32[1024,128]{1,0:T(8,128)S(1)}, f32[160,128]{1,0:T(8,128)S(1)}) custom-call(s32[2]{0:T(128)S(4)} %get-tuple-element.76.me_ref, bf16[4,1024,128]{2,1,0:T(8,128)(2,1)S(1)} %get-tuple-element.87.t_ref, f32[2,1024,128]{2,1,0:T(8,128)S(1)} %get-tuple-element.102.rest_0_, ...), custom_call_target="tpu_custom_call" | custom-call | flops 268435456 | tf_op jit(solution)/shard_map/pallas_call | solution.py:415
  36.0 1.1 %collective-permute-start.10 = (f32[160,128]{1,0:T(8,128)S(1)}, f32[160,128]{1,0:T(8,128)S(1)}, u32[]{:S(2)}, u32[]{:S(2)}) collective-permute-start(f32[160,128]{1,0:T(8,128)S(1)} %get-tuple-element.125), channel_id=1, source_target_pairs={{0,16},{8,24},{16,0},{24,8},{1,17},{9,25},{17,1},{25,9},{2,18},{10... | collective-permute-start | bytes 245768 | tf_op jit(solution)/shard_map/ppermute | solution.py:430
  37.1 0.8 %shard_map.93 = (bf16[1024,128]{1,0:T(8,128)(2,1)S(1)}, f32[1024,128]{1,0:T(8,128)S(1)}, f32[1024,128]{1,0:T(8,128)S(1)}, f32[160,128]{1,0:T(8,128)S(1)}) custom-call(s32[2]{0:T(128)S(4)} %get-tuple-element.76.me_ref, bf16[4,1024,128]{2,1,0:T(8,128)(2,1)S(1)} %get-tuple-element.87.t_ref, f32[2,1024,128]{2,1,0:T(8,128)S(1)} %get-tuple-element.102.rest_0_, ...), custom_call_target="tpu_custom_call" | custom-call | flops 268435456 | tf_op jit(solution)/shard_map/pallas_call | solution.py:415
  37.9 1.5 %collective-permute-start.9 = (f32[160,128]{1,0:T(8,128)S(1)}, f32[160,128]{1,0:T(8,128)S(1)}, u32[]{:S(2)}, u32[]{:S(2)}) collective-permute-start(f32[160,128]{1,0:T(8,128)S(1)} %get-tuple-element.124), channel_id=1, source_target_pairs={{0,8},{8,0},{16,24},{24,16},{1,9},{9,1},{17,25},{25,17},{2,10},{10... | collective-permute-start | bytes 245768 | tf_op jit(solution)/shard_map/ppermute | solution.py:430
  39.4 5.1 %shard_map.100 = (f32[2,16,1024]{2,1,0:T(8,128)S(1)}, f32[16,128]{1,0:T(8,128)S(1)}) custom-call(s32[2]{0:T(128)S(4)} %get-tuple-element.76.me_ref, bf16[4,1024,128]{2,1,0:T(8,128)(2,1)S(1)} %get-tuple-element.78.q_ref.refs_0_, bf16[4,128,1024]{2,1,0:T(8,128)(2,1)S(1)} %get-tuple-element.79.refs_1_.vt_ref, ...), custom_call_target="tpu_custom_call" | custom-call | flops 2147483648 | tf_op jit(solution)/shard_map/pallas_call | solution.py:415
  44.7 1.8 %collective-permute-start.13 = (f32[160,128]{1,0:T(8,128)S(1)}, f32[160,128]{1,0:T(8,128)S(1)}, u32[]{:S(2)}, u32[]{:S(2)}) collective-permute-start(f32[160,128]{1,0:T(8,128)S(1)} %add_add_fusion), channel_id=1, source_target_pairs={{0,4},{2,6},{4,0},{6,2},{1,5},{3,7},{5,1},{7,3},{8,12},{10,14},{12... | collective-permute-start | bytes 245768 | tf_op jit(solution)/shard_map/ppermute | solution.py:430
  46.5 2.6 %collective-permute-start.14 = (f32[160,128]{1,0:T(8,128)S(1)}, f32[160,128]{1,0:T(8,128)S(1)}, u32[]{:S(2)}, u32[]{:S(2)}) collective-permute-start(f32[160,128]{1,0:T(8,128)S(1)} %add_add_fusion), channel_id=1, source_target_pairs={{0,6},{2,4},{4,2},{6,0},{1,7},{3,5},{5,3},{7,1},{8,14},{10,12},{12... | collective-permute-start | bytes 245768 | tf_op jit(solution)/shard_map/ppermute | solution.py:430
  49.0 3.4 %shard_map.98 = (f32[1,16,1024]{2,1,0:T(8,128)S(1)}, f32[16,128]{1,0:T(8,128)S(1)}, bf16[4,1024,128]{2,1,0:T(8,128)(2,1)}) custom-call(s32[2]{0:T(128)S(4)} %get-tuple-element.76.me_ref, bf16[4,1024,128]{2,1,0:T(8,128)(2,1)S(1)} %get-tuple-element.78.q_ref.refs_0_, bf16[4,128,1024]{2,1,0:T(8,128)(2,1)S(1)} %get-tuple-element.79.refs_1_.vt_ref, ...), custom_call_target="tpu_custom_call" | custom-call | flops 1073741824 | tf_op jit(solution)/shard_map/pallas_call | solution.py:415
  52.8 1.1 %collective-permute-start.15 = (f32[160,128]{1,0:T(8,128)S(1)}, f32[160,128]{1,0:T(8,128)S(1)}, u32[]{:S(2)}, u32[]{:S(2)}) collective-permute-start(f32[160,128]{1,0:T(8,128)S(1)} %get-tuple-element.128), channel_id=1, source_target_pairs={{0,8},{8,0},{16,24},{24,16},{1,9},{9,1},{17,25},{25,17},{2,10},{10... | collective-permute-start | bytes 245768 | tf_op jit(solution)/shard_map/ppermute | solution.py:430
  53.9 1.3 %collective-permute-start.16 = (f32[160,128]{1,0:T(8,128)S(1)}, f32[160,128]{1,0:T(8,128)S(1)}, u32[]{:S(2)}, u32[]{:S(2)}) collective-permute-start(f32[160,128]{1,0:T(8,128)S(1)} %get-tuple-element.129), channel_id=1, source_target_pairs={{0,16},{8,24},{16,0},{24,8},{1,17},{9,25},{17,1},{25,9},{2,18},{10... | collective-permute-start | bytes 245768 | tf_op jit(solution)/shard_map/ppermute | solution.py:430
  55.2 1.1 %collective-permute-start.17 = (f32[160,128]{1,0:T(8,128)S(1)}, f32[160,128]{1,0:T(8,128)S(1)}, u32[]{:S(2)}, u32[]{:S(2)}) collective-permute-start(f32[160,128]{1,0:T(8,128)S(1)} %get-tuple-element.130), channel_id=1, source_target_pairs={{0,24},{8,16},{16,8},{24,0},{1,25},{9,17},{17,9},{25,1},{2,26},{10... | collective-permute-start | bytes 245768 | tf_op jit(solution)/shard_map/ppermute | solution.py:430
  56.4 2.9 %shard_map.101 = (f32[1,16,1024]{2,1,0:T(8,128)S(1)}, f32[16,128]{1,0:T(8,128)S(1)}) custom-call(s32[2]{0:T(128)S(4)} %get-tuple-element.76.me_ref, bf16[4,1024,128]{2,1,0:T(8,128)(2,1)S(1)} %get-tuple-element.78.q_ref.refs_0_, bf16[4,128,1024]{2,1,0:T(8,128)(2,1)S(1)} %get-tuple-element.79.refs_1_.vt_ref, ...), custom_call_target="tpu_custom_call" | custom-call | flops 1073741824 | tf_op jit(solution)/shard_map/pallas_call | solution.py:415
  59.3 1.3 %collective-permute-done.17.rest_3_ = f32[160,128]{1,0:T(8,128)S(1)} collective-permute-done((f32[160,128]{1,0:T(8,128)S(1)}, f32[160,128]{1,0:T(8,128)S(1)}, u32[]{:S(2)}, u32[]{:S(2)}) %collective-permute-start.17) | collective-permute-done | bytes 81952 | tf_op jit(solution)/shard_map/ppermute | solution.py:430
  60.6 1.4 %shard_map.102 = f32[32,128]{1,0:T(8,128)S(1)} custom-call(s32[2]{0:T(128)S(4)} %get-tuple-element.76.me_ref, bf16[4,1024,128]{2,1,0:T(8,128)(2,1)S(1)} %get-tuple-element.80.k_ref, bf16[4,128,1024]{2,1,0:T(8,128)(2,1)S(1)} %get-tuple-element.79.refs_1_.vt_ref, f32[16,128]{1,0:T(8,128)S(1)} %get-tuple-element.82.wk_ref, ...), custom_call_target="tpu_custom_call" | custom-call | flops 335544320 | tf_op jit(solution)/shard_map/pallas_call | solution.py:415
  62.0 1.2 %collective-permute-done.18 = f32[32,128]{1,0:T(8,128)S(1)} collective-permute-done((f32[32,128]{1,0:T(8,128)S(1)}, f32[32,128]{1,0:T(8,128)S(1)}, u32[]{:S(2)}, u32[]{:S(2)}) %collective-permute-start.18) | collective-permute-done | bytes 16416 | tf_op jit(solution)/shard_map/ppermute | solution.py:430
  63.2 0.6 collective-permute-start.19
  63.8 1.1 %collective-permute-start.20 = (f32[32,128]{1,0:T(8,128)S(1)}, f32[32,128]{1,0:T(8,128)S(1)}, u32[]{:S(2)}, u32[]{:S(2)}) collective-permute-start(f32[32,128]{1,0:T(8,128)S(1)} %add.45), channel_id=1, source_target_pairs={{0,16},{8,24},{16,0},{24,8},{1,17},{9,25},{17,1},{25,9},{2,18},{10... | collective-permute-start | bytes 49160 | tf_op jit(solution)/shard_map/ppermute | solution.py:430
  64.9 1.8 %collective-permute-start.21 = (f32[32,128]{1,0:T(8,128)S(1)}, f32[32,128]{1,0:T(8,128)S(1)}, u32[]{:S(2)}, u32[]{:S(2)}) collective-permute-start(f32[32,128]{1,0:T(8,128)S(1)} %add.45), channel_id=1, source_target_pairs={{0,24},{8,16},{16,8},{24,0},{1,25},{9,17},{17,9},{25,1},{2,26},{10... | collective-permute-start | bytes 49160 | tf_op jit(solution)/shard_map/ppermute | solution.py:430
  66.9 0.6 collective-permute-done.20
  67.5 2.0 %collective-permute-done.21 = f32[32,128]{1,0:T(8,128)S(1)} collective-permute-done((f32[32,128]{1,0:T(8,128)S(1)}, f32[32,128]{1,0:T(8,128)S(1)}, u32[]{:S(2)}, u32[]{:S(2)}) %collective-permute-start.21) | collective-permute-done | bytes 16416 | tf_op jit(solution)/shard_map/ppermute | solution.py:430
  69.5 1.1 %collective-permute-start.22 = (f32[32,128]{1,0:T(8,128)S(1)}, f32[32,128]{1,0:T(8,128)S(1)}, u32[]{:S(2)}, u32[]{:S(2)}) collective-permute-start(f32[32,128]{1,0:T(8,128)S(1)} %add_add_fusion.3), channel_id=1, source_target_pairs={{0,2},{2,0},{4,6},{6,4},{1,3},{3,1},{5,7},{7,5},{8,10},{10,8},{12,... | collective-permute-start | bytes 49160 | tf_op jit(solution)/shard_map/ppermute | solution.py:430
  70.6 2.1 %collective-permute-start.23 = (f32[32,128]{1,0:T(8,128)S(1)}, f32[32,128]{1,0:T(8,128)S(1)}, u32[]{:S(2)}, u32[]{:S(2)}) collective-permute-start(f32[32,128]{1,0:T(8,128)S(1)} %add_add_fusion.3), channel_id=1, source_target_pairs={{0,4},{2,6},{4,0},{6,2},{1,5},{3,7},{5,1},{7,3},{8,12},{10,14},{12... | collective-permute-start | bytes 49160 | tf_op jit(solution)/shard_map/ppermute | solution.py:430
  72.7 1.2 %collective-permute-start.24 = (f32[32,128]{1,0:T(8,128)S(1)}, f32[32,128]{1,0:T(8,128)S(1)}, u32[]{:S(2)}, u32[]{:S(2)}) collective-permute-start(f32[32,128]{1,0:T(8,128)S(1)} %add_add_fusion.3), channel_id=1, source_target_pairs={{0,6},{2,4},{4,2},{6,0},{1,7},{3,5},{5,3},{7,1},{8,14},{10,12},{12... | collective-permute-start | bytes 49160 | tf_op jit(solution)/shard_map/ppermute | solution.py:430
  73.9 1.4 %collective-permute-done.23 = f32[32,128]{1,0:T(8,128)S(1)} collective-permute-done((f32[32,128]{1,0:T(8,128)S(1)}, f32[32,128]{1,0:T(8,128)S(1)}, u32[]{:S(2)}, u32[]{:S(2)}) %collective-permute-start.23) | collective-permute-done | bytes 16416 | tf_op jit(solution)/shard_map/ppermute | solution.py:430
  75.3 2.9 %collective-permute-done.24 = f32[32,128]{1,0:T(8,128)S(1)} collective-permute-done((f32[32,128]{1,0:T(8,128)S(1)}, f32[32,128]{1,0:T(8,128)S(1)}, u32[]{:S(2)}, u32[]{:S(2)}) %collective-permute-start.24) | collective-permute-done | bytes 16416 | tf_op jit(solution)/shard_map/ppermute | solution.py:430
  78.2 0.6 slice_bitcast_fusion
  (27 shorter events, 1.2 us)
Async XLA Ops:
  3.5 7.9 %collective-permute-start = (f32[160,128]{1,0:T(8,128)S(1)}, f32[160,128]{1,0:T(8,128)S(1)}, u32[]{:S(2)}, u32[]{:S(2)}) collective-permute-start(f32[160,128]{1,0:T(8,128)S(1)} %get-tuple-element.95), channel_id=1, source_target_pairs={{0,8},{8,0},{16,24},{24,16},{1,9},{9,1},{17,25},{25,17},{2,10},{10... | collective-permute-start | bytes 245768 | tf_op jit(solution)/shard_map/ppermute | solution.py:430
  6.6 5.3 %collective-permute-start.1 = (f32[160,128]{1,0:T(8,128)S(1)}, f32[160,128]{1,0:T(8,128)S(1)}, u32[]{:S(2)}, u32[]{:S(2)}) collective-permute-start(f32[160,128]{1,0:T(8,128)S(1)} %get-tuple-element.96), channel_id=1, source_target_pairs={{0,16},{8,24},{16,0},{24,8},{1,17},{9,25},{17,1},{25,9},{2,18},{10... | collective-permute-start | bytes 245768 | tf_op jit(solution)/shard_map/ppermute | solution.py:430
  8.1 5.3 %collective-permute-start.2 = (f32[160,128]{1,0:T(8,128)S(1)}, f32[160,128]{1,0:T(8,128)S(1)}, u32[]{:S(2)}, u32[]{:S(2)}) collective-permute-start(f32[160,128]{1,0:T(8,128)S(1)} %get-tuple-element.97), channel_id=1, source_target_pairs={{0,24},{8,16},{16,8},{24,0},{1,25},{9,17},{17,9},{25,1},{2,26},{10... | collective-permute-start | bytes 245768 | tf_op jit(solution)/shard_map/ppermute | solution.py:430
  13.4 8.1 %collective-permute-start.3 = (f32[160,128]{1,0:T(8,128)S(1)}, f32[160,128]{1,0:T(8,128)S(1)}, u32[]{:S(2)}, u32[]{:S(2)}) collective-permute-start(f32[160,128]{1,0:T(8,128)S(1)} %add_add_fusion.1), channel_id=1, source_target_pairs={{0,2},{2,0},{4,6},{6,4},{1,3},{3,1},{5,7},{7,5},{8,10},{10,8},{12,... | collective-permute-start | bytes 245768 | tf_op jit(solution)/shard_map/ppermute | solution.py:430
  15.1 7.1 %collective-permute-start.4 = (f32[160,128]{1,0:T(8,128)S(1)}, f32[160,128]{1,0:T(8,128)S(1)}, u32[]{:S(2)}, u32[]{:S(2)}) collective-permute-start(f32[160,128]{1,0:T(8,128)S(1)} %add_add_fusion.1), channel_id=1, source_target_pairs={{0,4},{2,6},{4,0},{6,2},{1,5},{3,7},{5,1},{7,3},{8,12},{10,14},{12... | collective-permute-start | bytes 245768 | tf_op jit(solution)/shard_map/ppermute | solution.py:430
  17.7 6.3 %collective-permute-start.5 = (f32[160,128]{1,0:T(8,128)S(1)}, f32[160,128]{1,0:T(8,128)S(1)}, u32[]{:S(2)}, u32[]{:S(2)}) collective-permute-start(f32[160,128]{1,0:T(8,128)S(1)} %add_add_fusion.1), channel_id=1, source_target_pairs={{0,6},{2,4},{4,2},{6,0},{1,7},{3,5},{5,3},{7,1},{8,14},{10,12},{12... | collective-permute-start | bytes 245768 | tf_op jit(solution)/shard_map/ppermute | solution.py:430
  24.0 9.2 %collective-permute-start.8 = (f32[160,128]{1,0:T(8,128)S(1)}, f32[160,128]{1,0:T(8,128)S(1)}, u32[]{:S(2)}, u32[]{:S(2)}) collective-permute-start(f32[160,128]{1,0:T(8,128)S(1)} %get-tuple-element.120), channel_id=1, source_target_pairs={{0,24},{8,16},{16,8},{24,0},{1,25},{9,17},{17,9},{25,1},{2,26},{10... | collective-permute-start | bytes 245768 | tf_op jit(solution)/shard_map/ppermute | solution.py:430
  26.9 8.2 %collective-permute-start.7 = (f32[160,128]{1,0:T(8,128)S(1)}, f32[160,128]{1,0:T(8,128)S(1)}, u32[]{:S(2)}, u32[]{:S(2)}) collective-permute-start(f32[160,128]{1,0:T(8,128)S(1)} %get-tuple-element.111), channel_id=1, source_target_pairs={{0,16},{8,24},{16,0},{24,8},{1,17},{9,25},{17,1},{25,9},{2,18},{10... | collective-permute-start | bytes 245768 | tf_op jit(solution)/shard_map/ppermute | solution.py:430
  30.2 6.9 %collective-permute-start.6 = (f32[160,128]{1,0:T(8,128)S(1)}, f32[160,128]{1,0:T(8,128)S(1)}, u32[]{:S(2)}, u32[]{:S(2)}) collective-permute-start(f32[160,128]{1,0:T(8,128)S(1)} %get-tuple-element.109), channel_id=1, source_target_pairs={{0,8},{8,0},{16,24},{24,16},{1,9},{9,1},{17,25},{25,17},{2,10},{10... | collective-permute-start | bytes 245768 | tf_op jit(solution)/shard_map/ppermute | solution.py:430
  34.0 10.5 %collective-permute-start.11 = (f32[160,128]{1,0:T(8,128)S(1)}, f32[160,128]{1,0:T(8,128)S(1)}, u32[]{:S(2)}, u32[]{:S(2)}) collective-permute-start(f32[160,128]{1,0:T(8,128)S(1)} %get-tuple-element.126), channel_id=1, source_target_pairs={{0,24},{8,16},{16,8},{24,0},{1,25},{9,17},{17,9},{25,1},{2,26},{10... | collective-permute-start | bytes 245768 | tf_op jit(solution)/shard_map/ppermute | solution.py:430
  36.0 8.5 %collective-permute-start.10 = (f32[160,128]{1,0:T(8,128)S(1)}, f32[160,128]{1,0:T(8,128)S(1)}, u32[]{:S(2)}, u32[]{:S(2)}) collective-permute-start(f32[160,128]{1,0:T(8,128)S(1)} %get-tuple-element.125), channel_id=1, source_target_pairs={{0,16},{8,24},{16,0},{24,8},{1,17},{9,25},{17,1},{25,9},{2,18},{10... | collective-permute-start | bytes 245768 | tf_op jit(solution)/shard_map/ppermute | solution.py:430
  37.9 6.6 %collective-permute-start.9 = (f32[160,128]{1,0:T(8,128)S(1)}, f32[160,128]{1,0:T(8,128)S(1)}, u32[]{:S(2)}, u32[]{:S(2)}) collective-permute-start(f32[160,128]{1,0:T(8,128)S(1)} %get-tuple-element.124), channel_id=1, source_target_pairs={{0,8},{8,0},{16,24},{24,16},{1,9},{9,1},{17,25},{25,17},{2,10},{10... | collective-permute-start | bytes 245768 | tf_op jit(solution)/shard_map/ppermute | solution.py:430
  44.6 7.9 %collective-permute-start.12 = (f32[160,128]{1,0:T(8,128)S(1)}, f32[160,128]{1,0:T(8,128)S(1)}, u32[]{:S(2)}, u32[]{:S(2)}) collective-permute-start(f32[160,128]{1,0:T(8,128)S(1)} %add_add_fusion), channel_id=1, source_target_pairs={{0,2},{2,0},{4,6},{6,4},{1,3},{3,1},{5,7},{7,5},{8,10},{10,8},{12,... | collective-permute-start | bytes 245768 | tf_op jit(solution)/shard_map/ppermute | solution.py:430
  44.7 7.8 %collective-permute-start.13 = (f32[160,128]{1,0:T(8,128)S(1)}, f32[160,128]{1,0:T(8,128)S(1)}, u32[]{:S(2)}, u32[]{:S(2)}) collective-permute-start(f32[160,128]{1,0:T(8,128)S(1)} %add_add_fusion), channel_id=1, source_target_pairs={{0,4},{2,6},{4,0},{6,2},{1,5},{3,7},{5,1},{7,3},{8,12},{10,14},{12... | collective-permute-start | bytes 245768 | tf_op jit(solution)/shard_map/ppermute | solution.py:430
  46.5 6.2 %collective-permute-start.14 = (f32[160,128]{1,0:T(8,128)S(1)}, f32[160,128]{1,0:T(8,128)S(1)}, u32[]{:S(2)}, u32[]{:S(2)}) collective-permute-start(f32[160,128]{1,0:T(8,128)S(1)} %add_add_fusion), channel_id=1, source_target_pairs={{0,6},{2,4},{4,2},{6,0},{1,7},{3,5},{5,3},{7,1},{8,14},{10,12},{12... | collective-permute-start | bytes 245768 | tf_op jit(solution)/shard_map/ppermute | solution.py:430
  52.8 6.5 %collective-permute-start.15 = (f32[160,128]{1,0:T(8,128)S(1)}, f32[160,128]{1,0:T(8,128)S(1)}, u32[]{:S(2)}, u32[]{:S(2)}) collective-permute-start(f32[160,128]{1,0:T(8,128)S(1)} %get-tuple-element.128), channel_id=1, source_target_pairs={{0,8},{8,0},{16,24},{24,16},{1,9},{9,1},{17,25},{25,17},{2,10},{10... | collective-permute-start | bytes 245768 | tf_op jit(solution)/shard_map/ppermute | solution.py:430
  53.9 5.3 %collective-permute-start.16 = (f32[160,128]{1,0:T(8,128)S(1)}, f32[160,128]{1,0:T(8,128)S(1)}, u32[]{:S(2)}, u32[]{:S(2)}) collective-permute-start(f32[160,128]{1,0:T(8,128)S(1)} %get-tuple-element.129), channel_id=1, source_target_pairs={{0,16},{8,24},{16,0},{24,8},{1,17},{9,25},{17,1},{25,9},{2,18},{10... | collective-permute-start | bytes 245768 | tf_op jit(solution)/shard_map/ppermute | solution.py:430
  55.2 5.3 %collective-permute-start.17 = (f32[160,128]{1,0:T(8,128)S(1)}, f32[160,128]{1,0:T(8,128)S(1)}, u32[]{:S(2)}, u32[]{:S(2)}) collective-permute-start(f32[160,128]{1,0:T(8,128)S(1)} %get-tuple-element.130), channel_id=1, source_target_pairs={{0,24},{8,16},{16,8},{24,0},{1,25},{9,17},{17,9},{25,1},{2,26},{10... | collective-permute-start | bytes 245768 | tf_op jit(solution)/shard_map/ppermute | solution.py:430
  62.0 1.2 %collective-permute-start.18 = (f32[32,128]{1,0:T(8,128)S(1)}, f32[32,128]{1,0:T(8,128)S(1)}, u32[]{:S(2)}, u32[]{:S(2)}) collective-permute-start(f32[32,128]{1,0:T(8,128)S(1)} %shard_map.102), channel_id=1, source_target_pairs={{0,1},{1,0},{2,3},{3,2},{4,5},{5,4},{6,7},{7,6},{8,9},{9,8},{10,11... | collective-permute-start | bytes 49160 | tf_op jit(solution)/shard_map/ppermute | solution.py:430
  63.2 3.7 %collective-permute-start.19 = (f32[32,128]{1,0:T(8,128)S(1)}, f32[32,128]{1,0:T(8,128)S(1)}, u32[]{:S(2)}, u32[]{:S(2)}) collective-permute-start(f32[32,128]{1,0:T(8,128)S(1)} %add.45), channel_id=1, source_target_pairs={{0,8},{8,0},{16,24},{24,16},{1,9},{9,1},{17,25},{25,17},{2,10},{10... | collective-permute-start | bytes 49160 | tf_op jit(solution)/shard_map/ppermute | solution.py:430
  63.8 3.7 %collective-permute-start.20 = (f32[32,128]{1,0:T(8,128)S(1)}, f32[32,128]{1,0:T(8,128)S(1)}, u32[]{:S(2)}, u32[]{:S(2)}) collective-permute-start(f32[32,128]{1,0:T(8,128)S(1)} %add.45), channel_id=1, source_target_pairs={{0,16},{8,24},{16,0},{24,8},{1,17},{9,25},{17,1},{25,9},{2,18},{10... | collective-permute-start | bytes 49160 | tf_op jit(solution)/shard_map/ppermute | solution.py:430
  64.9 4.6 %collective-permute-start.21 = (f32[32,128]{1,0:T(8,128)S(1)}, f32[32,128]{1,0:T(8,128)S(1)}, u32[]{:S(2)}, u32[]{:S(2)}) collective-permute-start(f32[32,128]{1,0:T(8,128)S(1)} %add.45), channel_id=1, source_target_pairs={{0,24},{8,16},{16,8},{24,0},{1,25},{9,17},{17,9},{25,1},{2,26},{10... | collective-permute-start | bytes 49160 | tf_op jit(solution)/shard_map/ppermute | solution.py:430
  69.5 4.4 %collective-permute-start.22 = (f32[32,128]{1,0:T(8,128)S(1)}, f32[32,128]{1,0:T(8,128)S(1)}, u32[]{:S(2)}, u32[]{:S(2)}) collective-permute-start(f32[32,128]{1,0:T(8,128)S(1)} %add_add_fusion.3), channel_id=1, source_target_pairs={{0,2},{2,0},{4,6},{6,4},{1,3},{3,1},{5,7},{7,5},{8,10},{10,8},{12,... | collective-permute-start | bytes 49160 | tf_op jit(solution)/shard_map/ppermute | solution.py:430
  70.6 4.7 %collective-permute-start.23 = (f32[32,128]{1,0:T(8,128)S(1)}, f32[32,128]{1,0:T(8,128)S(1)}, u32[]{:S(2)}, u32[]{:S(2)}) collective-permute-start(f32[32,128]{1,0:T(8,128)S(1)} %add_add_fusion.3), channel_id=1, source_target_pairs={{0,4},{2,6},{4,0},{6,2},{1,5},{3,7},{5,1},{7,3},{8,12},{10,14},{12... | collective-permute-start | bytes 49160 | tf_op jit(solution)/shard_map/ppermute | solution.py:430
  72.7 5.5 %collective-permute-start.24 = (f32[32,128]{1,0:T(8,128)S(1)}, f32[32,128]{1,0:T(8,128)S(1)}, u32[]{:S(2)}, u32[]{:S(2)}) collective-permute-start(f32[32,128]{1,0:T(8,128)S(1)} %add_add_fusion.3), channel_id=1, source_target_pairs={{0,6},{2,4},{4,2},{6,0},{1,7},{3,5},{5,3},{7,1},{8,14},{10,12},{12... | collective-permute-start | bytes 49160 | tf_op jit(solution)/shard_map/ppermute | solution.py:430

commit v5 on v4

--- a/solution.py
+++ b/solution.py
@@ -168,12 +168,21 @@
     wk_ref, k_ref, v_ref = kept[:3]
     heads = k_ref.shape[0]
     per = n // heads
-    copies = [pltpu.make_async_copy(a, b, sems.at[i]) for i, (a, b) in enumerate(zip(sources, kept))]
-    for copy in copies:
-        copy.start()
-    copies[0].wait()
+    whole = [pltpu.make_async_copy(a, b, sems.at[i]) for i, (a, b) in enumerate(zip(sources, kept)) if i in (0, 3)]
+
+    def one(i, p):
+        at = head_at(me_ref, per, p)
+        return pltpu.make_async_copy(sources[i].at[at], kept[i].at[at], sems.at[4 + 2 * p + i - 1])
+
+    whole[0].start()
+    for i in (1, 2):
+        for p in range(heads):
+            one(i, p).start()
+    whole[1].start()
+    whole[0].wait()
     w_ext = rolled(wk_ref[...].astype(bf16), dm)
-    copies[1].wait()
+    for p in range(heads):
+        one(1, p).wait()
     phis, parts = [], []
     for p in range(heads):
         phi = features_t(dot(w_ext, k_ref[head_at(me_ref, per, p)], NT), dm)
@@ -182,8 +191,9 @@
             part = part + phi[:, c : c + LANES]
         phis.append(phi.astype(bf16))
         parts.append(part)
-    for copy in copies[2:]:
-        copy.wait()
+    for p in range(heads):
+        one(2, p).wait()
+    whole[1].wait()
     for p in range(heads):
         state = with_count(dot(phis[p], v_ref[head_at(me_ref, per, p)]), column_row(parts[p], dm), dm)
         put_slots(me_ref, slots[p * per : (p + 1) * per], scr, state)
@@ -378,22 +388,21 @@
         copy.wait()
 
 
-def key_kernel(dm, n, parts, me_ref, k_ref, vt_ref, wk_ref, *rest):
-    slots, backs, (out_ref, scr) = rest[:n], rest[n:-2], rest[-2:]
-    per = n // k_ref.shape[0]
+def key_kernel(dm, per, places, first, me_ref, k_ref, vt_ref, wk_ref, *rest):
+    count = len(places)
+    slots, backs = rest[: per * count], rest[per * count : (per + 1) * count]
+    before, (out_ref, scr) = rest[(per + 1) * count : -2], rest[-2:]
     w = dm.width
-    out_ref[:w] = functools.reduce(jnp.add, [g[...] for g in backs[1::2]])
     w_ext = rolled(wk_ref[...].astype(bf16), dm)
-    grad = jnp.zeros((w, out_ref.shape[1]), f32)
-    for (p0, count), gk_ref in zip(parts, backs[::2]):
-        for i in range(count):
-            p = p0 + i
-            state = get_slots(me_ref, slots[p * per : (p + 1) * per], scr)
-            at = head_at(me_ref, per, p)
-            k = k_ref[at]
-            g_phi = dot(state.astype(bf16), vt_ref[at]) + count_column(state, dm)
-            total = gk_ref[i] + feature_grad_t(dot(w_ext, k, NT), g_phi, dm)
-            grad = grad + dot(total.astype(bf16), k)
+    grad = jnp.zeros((w, out_ref.shape[1]), f32) if first else before[0][w:]
+    for at, ((p, i), gk_ref) in enumerate(zip(places, backs)):
+        state = get_slots(me_ref, slots[at * per : (at + 1) * per], scr)
+        h = head_at(me_ref, per, p)
+        k = k_ref[h]
+        g_phi = dot(state.astype(bf16), vt_ref[h]) + count_column(state, dm)
+        total = gk_ref[i] + feature_grad_t(dot(w_ext, k, NT), g_phi, dm)
+        grad = grad + dot(total.astype(bf16), k)
+    out_ref[:w] = functools.reduce(jnp.add, [g[...] for g in before]) if first else before[0][:w]
     out_ref[w:] = grad
 
 
@@ -430,17 +439,26 @@
     return lax.ppermute(array, axis, pairs)
 
 
-def exchange(parts, axis):
+def crossed(array, axis, d):
+    n, h = lax.axis_size(axis), lax.axis_size("head")
+    return shifted(array, (axis, "head"), [(i * h + c, (i ^ d) * h + h - 1 - c) for i in range(n) for c in range(h)])
+
+
+def exchange(parts, axis, cross=False):
     n = lax.axis_size(axis)
     got = []
     for d, part in enumerate(parts):
-        got.append(part if d == 0 else shifted(part, axis, [(i, i ^ d) for i in range(n)]))
+        if cross:
+            got.append(crossed(part, axis, d))
+        else:
+            got.append(part if d == 0 else shifted(part, axis, [(i, i ^ d) for i in range(n)]))
     return got
 
 
-def carried(me, parts, backward):
+def carried(me, parts, backward, label):
     n, m = lax.axis_size("seq"), lax.axis_size("seg")
-    got = exchange(parts, "seq")
+    cross = label in CROSSED and lax.axis_size("head") > 1
+    got = exchange(parts, "seq", cross)
     total = functools.reduce(jnp.add, got)
     far = exchange([total] * m, "seg")[1:]
     shape = pltpu.VMEM(parts[0].shape, f32)
@@ -454,16 +472,21 @@
         [],
         parts[0].size * n * n,
     )
-    return exchange(before, "seq")
+    return exchange(before, "seq", cross)
 
 
 def summed(array):
-    for axis in ("head", "seq", "seg"):
-        array = functools.reduce(jnp.add, exchange([array] * lax.axis_size(axis), axis))
+    array = functools.reduce(jnp.add, exchange([array] * lax.axis_size("head"), "head"))
+    for axis in ("seq", "seg"):
+        got = array
+        for d in range(1, lax.axis_size(axis)):
+            got = got + crossed(array, axis, d)
+        array = got
     return array
 
 
 SPLIT = (1, 2, 1)
+CROSSED = ("f",)
 
 
 def split_heads(heads, split):
@@ -500,7 +523,7 @@
         [SMEM] + [HBM] * len(sources),
         [slot_shape] * n + [pltpu.VMEM(a.shape, a.dtype) for a in sources] + [pltpu.SMEM((2,), jnp.int32)],
         [VMEM] * (n + len(sources)) + [SMEM],
-        scr + [pltpu.SemaphoreType.DMA((len(sources),))],
+        scr + [pltpu.SemaphoreType.DMA((4 + 2 * heads,))],
         4 * heads * tokens * dm.rows * hd,
     )
     states, (wk, keys, values, wq, me) = called[:n], called[n:]
@@ -550,7 +573,7 @@
         )
         intra.append(outs[:2] + outs[6:])
         packed.append(outs[2:6])
-    prev = carried(me, states, False)
+    prev = carried(me, states, False, "f")
     heads_out = {}
     for p, i, part in reversed([(p0 + i, i, part) for part, (p0, count) in enumerate(parts) for i in range(count)]):
         heads_out[p] = call(
@@ -568,7 +591,7 @@
             scr,
             8 * tokens * dm.lanes * hd,
         )
-    later = carried(me, [b for p in range(heads) for b in heads_out[p][3:]], True)
+    later = carried(me, [b for p in range(heads) for b in heads_out[p][3:]], True, "b")
     backs = []
     for part, (p0, count) in enumerate(parts):
         body = functools.partial(backward_kernel, dm, tile, per, p0, count)
@@ -589,16 +612,24 @@
         if part == 0:
             student = outs[2]
         backs += outs[:2]
-    grads = call(
-        functools.partial(key_kernel, dm, n, parts),
-        (),
-        (me, keys, vt, wk, *later, *backs),
-        [SMEM] + [VMEM] * (3 + n + len(backs)),
-        [pltpu.VMEM((2 * dm.width, hd), f32)],
-        [VMEM],
-        scr,
-        4 * heads * tokens * dm.rows * hd,
-    )[0]
+    spots = [(p0 + i, i, part) for part, (p0, count) in enumerate(parts) for i in range(count)]
+    grads = backs[1::2]
+    for step, group in enumerate((spots[:1], spots[1:])):
+        args = (me, keys, vt, wk)
+        for p, _, _ in group:
+            args += tuple(later[p * per : (p + 1) * per])
+        args += tuple(backs[2 * part] for _, _, part in group) + tuple(grads)
+        grads = call(
+            functools.partial(key_kernel, dm, per, [(p, i) for p, i, _ in group], step == 0),
+            (),
+            args,
+            [SMEM] + [VMEM] * (len(args) - 1),
+            [pltpu.VMEM((2 * dm.width, hd), f32)],
+            [VMEM],
+            scr,
+            4 * len(group) * tokens * dm.rows * hd,
+        )
+    (grads,) = grads
     grads = summed(grads)
     return student, grads[: dm.width].T, grads[dm.width :].T
 

time: 79 us -> 79.1 us (level)
  starting transfers between devices: 32.3 us -> 30.9 us
  waiting for transfers between devices: 14.3 us -> 15.4 us
    ppermute x25 -> x27, starting transfers between devices: 32.3 us -> 30.9 us  [shifted(): return lax.ppermute(array, axis, pairs)]
    ppermute x25 -> x27, waiting for transfers between devices: 14.3 us -> 15.4 us  [shifted(): return lax.ppermute(array, axis, pairs)]
    pallas_call x18 -> x19, Pallas kernels: 30.7 us -> 31 us  [call(): pl.pallas_call(body, grid=grid, in_specs=specs, out_specs=out_specs, out_...]
  transfers between devices with their start and end apart: 25 -> 27, of which waited for: 12 -> 10; matrix products, arithmetic and copies ran while one was open for 0% -> 0% of each run, Pallas kernels for 33% -> 34%
where the time goes in v5:
time: 79.1 us; the launch traced here: 78.9 us
  Pallas kernels  31 us (39%)
  starting transfers between devices  30.9 us (39%)
  waiting for transfers between devices  15.4 us (19%)
  between operations  0.87 us (1%)
    pallas_call x19, Pallas kernels, call(): pl.pallas_call(body, grid=grid, in_specs=specs, out_specs=out_specs, out_...  31 us
    ppermute x27, starting transfers between devices, shifted(): return lax.ppermute(array, axis, pairs)  30.9 us
    ppermute x27, waiting for transfers between devices, shifted(): return lax.ppermute(array, axis, pairs)  15.4 us
  transfers between devices with their start and end apart: 27, of which 10 were waited for; matrix products, arithmetic and copies ran while one was open for 0% of the time, Pallas kernels for 34%

profile of v5, /device:TPU:0, one launch (start us, length us, event | category | flops | bytes accessed | tf_op | source)
XLA Modules:
  0.0 78.9 jit_solution(6920694286180378619)
XLA Ops:
  0.7 2.8 %shard_map.85 = (f32[160,128]{1,0:T(8,128)S(1)}, f32[160,128]{1,0:T(8,128)S(1)}, f32[160,128]{1,0:T(8,128)S(1)}, f32[160,128]{1,0:T(8,128)S(1)}, f32[16,128]{1,0...) custom-call(s32[2]{0:T(128)S(1)} %pad_add_fusion.me_ref, ...), custom_call_target="tpu_custom_call" | custom-call | flops 335544320 | tf_op jit(solution)/shard_map/pallas_call | solution.py:424
  4.1 2.6 %collective-permute-start.1 = (f32[160,128]{1,0:T(8,128)S(1)}, f32[160,128]{1,0:T(8,128)S(1)}, u32[]{:S(2)}, u32[]{:S(2)}) collective-permute-start(f32[160,128]{1,0:T(8,128)S(1)} %get-tuple-element.95), channel_id=1, source_target_pairs={{0,9},{1,8},{8,1},{9,0},{16,25},{17,24},{24,17},{25,16},{2,11},{3,... | collective-permute-start | bytes 245768 | tf_op jit(solution)/shard_map/ppermute | solution.py:439
  6.7 1.2 %collective-permute-start.2 = (f32[160,128]{1,0:T(8,128)S(1)}, f32[160,128]{1,0:T(8,128)S(1)}, u32[]{:S(2)}, u32[]{:S(2)}) collective-permute-start(f32[160,128]{1,0:T(8,128)S(1)} %get-tuple-element.96), channel_id=1, source_target_pairs={{0,17},{1,16},{8,25},{9,24},{16,1},{17,0},{24,9},{25,8},{2,19},{3,... | collective-permute-start | bytes 245768 | tf_op jit(solution)/shard_map/ppermute | solution.py:439
  7.9 1.6 %shard_map.86 = (bf16[4,128,1024]{2,1,0:T(8,128)(2,1)S(1)}, bf16[4,1024,128]{2,1,0:T(8,128)(2,1)S(1)}, bf16[4,1024,128]{2,1,0:T(8,128)(2,1)S(1)}) custom-call(bf16[4,1024,128]{2,1,0:T(8,128)(2,1)S(1)} %get-tuple-element.77.v_ref, bf16[4,1024,128]{2,1,0:T(8,128)(2,1)} %q_hbm.1, bf16[4,1024,128]{2,1,0:T(8,128)(2,1)} %t_hbm.1), custom_call_target="tpu_custom_call" | custom-call | flops 67108864 | tf_op jit(solution)/shard_map/pallas_call | solution.py:424
  9.5 1.8 %shard_map.95 = (f32[1,1024,128]{2,1,0:T(8,128)S(1)}, f32[1,1024,128]{2,1,0:T(8,128)S(1)}, bf16[1,1024,128]{2,1,0:T(8,128)(2,1)S(1)}, bf16[1,128,1024]{2,1,0:T(8...) custom-call(s32[2]{0:T(128)S(4)} %get-tuple-element.76.me_ref, ...), custom_call_target="tpu_custom_call" | custom-call | flops 536870912 | tf_op jit(solution)/shard_map/pallas_call | solution.py:424
  11.3 1.0 %collective-permute-done.2.refs_5_ = f32[160,128]{1,0:T(8,128)S(1)} collective-permute-done((f32[160,128]{1,0:T(8,128)S(1)}, f32[160,128]{1,0:T(8,128)S(1)}, u32[]{:S(2)}, u32[]{:S(2)}) %collective-permute-start.2) | collective-permute-done | bytes 81952 | tf_op jit(solution)/shard_map/ppermute | solution.py:439
  12.3 0.7 collective-permute-done.3.refs_6_
  13.0 1.6 %collective-permute-start.4 = (f32[160,128]{1,0:T(8,128)S(1)}, f32[160,128]{1,0:T(8,128)S(1)}, u32[]{:S(2)}, u32[]{:S(2)}) collective-permute-start(f32[160,128]{1,0:T(8,128)S(1)} %add_add_fusion.1), channel_id=1, source_target_pairs={{0,2},{2,0},{4,6},{6,4},{1,3},{3,1},{5,7},{7,5},{8,10},{10,8},{12,... | collective-permute-start | bytes 245768 | tf_op jit(solution)/shard_map/ppermute | solution.py:439
  14.6 2.6 %collective-permute-start.5 = (f32[160,128]{1,0:T(8,128)S(1)}, f32[160,128]{1,0:T(8,128)S(1)}, u32[]{:S(2)}, u32[]{:S(2)}) collective-permute-start(f32[160,128]{1,0:T(8,128)S(1)} %add_add_fusion.1), channel_id=1, source_target_pairs={{0,4},{2,6},{4,0},{6,2},{1,5},{3,7},{5,1},{7,3},{8,12},{10,14},{12... | collective-permute-start | bytes 245768 | tf_op jit(solution)/shard_map/ppermute | solution.py:439
  17.4 3.6 %shard_map.91 = (f32[2,1024,128]{2,1,0:T(8,128)S(1)}, f32[2,1024,128]{2,1,0:T(8,128)S(1)}, bf16[2,1024,128]{2,1,0:T(8,128)(2,1)S(1)}, bf16[2,128,1024]{2,1,0:T(8...) custom-call(s32[2]{0:T(128)S(4)} %get-tuple-element.76.me_ref, ...), custom_call_target="tpu_custom_call" | custom-call | flops 1073741824 | tf_op jit(solution)/shard_map/pallas_call | solution.py:424
  21.0 3.1 %collective-permute-done.5.refs_1_ = f32[160,128]{1,0:T(8,128)S(1)} collective-permute-done((f32[160,128]{1,0:T(8,128)S(1)}, f32[160,128]{1,0:T(8,128)S(1)}, u32[]{:S(2)}, u32[]{:S(2)}) %collective-permute-start.5) | collective-permute-done | bytes 81952 | tf_op jit(solution)/shard_map/ppermute | solution.py:439
  24.3 1.8 %collective-permute-start.9 = (f32[160,128]{1,0:T(8,128)S(1)}, f32[160,128]{1,0:T(8,128)S(1)}, u32[]{:S(2)}, u32[]{:S(2)}) collective-permute-start(f32[160,128]{1,0:T(8,128)S(1)} %get-tuple-element.111), channel_id=1, source_target_pairs={{0,17},{1,16},{8,25},{9,24},{16,1},{17,0},{24,9},{25,8},{2,19},{3,... | collective-permute-start | bytes 245768 | tf_op jit(solution)/shard_map/ppermute | solution.py:439
  26.0 1.8 %shard_map.87 = (f32[1,1024,128]{2,1,0:T(8,128)S(1)}, f32[1,1024,128]{2,1,0:T(8,128)S(1)}, bf16[1,1024,128]{2,1,0:T(8,128)(2,1)S(1)}, bf16[1,128,1024]{2,1,0:T(8...) custom-call(s32[2]{0:T(128)S(4)} %get-tuple-element.76.me_ref, ...), custom_call_target="tpu_custom_call" | custom-call | flops 536870912 | tf_op jit(solution)/shard_map/pallas_call | solution.py:424
  27.8 0.6 shard_map.96
  28.5 1.0 %collective-permute-start.8 = (f32[160,128]{1,0:T(8,128)S(1)}, f32[160,128]{1,0:T(8,128)S(1)}, u32[]{:S(2)}, u32[]{:S(2)}) collective-permute-start(f32[160,128]{1,0:T(8,128)S(1)} %get-tuple-element.109), channel_id=1, source_target_pairs={{0,9},{1,8},{8,1},{9,0},{16,25},{17,24},{24,17},{25,16},{2,11},{3,... | collective-permute-start | bytes 245768 | tf_op jit(solution)/shard_map/ppermute | solution.py:439
  29.4 0.6 shard_map.88
  30.1 1.5 %shard_map.92 = (f32[2,1024,256]{2,1,0:T(8,128)S(1)}, bf16[2,1024,256]{2,1,0:T(8,128)(2,1)S(1)}, bf16[2,1024,256]{2,1,0:T(8,128)(2,1)S(1)}, bf16[2,320,1024]{2,1,0:T(8,128)(2,1)S(1)}) custom-call(s32[2]{0:T(128)S(4)} %get-tuple-element.76.me_ref, bf16[4,1024,128]{2,1,0:T(8,128)(2,1)S(1)} %get-tuple-element.78.q_ref.refs_0_, ...), custom_call_target="tpu_custom_call" | custom-call | flops 268435456 | tf_op jit(solution)/shard_map/pallas_call | solution.py:424
  31.6 0.7 collective-permute-start.7
  32.3 0.8 %shard_map.97 = (bf16[1024,128]{1,0:T(8,128)(2,1)S(1)}, f32[1024,128]{1,0:T(8,128)S(1)}, f32[1024,128]{1,0:T(8,128)S(1)}, f32[160,128]{1,0:T(8,128)S(1)}) custom-call(s32[2]{0:T(128)S(4)} %get-tuple-element.76.me_ref, bf16[4,1024,128]{2,1,0:T(8,128)(2,1)S(1)} %get-tuple-element.87.t_ref, f32[1,1024,128]{2,1,0:T(8,128)S(1)} %get-tuple-element.113.rest_0_, ...), custom_call_target="tpu_custom_call" | custom-call | flops 268435456 | tf_op jit(solution)/shard_map/pallas_call | solution.py:424
  33.2 1.5 %collective-permute-start.13 = (f32[160,128]{1,0:T(8,128)S(1)}, f32[160,128]{1,0:T(8,128)S(1)}, u32[]{:S(2)}, u32[]{:S(2)}) collective-permute-start(f32[160,128]{1,0:T(8,128)S(1)} %get-tuple-element.126), channel_id=1, source_target_pairs={{0,24},{8,16},{16,8},{24,0},{1,25},{9,17},{17,9},{25,1},{2,26},{10... | collective-permute-start | bytes 245768 | tf_op jit(solution)/shard_map/ppermute | solution.py:439
  34.7 0.8 %shard_map.94 = (bf16[1024,128]{1,0:T(8,128)(2,1)S(1)}, f32[1024,128]{1,0:T(8,128)S(1)}, f32[1024,128]{1,0:T(8,128)S(1)}, f32[160,128]{1,0:T(8,128)S(1)}) custom-call(s32[2]{0:T(128)S(4)} %get-tuple-element.76.me_ref, bf16[4,1024,128]{2,1,0:T(8,128)(2,1)S(1)} %get-tuple-element.87.t_ref, f32[2,1024,128]{2,1,0:T(8,128)S(1)} %get-tuple-element.102.rest_0_, ...), custom_call_target="tpu_custom_call" | custom-call | flops 268435456 | tf_op jit(solution)/shard_map/pallas_call | solution.py:424
  35.5 0.7 collective-permute-start.12
  36.2 0.8 %shard_map.93 = (bf16[1024,128]{1,0:T(8,128)(2,1)S(1)}, f32[1024,128]{1,0:T(8,128)S(1)}, f32[1024,128]{1,0:T(8,128)S(1)}, f32[160,128]{1,0:T(8,128)S(1)}) custom-call(s32[2]{0:T(128)S(4)} %get-tuple-element.76.me_ref, bf16[4,1024,128]{2,1,0:T(8,128)(2,1)S(1)} %get-tuple-element.87.t_ref, f32[2,1024,128]{2,1,0:T(8,128)S(1)} %get-tuple-element.102.rest_0_, ...), custom_call_target="tpu_custom_call" | custom-call | flops 268435456 | tf_op jit(solution)/shard_map/pallas_call | solution.py:424
  37.0 1.5 %collective-permute-start.11 = (f32[160,128]{1,0:T(8,128)S(1)}, f32[160,128]{1,0:T(8,128)S(1)}, u32[]{:S(2)}, u32[]{:S(2)}) collective-permute-start(f32[160,128]{1,0:T(8,128)S(1)} %get-tuple-element.124), channel_id=1, source_target_pairs={{0,8},{8,0},{16,24},{24,16},{1,9},{9,1},{17,25},{25,17},{2,10},{10... | collective-permute-start | bytes 245768 | tf_op jit(solution)/shard_map/ppermute | solution.py:439
  38.5 5.1 %shard_map.100 = (f32[2,16,1024]{2,1,0:T(8,128)S(1)}, f32[16,128]{1,0:T(8,128)S(1)}) custom-call(s32[2]{0:T(128)S(4)} %get-tuple-element.76.me_ref, bf16[4,1024,128]{2,1,0:T(8,128)(2,1)S(1)} %get-tuple-element.78.q_ref.refs_0_, bf16[4,128,1024]{2,1,0:T(8,128)(2,1)S(1)} %get-tuple-element.79.refs_1_.vt_ref, ...), custom_call_target="tpu_custom_call" | custom-call | flops 2147483648 | tf_op jit(solution)/shard_map/pallas_call | solution.py:424
  43.7 0.9 %shard_map.90 = (bf16[1024,128]{1,0:T(8,128)(2,1)S(1)}, f32[1024,128]{1,0:T(8,128)S(1)}, f32[1024,128]{1,0:T(8,128)S(1)}, f32[160,128]{1,0:T(8,128)S(1)}) custom-call(s32[2]{0:T(128)S(4)} %get-tuple-element.76.me_ref, bf16[4,1024,128]{2,1,0:T(8,128)(2,1)S(1)} %get-tuple-element.87.t_ref, f32[1,1024,128]{2,1,0:T(8,128)S(1)} %get-tuple-element.88.rest_0_, ...), custom_call_target="tpu_custom_call" | custom-call | flops 268435456 | tf_op jit(solution)/shard_map/pallas_call | solution.py:424
  44.6 1.8 %collective-permute-start.14 = (f32[160,128]{1,0:T(8,128)S(1)}, f32[160,128]{1,0:T(8,128)S(1)}, u32[]{:S(2)}, u32[]{:S(2)}) collective-permute-start(f32[160,128]{1,0:T(8,128)S(1)} %add_add_fusion), channel_id=1, source_target_pairs={{0,2},{2,0},{4,6},{6,4},{1,3},{3,1},{5,7},{7,5},{8,10},{10,8},{12,... | collective-permute-start | bytes 245768 | tf_op jit(solution)/shard_map/ppermute | solution.py:439
  46.4 1.5 %collective-permute-start.15 = (f32[160,128]{1,0:T(8,128)S(1)}, f32[160,128]{1,0:T(8,128)S(1)}, u32[]{:S(2)}, u32[]{:S(2)}) collective-permute-start(f32[160,128]{1,0:T(8,128)S(1)} %add_add_fusion), channel_id=1, source_target_pairs={{0,4},{2,6},{4,0},{6,2},{1,5},{3,7},{5,1},{7,3},{8,12},{10,14},{12... | collective-permute-start | bytes 245768 | tf_op jit(solution)/shard_map/ppermute | solution.py:439
  48.0 1.1 %collective-permute-start.16 = (f32[160,128]{1,0:T(8,128)S(1)}, f32[160,128]{1,0:T(8,128)S(1)}, u32[]{:S(2)}, u32[]{:S(2)}) collective-permute-start(f32[160,128]{1,0:T(8,128)S(1)} %add_add_fusion), channel_id=1, source_target_pairs={{0,6},{2,4},{4,2},{6,0},{1,7},{3,5},{5,3},{7,1},{8,14},{10,12},{12... | collective-permute-start | bytes 245768 | tf_op jit(solution)/shard_map/ppermute | solution.py:439
  49.1 2.7 %shard_map.101 = (f32[1,16,1024]{2,1,0:T(8,128)S(1)}, f32[16,128]{1,0:T(8,128)S(1)}) custom-call(s32[2]{0:T(128)S(4)} %get-tuple-element.76.me_ref, bf16[4,1024,128]{2,1,0:T(8,128)(2,1)S(1)} %get-tuple-element.78.q_ref.refs_0_, bf16[4,128,1024]{2,1,0:T(8,128)(2,1)S(1)} %get-tuple-element.79.refs_1_.vt_ref, ...), custom_call_target="tpu_custom_call" | custom-call | flops 1073741824 | tf_op jit(solution)/shard_map/pallas_call | solution.py:424
  51.8 3.2 %collective-permute-done.15.refs_1_ = f32[160,128]{1,0:T(8,128)S(1)} collective-permute-done((f32[160,128]{1,0:T(8,128)S(1)}, f32[160,128]{1,0:T(8,128)S(1)}, u32[]{:S(2)}, u32[]{:S(2)}) %collective-permute-start.15) | collective-permute-done | bytes 81952 | tf_op jit(solution)/shard_map/ppermute | solution.py:439
  55.0 0.6 collective-permute-start.17
  55.7 1.2 %collective-permute-start.18 = (f32[160,128]{1,0:T(8,128)S(1)}, f32[160,128]{1,0:T(8,128)S(1)}, u32[]{:S(2)}, u32[]{:S(2)}) collective-permute-start(f32[160,128]{1,0:T(8,128)S(1)} %get-tuple-element.128), channel_id=1, source_target_pairs={{0,16},{8,24},{16,0},{24,8},{1,17},{9,25},{17,1},{25,9},{2,18},{10... | collective-permute-start | bytes 245768 | tf_op jit(solution)/shard_map/ppermute | solution.py:439
  56.9 1.7 %collective-permute-start.19 = (f32[160,128]{1,0:T(8,128)S(1)}, f32[160,128]{1,0:T(8,128)S(1)}, u32[]{:S(2)}, u32[]{:S(2)}) collective-permute-start(f32[160,128]{1,0:T(8,128)S(1)} %get-tuple-element.129), channel_id=1, source_target_pairs={{0,24},{8,16},{16,8},{24,0},{1,25},{9,17},{17,9},{25,1},{2,26},{10... | collective-permute-start | bytes 245768 | tf_op jit(solution)/shard_map/ppermute | solution.py:439
  58.6 3.6 %shard_map.98 = (f32[1,16,1024]{2,1,0:T(8,128)S(1)}, f32[16,128]{1,0:T(8,128)S(1)}, bf16[4,1024,128]{2,1,0:T(8,128)(2,1)}) custom-call(s32[2]{0:T(128)S(4)} %get-tuple-element.76.me_ref, bf16[4,1024,128]{2,1,0:T(8,128)(2,1)S(1)} %get-tuple-element.78.q_ref.refs_0_, bf16[4,128,1024]{2,1,0:T(8,128)(2,1)S(1)} %get-tuple-element.79.refs_1_.vt_ref, ...), custom_call_target="tpu_custom_call" | custom-call | flops 1073741824 | tf_op jit(solution)/shard_map/pallas_call | solution.py:424
  62.7 1.2 %shard_map.103 = f32[32,128]{1,0:T(8,128)S(1)} custom-call(s32[2]{0:T(128)S(4)} %get-tuple-element.76.me_ref, bf16[4,1024,128]{2,1,0:T(8,128)(2,1)S(1)} %get-tuple-element.80.k_ref, bf16[4,128,1024]{2,1,0:T(8,128)(2,1)S(1)} %get-tuple-element.79.refs_1_.vt_ref, f32[16,128]{1,0:T(8,128)S(1)} %get-tuple-element.82.wk_ref, ...), custom_call_target="tpu_custom_call" | custom-call | flops 251658240 | tf_op jit(solution)/shard_map/pallas_call | solution.py:424
  63.9 1.2 %collective-permute-done.20 = f32[32,128]{1,0:T(8,128)S(1)} collective-permute-done((f32[32,128]{1,0:T(8,128)S(1)}, f32[32,128]{1,0:T(8,128)S(1)}, u32[]{:S(2)}, u32[]{:S(2)}) %collective-permute-start.20) | collective-permute-done | bytes 16416 | tf_op jit(solution)/shard_map/ppermute | solution.py:439
  65.1 0.8 %collective-permute-start.21 = (f32[32,128]{1,0:T(8,128)S(1)}, f32[32,128]{1,0:T(8,128)S(1)}, u32[]{:S(2)}, u32[]{:S(2)}) collective-permute-start(f32[32,128]{1,0:T(8,128)S(1)} %add.45), channel_id=1, source_target_pairs={{0,9},{1,8},{8,1},{9,0},{16,25},{17,24},{24,17},{25,16},{2,11},{3,... | collective-permute-start | bytes 49160 | tf_op jit(solution)/shard_map/ppermute | solution.py:439
  65.9 0.7 collective-permute-start.22
  66.6 1.5 %collective-permute-start.23 = (f32[32,128]{1,0:T(8,128)S(1)}, f32[32,128]{1,0:T(8,128)S(1)}, u32[]{:S(2)}, u32[]{:S(2)}) collective-permute-start(f32[32,128]{1,0:T(8,128)S(1)} %add.45), channel_id=1, source_target_pairs={{0,25},{1,24},{8,17},{9,16},{16,9},{17,8},{24,1},{25,0},{2,27},{3,... | collective-permute-start | bytes 49160 | tf_op jit(solution)/shard_map/ppermute | solution.py:439
  68.3 0.8 %collective-permute-done.22 = f32[32,128]{1,0:T(8,128)S(1)} collective-permute-done((f32[32,128]{1,0:T(8,128)S(1)}, f32[32,128]{1,0:T(8,128)S(1)}, u32[]{:S(2)}, u32[]{:S(2)}) %collective-permute-start.22) | collective-permute-done | bytes 16416 | tf_op jit(solution)/shard_map/ppermute | solution.py:439
  69.1 1.6 %collective-permute-done.23 = f32[32,128]{1,0:T(8,128)S(1)} collective-permute-done((f32[32,128]{1,0:T(8,128)S(1)}, f32[32,128]{1,0:T(8,128)S(1)}, u32[]{:S(2)}, u32[]{:S(2)}) %collective-permute-start.23) | collective-permute-done | bytes 16416 | tf_op jit(solution)/shard_map/ppermute | solution.py:439
  70.7 1.2 %collective-permute-start.24 = (f32[32,128]{1,0:T(8,128)S(1)}, f32[32,128]{1,0:T(8,128)S(1)}, u32[]{:S(2)}, u32[]{:S(2)}) collective-permute-start(f32[32,128]{1,0:T(8,128)S(1)} %add_add_fusion.3), channel_id=1, source_target_pairs={{0,3},{1,2},{2,1},{3,0},{4,7},{5,6},{6,5},{7,4},{8,11},{9,10},{10,... | collective-permute-start | bytes 49160 | tf_op jit(solution)/shard_map/ppermute | solution.py:439
  71.9 1.4 %collective-permute-start.25 = (f32[32,128]{1,0:T(8,128)S(1)}, f32[32,128]{1,0:T(8,128)S(1)}, u32[]{:S(2)}, u32[]{:S(2)}) collective-permute-start(f32[32,128]{1,0:T(8,128)S(1)} %add_add_fusion.3), channel_id=1, source_target_pairs={{0,5},{1,4},{2,7},{3,6},{4,1},{5,0},{6,3},{7,2},{8,13},{9,12},{10,... | collective-permute-start | bytes 49160 | tf_op jit(solution)/shard_map/ppermute | solution.py:439
  73.3 1.2 %collective-permute-start.26 = (f32[32,128]{1,0:T(8,128)S(1)}, f32[32,128]{1,0:T(8,128)S(1)}, u32[]{:S(2)}, u32[]{:S(2)}) collective-permute-start(f32[32,128]{1,0:T(8,128)S(1)} %add_add_fusion.3), channel_id=1, source_target_pairs={{0,7},{1,6},{2,5},{3,4},{4,3},{5,2},{6,1},{7,0},{8,15},{9,14},{10,... | collective-permute-start | bytes 49160 | tf_op jit(solution)/shard_map/ppermute | solution.py:439
  74.6 1.6 %collective-permute-done.25 = f32[32,128]{1,0:T(8,128)S(1)} collective-permute-done((f32[32,128]{1,0:T(8,128)S(1)}, f32[32,128]{1,0:T(8,128)S(1)}, u32[]{:S(2)}, u32[]{:S(2)}) %collective-permute-start.25) | collective-permute-done | bytes 16416 | tf_op jit(solution)/shard_map/ppermute | solution.py:439
  76.1 2.1 %collective-permute-done.26 = f32[32,128]{1,0:T(8,128)S(1)} collective-permute-done((f32[32,128]{1,0:T(8,128)S(1)}, f32[32,128]{1,0:T(8,128)S(1)}, u32[]{:S(2)}, u32[]{:S(2)}) %collective-permute-start.26) | collective-permute-done | bytes 16416 | tf_op jit(solution)/shard_map/ppermute | solution.py:439
  78.3 0.6 slice_bitcast_fusion
  (32 shorter events, 1.9 us)
Async XLA Ops:
  3.6 7.7 %collective-permute-start = (f32[160,128]{1,0:T(8,128)S(1)}, f32[160,128]{1,0:T(8,128)S(1)}, u32[]{:S(2)}, u32[]{:S(2)}) collective-permute-start(f32[160,128]{1,0:T(8,128)S(1)} %get-tuple-element.94), channel_id=1, source_target_pairs={{0,1},{1,0},{8,9},{9,8},{16,17},{17,16},{24,25},{25,24},{2,3},{3,2... | collective-permute-start | bytes 245768 | tf_op jit(solution)/shard_map/ppermute | solution.py:439
  4.1 7.2 %collective-permute-start.1 = (f32[160,128]{1,0:T(8,128)S(1)}, f32[160,128]{1,0:T(8,128)S(1)}, u32[]{:S(2)}, u32[]{:S(2)}) collective-permute-start(f32[160,128]{1,0:T(8,128)S(1)} %get-tuple-element.95), channel_id=1, source_target_pairs={{0,9},{1,8},{8,1},{9,0},{16,25},{17,24},{24,17},{25,16},{2,11},{3,... | collective-permute-start | bytes 245768 | tf_op jit(solution)/shard_map/ppermute | solution.py:439
  6.7 5.6 %collective-permute-start.2 = (f32[160,128]{1,0:T(8,128)S(1)}, f32[160,128]{1,0:T(8,128)S(1)}, u32[]{:S(2)}, u32[]{:S(2)}) collective-permute-start(f32[160,128]{1,0:T(8,128)S(1)} %get-tuple-element.96), channel_id=1, source_target_pairs={{0,17},{1,16},{8,25},{9,24},{16,1},{17,0},{24,9},{25,8},{2,19},{3,... | collective-permute-start | bytes 245768 | tf_op jit(solution)/shard_map/ppermute | solution.py:439
  7.9 5.0 %collective-permute-start.3 = (f32[160,128]{1,0:T(8,128)S(1)}, f32[160,128]{1,0:T(8,128)S(1)}, u32[]{:S(2)}, u32[]{:S(2)}) collective-permute-start(f32[160,128]{1,0:T(8,128)S(1)} %get-tuple-element.97), channel_id=1, source_target_pairs={{0,25},{1,24},{8,17},{9,16},{16,9},{17,8},{24,1},{25,0},{2,27},{3,... | collective-permute-start | bytes 245768 | tf_op jit(solution)/shard_map/ppermute | solution.py:439
  13.0 8.1 %collective-permute-start.4 = (f32[160,128]{1,0:T(8,128)S(1)}, f32[160,128]{1,0:T(8,128)S(1)}, u32[]{:S(2)}, u32[]{:S(2)}) collective-permute-start(f32[160,128]{1,0:T(8,128)S(1)} %add_add_fusion.1), channel_id=1, source_target_pairs={{0,2},{2,0},{4,6},{6,4},{1,3},{3,1},{5,7},{7,5},{8,10},{10,8},{12,... | collective-permute-start | bytes 245768 | tf_op jit(solution)/shard_map/ppermute | solution.py:439
  14.6 9.5 %collective-permute-start.5 = (f32[160,128]{1,0:T(8,128)S(1)}, f32[160,128]{1,0:T(8,128)S(1)}, u32[]{:S(2)}, u32[]{:S(2)}) collective-permute-start(f32[160,128]{1,0:T(8,128)S(1)} %add_add_fusion.1), channel_id=1, source_target_pairs={{0,4},{2,6},{4,0},{6,2},{1,5},{3,7},{5,1},{7,3},{8,12},{10,14},{12... | collective-permute-start | bytes 245768 | tf_op jit(solution)/shard_map/ppermute | solution.py:439
  17.2 6.9 %collective-permute-start.6 = (f32[160,128]{1,0:T(8,128)S(1)}, f32[160,128]{1,0:T(8,128)S(1)}, u32[]{:S(2)}, u32[]{:S(2)}) collective-permute-start(f32[160,128]{1,0:T(8,128)S(1)} %add_add_fusion.1), channel_id=1, source_target_pairs={{0,6},{2,4},{4,2},{6,0},{1,7},{3,5},{5,3},{7,1},{8,14},{10,12},{12... | collective-permute-start | bytes 245768 | tf_op jit(solution)/shard_map/ppermute | solution.py:439
  24.2 8.1 %collective-permute-start.10 = (f32[160,128]{1,0:T(8,128)S(1)}, f32[160,128]{1,0:T(8,128)S(1)}, u32[]{:S(2)}, u32[]{:S(2)}) collective-permute-start(f32[160,128]{1,0:T(8,128)S(1)} %get-tuple-element.120), channel_id=1, source_target_pairs={{0,25},{1,24},{8,17},{9,16},{16,9},{17,8},{24,1},{25,0},{2,27},{3,... | collective-permute-start | bytes 245768 | tf_op jit(solution)/shard_map/ppermute | solution.py:439
  24.3 10.4 %collective-permute-start.9 = (f32[160,128]{1,0:T(8,128)S(1)}, f32[160,128]{1,0:T(8,128)S(1)}, u32[]{:S(2)}, u32[]{:S(2)}) collective-permute-start(f32[160,128]{1,0:T(8,128)S(1)} %get-tuple-element.111), channel_id=1, source_target_pairs={{0,17},{1,16},{8,25},{9,24},{16,1},{17,0},{24,9},{25,8},{2,19},{3,... | collective-permute-start | bytes 245768 | tf_op jit(solution)/shard_map/ppermute | solution.py:439
  28.5 7.7 %collective-permute-start.8 = (f32[160,128]{1,0:T(8,128)S(1)}, f32[160,128]{1,0:T(8,128)S(1)}, u32[]{:S(2)}, u32[]{:S(2)}) collective-permute-start(f32[160,128]{1,0:T(8,128)S(1)} %get-tuple-element.109), channel_id=1, source_target_pairs={{0,9},{1,8},{8,1},{9,0},{16,25},{17,24},{24,17},{25,16},{2,11},{3,... | collective-permute-start | bytes 245768 | tf_op jit(solution)/shard_map/ppermute | solution.py:439
  31.6 12.0 %collective-permute-start.7 = (f32[160,128]{1,0:T(8,128)S(1)}, f32[160,128]{1,0:T(8,128)S(1)}, u32[]{:S(2)}, u32[]{:S(2)}) collective-permute-start(f32[160,128]{1,0:T(8,128)S(1)} %get-tuple-element.98), channel_id=1, source_target_pairs={{0,1},{1,0},{8,9},{9,8},{16,17},{17,16},{24,25},{25,24},{2,3},{3,2... | collective-permute-start | bytes 245768 | tf_op jit(solution)/shard_map/ppermute | solution.py:439
  33.2 11.4 %collective-permute-start.13 = (f32[160,128]{1,0:T(8,128)S(1)}, f32[160,128]{1,0:T(8,128)S(1)}, u32[]{:S(2)}, u32[]{:S(2)}) collective-permute-start(f32[160,128]{1,0:T(8,128)S(1)} %get-tuple-element.126), channel_id=1, source_target_pairs={{0,24},{8,16},{16,8},{24,0},{1,25},{9,17},{17,9},{25,1},{2,26},{10... | collective-permute-start | bytes 245768 | tf_op jit(solution)/shard_map/ppermute | solution.py:439
  35.5 9.0 %collective-permute-start.12 = (f32[160,128]{1,0:T(8,128)S(1)}, f32[160,128]{1,0:T(8,128)S(1)}, u32[]{:S(2)}, u32[]{:S(2)}) collective-permute-start(f32[160,128]{1,0:T(8,128)S(1)} %get-tuple-element.125), channel_id=1, source_target_pairs={{0,16},{8,24},{16,0},{24,8},{1,17},{9,25},{17,1},{25,9},{2,18},{10... | collective-permute-start | bytes 245768 | tf_op jit(solution)/shard_map/ppermute | solution.py:439
  37.0 7.5 %collective-permute-start.11 = (f32[160,128]{1,0:T(8,128)S(1)}, f32[160,128]{1,0:T(8,128)S(1)}, u32[]{:S(2)}, u32[]{:S(2)}) collective-permute-start(f32[160,128]{1,0:T(8,128)S(1)} %get-tuple-element.124), channel_id=1, source_target_pairs={{0,8},{8,0},{16,24},{24,16},{1,9},{9,1},{17,25},{25,17},{2,10},{10... | collective-permute-start | bytes 245768 | tf_op jit(solution)/shard_map/ppermute | solution.py:439
  44.6 7.1 %collective-permute-start.14 = (f32[160,128]{1,0:T(8,128)S(1)}, f32[160,128]{1,0:T(8,128)S(1)}, u32[]{:S(2)}, u32[]{:S(2)}) collective-permute-start(f32[160,128]{1,0:T(8,128)S(1)} %add_add_fusion), channel_id=1, source_target_pairs={{0,2},{2,0},{4,6},{6,4},{1,3},{3,1},{5,7},{7,5},{8,10},{10,8},{12,... | collective-permute-start | bytes 245768 | tf_op jit(solution)/shard_map/ppermute | solution.py:439
  46.4 8.5 %collective-permute-start.15 = (f32[160,128]{1,0:T(8,128)S(1)}, f32[160,128]{1,0:T(8,128)S(1)}, u32[]{:S(2)}, u32[]{:S(2)}) collective-permute-start(f32[160,128]{1,0:T(8,128)S(1)} %add_add_fusion), channel_id=1, source_target_pairs={{0,4},{2,6},{4,0},{6,2},{1,5},{3,7},{5,1},{7,3},{8,12},{10,14},{12... | collective-permute-start | bytes 245768 | tf_op jit(solution)/shard_map/ppermute | solution.py:439
  48.0 7.0 %collective-permute-start.16 = (f32[160,128]{1,0:T(8,128)S(1)}, f32[160,128]{1,0:T(8,128)S(1)}, u32[]{:S(2)}, u32[]{:S(2)}) collective-permute-start(f32[160,128]{1,0:T(8,128)S(1)} %add_add_fusion), channel_id=1, source_target_pairs={{0,6},{2,4},{4,2},{6,0},{1,7},{3,5},{5,3},{7,1},{8,14},{10,12},{12... | collective-permute-start | bytes 245768 | tf_op jit(solution)/shard_map/ppermute | solution.py:439
  55.0 7.6 %collective-permute-start.17 = (f32[160,128]{1,0:T(8,128)S(1)}, f32[160,128]{1,0:T(8,128)S(1)}, u32[]{:S(2)}, u32[]{:S(2)}) collective-permute-start(f32[160,128]{1,0:T(8,128)S(1)} %get-tuple-element.127), channel_id=1, source_target_pairs={{0,8},{8,0},{16,24},{24,16},{1,9},{9,1},{17,25},{25,17},{2,10},{10... | collective-permute-start | bytes 245768 | tf_op jit(solution)/shard_map/ppermute | solution.py:439
  55.7 7.0 %collective-permute-start.18 = (f32[160,128]{1,0:T(8,128)S(1)}, f32[160,128]{1,0:T(8,128)S(1)}, u32[]{:S(2)}, u32[]{:S(2)}) collective-permute-start(f32[160,128]{1,0:T(8,128)S(1)} %get-tuple-element.128), channel_id=1, source_target_pairs={{0,16},{8,24},{16,0},{24,8},{1,17},{9,25},{17,1},{25,9},{2,18},{10... | collective-permute-start | bytes 245768 | tf_op jit(solution)/shard_map/ppermute | solution.py:439
  56.9 5.8 %collective-permute-start.19 = (f32[160,128]{1,0:T(8,128)S(1)}, f32[160,128]{1,0:T(8,128)S(1)}, u32[]{:S(2)}, u32[]{:S(2)}) collective-permute-start(f32[160,128]{1,0:T(8,128)S(1)} %get-tuple-element.129), channel_id=1, source_target_pairs={{0,24},{8,16},{16,8},{24,0},{1,25},{9,17},{17,9},{25,1},{2,26},{10... | collective-permute-start | bytes 245768 | tf_op jit(solution)/shard_map/ppermute | solution.py:439
  63.9 1.2 %collective-permute-start.20 = (f32[32,128]{1,0:T(8,128)S(1)}, f32[32,128]{1,0:T(8,128)S(1)}, u32[]{:S(2)}, u32[]{:S(2)}) collective-permute-start(f32[32,128]{1,0:T(8,128)S(1)} %shard_map.103), channel_id=1, source_target_pairs={{0,1},{1,0},{2,3},{3,2},{4,5},{5,4},{6,7},{7,6},{8,9},{9,8},{10,11... | collective-permute-start | bytes 49160 | tf_op jit(solution)/shard_map/ppermute | solution.py:439
  65.1 3.2 %collective-permute-start.21 = (f32[32,128]{1,0:T(8,128)S(1)}, f32[32,128]{1,0:T(8,128)S(1)}, u32[]{:S(2)}, u32[]{:S(2)}) collective-permute-start(f32[32,128]{1,0:T(8,128)S(1)} %add.45), channel_id=1, source_target_pairs={{0,9},{1,8},{8,1},{9,0},{16,25},{17,24},{24,17},{25,16},{2,11},{3,... | collective-permute-start | bytes 49160 | tf_op jit(solution)/shard_map/ppermute | solution.py:439
  65.9 3.2 %collective-permute-start.22 = (f32[32,128]{1,0:T(8,128)S(1)}, f32[32,128]{1,0:T(8,128)S(1)}, u32[]{:S(2)}, u32[]{:S(2)}) collective-permute-start(f32[32,128]{1,0:T(8,128)S(1)} %add.45), channel_id=1, source_target_pairs={{0,17},{1,16},{8,25},{9,24},{16,1},{17,0},{24,9},{25,8},{2,19},{3,... | collective-permute-start | bytes 49160 | tf_op jit(solution)/shard_map/ppermute | solution.py:439
  66.6 4.1 %collective-permute-start.23 = (f32[32,128]{1,0:T(8,128)S(1)}, f32[32,128]{1,0:T(8,128)S(1)}, u32[]{:S(2)}, u32[]{:S(2)}) collective-permute-start(f32[32,128]{1,0:T(8,128)S(1)} %add.45), channel_id=1, source_target_pairs={{0,25},{1,24},{8,17},{9,16},{16,9},{17,8},{24,1},{25,0},{2,27},{3,... | collective-permute-start | bytes 49160 | tf_op jit(solution)/shard_map/ppermute | solution.py:439
  70.7 3.9 %collective-permute-start.24 = (f32[32,128]{1,0:T(8,128)S(1)}, f32[32,128]{1,0:T(8,128)S(1)}, u32[]{:S(2)}, u32[]{:S(2)}) collective-permute-start(f32[32,128]{1,0:T(8,128)S(1)} %add_add_fusion.3), channel_id=1, source_target_pairs={{0,3},{1,2},{2,1},{3,0},{4,7},{5,6},{6,5},{7,4},{8,11},{9,10},{10,... | collective-permute-start | bytes 49160 | tf_op jit(solution)/shard_map/ppermute | solution.py:439
  71.9 4.2 %collective-permute-start.25 = (f32[32,128]{1,0:T(8,128)S(1)}, f32[32,128]{1,0:T(8,128)S(1)}, u32[]{:S(2)}, u32[]{:S(2)}) collective-permute-start(f32[32,128]{1,0:T(8,128)S(1)} %add_add_fusion.3), channel_id=1, source_target_pairs={{0,5},{1,4},{2,7},{3,6},{4,1},{5,0},{6,3},{7,2},{8,13},{9,12},{10,... | collective-permute-start | bytes 49160 | tf_op jit(solution)/shard_map/ppermute | solution.py:439
  73.3 5.0 %collective-permute-start.26 = (f32[32,128]{1,0:T(8,128)S(1)}, f32[32,128]{1,0:T(8,128)S(1)}, u32[]{:S(2)}, u32[]{:S(2)}) collective-permute-start(f32[32,128]{1,0:T(8,128)S(1)} %add_add_fusion.3), channel_id=1, source_target_pairs={{0,7},{1,6},{2,5},{3,4},{4,3},{5,2},{6,1},{7,0},{8,15},{9,14},{10,... | collective-permute-start | bytes 49160 | tf_op jit(solution)/shard_map/ppermute | solution.py:439

commit v6 on v5

--- a/solution.py
+++ b/solution.py
@@ -242,18 +242,15 @@
     below = positions((tile, tile), 0) >= positions((tile, tile), 1)
     for i in range(tokens // tile):
         rows = slice(i * tile, (i + 1) * tile)
-        numer = jnp.zeros((tile, v.shape[1]), f32)
-        denom = jnp.zeros((tile, LANES), f32)
-        for j in range(i + 1):
-            cols = slice(j * tile, (j + 1) * tile)
-            t = dot(q_pack[rows], k_pack[:, cols])
-            weight = (0.5 * t) * t + 0.5
-            if j == i:
-                weight = jnp.where(below, weight, 0.0)
-            for c in range(tile // LANES):
-                denom = denom + weight[:, c * LANES : (c + 1) * LANES]
-            numer = numer + dot(weight.astype(bf16), v[cols])
-        numer_ref[h, rows, :] = numer
+        width = (i + 1) * tile
+        t = dot(q_pack[rows], k_pack[:, :width])
+        weight = (0.5 * t) * t + 0.5
+        last = jnp.where(below, weight[:, width - tile :], 0.0)
+        weight = jnp.concatenate([weight[:, : width - tile], last], 1) if i else last
+        numer_ref[h, rows, :] = dot(weight.astype(bf16), v[:width])
+        denom = weight[:, :LANES]
+        for c in range(LANES, width, LANES):
+            denom = denom + weight[:, c : c + LANES]
         denom_ref[h, rows, :] = denom
 
 
@@ -314,9 +311,8 @@
         inv = 1.0 / jnp.sum(part, 1, keepdims=True)
         y = numer * inv
         student_ref[rows] = y.astype(bf16)
-        g_out = scale * (y - teacher[rows].astype(f32))
-        g_numer = g_out * inv
-        g_denom = -jnp.sum(g_out * y, 1, keepdims=True) * inv
+        g_numer = (y - teacher[rows].astype(f32)) * (scale * inv)
+        g_denom = -jnp.sum(g_numer * y, 1, keepdims=True)
         g_ref[rows] = g_numer
         gd_ref[rows] = jnp.broadcast_to(g_denom, part.shape)
         count = count + jnp.sum(phi * g_denom, 0, keepdims=True)
@@ -614,7 +610,7 @@
         backs += outs[:2]
     spots = [(p0 + i, i, part) for part, (p0, count) in enumerate(parts) for i in range(count)]
     grads = backs[1::2]
-    for step, group in enumerate((spots[:1], spots[1:])):
+    for step, group in enumerate(g for g in (spots[:1], spots[1:][-1:], spots[1:-1]) if g):
         args = (me, keys, vt, wk)
         for p, _, _ in group:
             args += tuple(later[p * per : (p + 1) * per])

time: 79.1 us -> 78.9 us (level)
  Pallas kernels: 31 us -> 30 us
  waiting for transfers between devices: 15.4 us -> 16.2 us
    pallas_call x19 -> x20, Pallas kernels: 31 us -> 30 us  [call(): pl.pallas_call(body, grid=grid, in_specs=specs, out_specs=out_specs, out_...]
    ppermute x27, waiting for transfers between devices: 15.4 us -> 16.2 us  [shifted(): return lax.ppermute(array, axis, pairs)]
  transfers between devices with their start and end apart: 27 -> 27, of which waited for: 10 -> 10; matrix products, arithmetic and copies ran while one was open for 0% -> 0% of each run, Pallas kernels for 34% -> 33%
where the time goes in v6:
time: 78.9 us; the launch traced here: 78.7 us
  starting transfers between devices  30.9 us (39%)
  Pallas kernels  30 us (38%)
  waiting for transfers between devices  16.2 us (21%)
  between operations  0.87 us (1%)
    ppermute x27, starting transfers between devices, shifted(): return lax.ppermute(array, axis, pairs)  30.9 us
    pallas_call x20, Pallas kernels, call(): pl.pallas_call(body, grid=grid, in_specs=specs, out_specs=out_specs, out_...  30 us
    ppermute x27, waiting for transfers between devices, shifted(): return lax.ppermute(array, axis, pairs)  16.2 us
  transfers between devices with their start and end apart: 27, of which 10 were waited for; matrix products, arithmetic and copies ran while one was open for 0% of the time, Pallas kernels for 33%

profile of v6, /device:TPU:0, one launch (start us, length us, event | category | flops | bytes accessed | tf_op | source)
XLA Modules:
  0.0 78.7 jit_solution(4588603834984478448)
XLA Ops:
  0.7 2.8 %shard_map.85 = (f32[160,128]{1,0:T(8,128)S(1)}, f32[160,128]{1,0:T(8,128)S(1)}, f32[160,128]{1,0:T(8,128)S(1)}, f32[160,128]{1,0:T(8,128)S(1)}, f32[16,128]{1,0...) custom-call(s32[2]{0:T(128)S(1)} %pad_add_fusion.me_ref, ...), custom_call_target="tpu_custom_call" | custom-call | flops 335544320 | tf_op jit(solution)/shard_map/pallas_call | solution.py:420
  3.6 0.6 collective-permute-start
  4.1 2.6 %collective-permute-start.1 = (f32[160,128]{1,0:T(8,128)S(1)}, f32[160,128]{1,0:T(8,128)S(1)}, u32[]{:S(2)}, u32[]{:S(2)}) collective-permute-start(f32[160,128]{1,0:T(8,128)S(1)} %get-tuple-element.95), channel_id=1, source_target_pairs={{0,9},{1,8},{8,1},{9,0},{16,25},{17,24},{24,17},{25,16},{2,11},{3,... | collective-permute-start | bytes 245768 | tf_op jit(solution)/shard_map/ppermute | solution.py:435
  6.7 1.2 %collective-permute-start.2 = (f32[160,128]{1,0:T(8,128)S(1)}, f32[160,128]{1,0:T(8,128)S(1)}, u32[]{:S(2)}, u32[]{:S(2)}) collective-permute-start(f32[160,128]{1,0:T(8,128)S(1)} %get-tuple-element.96), channel_id=1, source_target_pairs={{0,17},{1,16},{8,25},{9,24},{16,1},{17,0},{24,9},{25,8},{2,19},{3,... | collective-permute-start | bytes 245768 | tf_op jit(solution)/shard_map/ppermute | solution.py:435
  7.9 1.6 %shard_map.86 = (bf16[4,128,1024]{2,1,0:T(8,128)(2,1)S(1)}, bf16[4,1024,128]{2,1,0:T(8,128)(2,1)S(1)}, bf16[4,1024,128]{2,1,0:T(8,128)(2,1)S(1)}) custom-call(bf16[4,1024,128]{2,1,0:T(8,128)(2,1)S(1)} %get-tuple-element.77.v_ref, bf16[4,1024,128]{2,1,0:T(8,128)(2,1)} %q_hbm.1, bf16[4,1024,128]{2,1,0:T(8,128)(2,1)} %t_hbm.1), custom_call_target="tpu_custom_call" | custom-call | flops 67108864 | tf_op jit(solution)/shard_map/pallas_call | solution.py:420
  9.5 1.5 %shard_map.95 = (f32[1,1024,128]{2,1,0:T(8,128)S(1)}, f32[1,1024,128]{2,1,0:T(8,128)S(1)}, bf16[1,1024,128]{2,1,0:T(8,128)(2,1)S(1)}, bf16[1,128,1024]{2,1,0:T(8...) custom-call(s32[2]{0:T(128)S(4)} %get-tuple-element.76.me_ref, ...), custom_call_target="tpu_custom_call" | custom-call | flops 536870912 | tf_op jit(solution)/shard_map/pallas_call | solution.py:420
  11.0 1.2 %collective-permute-done.2.refs_5_ = f32[160,128]{1,0:T(8,128)S(1)} collective-permute-done((f32[160,128]{1,0:T(8,128)S(1)}, f32[160,128]{1,0:T(8,128)S(1)}, u32[]{:S(2)}, u32[]{:S(2)}) %collective-permute-start.2) | collective-permute-done | bytes 81952 | tf_op jit(solution)/shard_map/ppermute | solution.py:435
  12.3 0.7 collective-permute-done.3.refs_6_
  13.0 1.6 %collective-permute-start.4 = (f32[160,128]{1,0:T(8,128)S(1)}, f32[160,128]{1,0:T(8,128)S(1)}, u32[]{:S(2)}, u32[]{:S(2)}) collective-permute-start(f32[160,128]{1,0:T(8,128)S(1)} %add_add_fusion.1), channel_id=1, source_target_pairs={{0,2},{2,0},{4,6},{6,4},{1,3},{3,1},{5,7},{7,5},{8,10},{10,8},{12,... | collective-permute-start | bytes 245768 | tf_op jit(solution)/shard_map/ppermute | solution.py:435
  14.6 2.6 %collective-permute-start.5 = (f32[160,128]{1,0:T(8,128)S(1)}, f32[160,128]{1,0:T(8,128)S(1)}, u32[]{:S(2)}, u32[]{:S(2)}) collective-permute-start(f32[160,128]{1,0:T(8,128)S(1)} %add_add_fusion.1), channel_id=1, source_target_pairs={{0,4},{2,6},{4,0},{6,2},{1,5},{3,7},{5,1},{7,3},{8,12},{10,14},{12... | collective-permute-start | bytes 245768 | tf_op jit(solution)/shard_map/ppermute | solution.py:435
  17.4 3.0 %shard_map.91 = (f32[2,1024,128]{2,1,0:T(8,128)S(1)}, f32[2,1024,128]{2,1,0:T(8,128)S(1)}, bf16[2,1024,128]{2,1,0:T(8,128)(2,1)S(1)}, bf16[2,128,1024]{2,1,0:T(8...) custom-call(s32[2]{0:T(128)S(4)} %get-tuple-element.76.me_ref, ...), custom_call_target="tpu_custom_call" | custom-call | flops 1073741824 | tf_op jit(solution)/shard_map/pallas_call | solution.py:420
  20.5 3.6 %collective-permute-done.5.refs_1_ = f32[160,128]{1,0:T(8,128)S(1)} collective-permute-done((f32[160,128]{1,0:T(8,128)S(1)}, f32[160,128]{1,0:T(8,128)S(1)}, u32[]{:S(2)}, u32[]{:S(2)}) %collective-permute-start.5) | collective-permute-done | bytes 81952 | tf_op jit(solution)/shard_map/ppermute | solution.py:435
  24.3 1.8 %collective-permute-start.9 = (f32[160,128]{1,0:T(8,128)S(1)}, f32[160,128]{1,0:T(8,128)S(1)}, u32[]{:S(2)}, u32[]{:S(2)}) collective-permute-start(f32[160,128]{1,0:T(8,128)S(1)} %get-tuple-element.111), channel_id=1, source_target_pairs={{0,17},{1,16},{8,25},{9,24},{16,1},{17,0},{24,9},{25,8},{2,19},{3,... | collective-permute-start | bytes 245768 | tf_op jit(solution)/shard_map/ppermute | solution.py:435
  26.0 1.5 %shard_map.87 = (f32[1,1024,128]{2,1,0:T(8,128)S(1)}, f32[1,1024,128]{2,1,0:T(8,128)S(1)}, bf16[1,1024,128]{2,1,0:T(8,128)(2,1)S(1)}, bf16[1,128,1024]{2,1,0:T(8...) custom-call(s32[2]{0:T(128)S(4)} %get-tuple-element.76.me_ref, ...), custom_call_target="tpu_custom_call" | custom-call | flops 536870912 | tf_op jit(solution)/shard_map/pallas_call | solution.py:420
  27.5 0.6 shard_map.96
  28.2 1.0 %collective-permute-start.8 = (f32[160,128]{1,0:T(8,128)S(1)}, f32[160,128]{1,0:T(8,128)S(1)}, u32[]{:S(2)}, u32[]{:S(2)}) collective-permute-start(f32[160,128]{1,0:T(8,128)S(1)} %get-tuple-element.109), channel_id=1, source_target_pairs={{0,9},{1,8},{8,1},{9,0},{16,25},{17,24},{24,17},{25,16},{2,11},{3,... | collective-permute-start | bytes 245768 | tf_op jit(solution)/shard_map/ppermute | solution.py:435
  29.1 0.6 shard_map.88
  29.8 1.5 %shard_map.92 = (f32[2,1024,256]{2,1,0:T(8,128)S(1)}, bf16[2,1024,256]{2,1,0:T(8,128)(2,1)S(1)}, bf16[2,1024,256]{2,1,0:T(8,128)(2,1)S(1)}, bf16[2,320,1024]{2,1,0:T(8,128)(2,1)S(1)}) custom-call(s32[2]{0:T(128)S(4)} %get-tuple-element.76.me_ref, bf16[4,1024,128]{2,1,0:T(8,128)(2,1)S(1)} %get-tuple-element.78.q_ref.refs_0_, ...), custom_call_target="tpu_custom_call" | custom-call | flops 268435456 | tf_op jit(solution)/shard_map/pallas_call | solution.py:420
  31.3 0.7 collective-permute-start.7
  32.0 0.8 %shard_map.97 = (bf16[1024,128]{1,0:T(8,128)(2,1)S(1)}, f32[1024,128]{1,0:T(8,128)S(1)}, f32[1024,128]{1,0:T(8,128)S(1)}, f32[160,128]{1,0:T(8,128)S(1)}) custom-call(s32[2]{0:T(128)S(4)} %get-tuple-element.76.me_ref, bf16[4,1024,128]{2,1,0:T(8,128)(2,1)S(1)} %get-tuple-element.87.t_ref, f32[1,1024,128]{2,1,0:T(8,128)S(1)} %get-tuple-element.113.rest_0_, ...), custom_call_target="tpu_custom_call" | custom-call | flops 268435456 | tf_op jit(solution)/shard_map/pallas_call | solution.py:420
  32.9 1.5 %collective-permute-start.13 = (f32[160,128]{1,0:T(8,128)S(1)}, f32[160,128]{1,0:T(8,128)S(1)}, u32[]{:S(2)}, u32[]{:S(2)}) collective-permute-start(f32[160,128]{1,0:T(8,128)S(1)} %get-tuple-element.126), channel_id=1, source_target_pairs={{0,24},{8,16},{16,8},{24,0},{1,25},{9,17},{17,9},{25,1},{2,26},{10... | collective-permute-start | bytes 245768 | tf_op jit(solution)/shard_map/ppermute | solution.py:435
  34.4 0.8 %shard_map.94 = (bf16[1024,128]{1,0:T(8,128)(2,1)S(1)}, f32[1024,128]{1,0:T(8,128)S(1)}, f32[1024,128]{1,0:T(8,128)S(1)}, f32[160,128]{1,0:T(8,128)S(1)}) custom-call(s32[2]{0:T(128)S(4)} %get-tuple-element.76.me_ref, bf16[4,1024,128]{2,1,0:T(8,128)(2,1)S(1)} %get-tuple-element.87.t_ref, f32[2,1024,128]{2,1,0:T(8,128)S(1)} %get-tuple-element.102.rest_0_, ...), custom_call_target="tpu_custom_call" | custom-call | flops 268435456 | tf_op jit(solution)/shard_map/pallas_call | solution.py:420
  35.2 0.7 collective-permute-start.12
  35.9 0.8 %shard_map.93 = (bf16[1024,128]{1,0:T(8,128)(2,1)S(1)}, f32[1024,128]{1,0:T(8,128)S(1)}, f32[1024,128]{1,0:T(8,128)S(1)}, f32[160,128]{1,0:T(8,128)S(1)}) custom-call(s32[2]{0:T(128)S(4)} %get-tuple-element.76.me_ref, bf16[4,1024,128]{2,1,0:T(8,128)(2,1)S(1)} %get-tuple-element.87.t_ref, f32[2,1024,128]{2,1,0:T(8,128)S(1)} %get-tuple-element.102.rest_0_, ...), custom_call_target="tpu_custom_call" | custom-call | flops 268435456 | tf_op jit(solution)/shard_map/pallas_call | solution.py:420
  36.8 1.5 %collective-permute-start.11 = (f32[160,128]{1,0:T(8,128)S(1)}, f32[160,128]{1,0:T(8,128)S(1)}, u32[]{:S(2)}, u32[]{:S(2)}) collective-permute-start(f32[160,128]{1,0:T(8,128)S(1)} %get-tuple-element.124), channel_id=1, source_target_pairs={{0,8},{8,0},{16,24},{24,16},{1,9},{9,1},{17,25},{25,17},{2,10},{10... | collective-permute-start | bytes 245768 | tf_op jit(solution)/shard_map/ppermute | solution.py:435
  38.3 5.1 %shard_map.100 = (f32[2,16,1024]{2,1,0:T(8,128)S(1)}, f32[16,128]{1,0:T(8,128)S(1)}) custom-call(s32[2]{0:T(128)S(4)} %get-tuple-element.76.me_ref, bf16[4,1024,128]{2,1,0:T(8,128)(2,1)S(1)} %get-tuple-element.78.q_ref.refs_0_, bf16[4,128,1024]{2,1,0:T(8,128)(2,1)S(1)} %get-tuple-element.79.refs_1_.vt_ref, ...), custom_call_target="tpu_custom_call" | custom-call | flops 2147483648 | tf_op jit(solution)/shard_map/pallas_call | solution.py:420
  43.4 0.9 %shard_map.90 = (bf16[1024,128]{1,0:T(8,128)(2,1)S(1)}, f32[1024,128]{1,0:T(8,128)S(1)}, f32[1024,128]{1,0:T(8,128)S(1)}, f32[160,128]{1,0:T(8,128)S(1)}) custom-call(s32[2]{0:T(128)S(4)} %get-tuple-element.76.me_ref, bf16[4,1024,128]{2,1,0:T(8,128)(2,1)S(1)} %get-tuple-element.87.t_ref, f32[1,1024,128]{2,1,0:T(8,128)S(1)} %get-tuple-element.88.rest_0_, ...), custom_call_target="tpu_custom_call" | custom-call | flops 268435456 | tf_op jit(solution)/shard_map/pallas_call | solution.py:420
  44.3 1.8 %collective-permute-start.14 = (f32[160,128]{1,0:T(8,128)S(1)}, f32[160,128]{1,0:T(8,128)S(1)}, u32[]{:S(2)}, u32[]{:S(2)}) collective-permute-start(f32[160,128]{1,0:T(8,128)S(1)} %add_add_fusion), channel_id=1, source_target_pairs={{0,2},{2,0},{4,6},{6,4},{1,3},{3,1},{5,7},{7,5},{8,10},{10,8},{12,... | collective-permute-start | bytes 245768 | tf_op jit(solution)/shard_map/ppermute | solution.py:435
  46.1 1.5 %collective-permute-start.15 = (f32[160,128]{1,0:T(8,128)S(1)}, f32[160,128]{1,0:T(8,128)S(1)}, u32[]{:S(2)}, u32[]{:S(2)}) collective-permute-start(f32[160,128]{1,0:T(8,128)S(1)} %add_add_fusion), channel_id=1, source_target_pairs={{0,4},{2,6},{4,0},{6,2},{1,5},{3,7},{5,1},{7,3},{8,12},{10,14},{12... | collective-permute-start | bytes 245768 | tf_op jit(solution)/shard_map/ppermute | solution.py:435
  47.7 1.1 %collective-permute-start.16 = (f32[160,128]{1,0:T(8,128)S(1)}, f32[160,128]{1,0:T(8,128)S(1)}, u32[]{:S(2)}, u32[]{:S(2)}) collective-permute-start(f32[160,128]{1,0:T(8,128)S(1)} %add_add_fusion), channel_id=1, source_target_pairs={{0,6},{2,4},{4,2},{6,0},{1,7},{3,5},{5,3},{7,1},{8,14},{10,12},{12... | collective-permute-start | bytes 245768 | tf_op jit(solution)/shard_map/ppermute | solution.py:435
  48.8 2.7 %shard_map.101 = (f32[1,16,1024]{2,1,0:T(8,128)S(1)}, f32[16,128]{1,0:T(8,128)S(1)}) custom-call(s32[2]{0:T(128)S(4)} %get-tuple-element.76.me_ref, bf16[4,1024,128]{2,1,0:T(8,128)(2,1)S(1)} %get-tuple-element.78.q_ref.refs_0_, bf16[4,128,1024]{2,1,0:T(8,128)(2,1)S(1)} %get-tuple-element.79.refs_1_.vt_ref, ...), custom_call_target="tpu_custom_call" | custom-call | flops 1073741824 | tf_op jit(solution)/shard_map/pallas_call | solution.py:420
  51.5 3.2 %collective-permute-done.15.refs_1_ = f32[160,128]{1,0:T(8,128)S(1)} collective-permute-done((f32[160,128]{1,0:T(8,128)S(1)}, f32[160,128]{1,0:T(8,128)S(1)}, u32[]{:S(2)}, u32[]{:S(2)}) %collective-permute-start.15) | collective-permute-done | bytes 81952 | tf_op jit(solution)/shard_map/ppermute | solution.py:435
  54.8 1.3 %collective-permute-start.19 = (f32[160,128]{1,0:T(8,128)S(1)}, f32[160,128]{1,0:T(8,128)S(1)}, u32[]{:S(2)}, u32[]{:S(2)}) collective-permute-start(f32[160,128]{1,0:T(8,128)S(1)} %get-tuple-element.137), channel_id=1, source_target_pairs={{0,24},{8,16},{16,8},{24,0},{1,25},{9,17},{17,9},{25,1},{2,26},{10... | collective-permute-start | bytes 245768 | tf_op jit(solution)/shard_map/ppermute | solution.py:435
  56.1 1.5 %collective-permute-start.17 = (f32[160,128]{1,0:T(8,128)S(1)}, f32[160,128]{1,0:T(8,128)S(1)}, u32[]{:S(2)}, u32[]{:S(2)}) collective-permute-start(f32[160,128]{1,0:T(8,128)S(1)} %get-tuple-element.127), channel_id=1, source_target_pairs={{0,8},{8,0},{16,24},{24,16},{1,9},{9,1},{17,25},{25,17},{2,10},{10... | collective-permute-start | bytes 245768 | tf_op jit(solution)/shard_map/ppermute | solution.py:435
  57.5 0.8 collective-permute-start.18
  58.3 3.6 %shard_map.98 = (f32[1,16,1024]{2,1,0:T(8,128)S(1)}, f32[16,128]{1,0:T(8,128)S(1)}, bf16[4,1024,128]{2,1,0:T(8,128)(2,1)}) custom-call(s32[2]{0:T(128)S(4)} %get-tuple-element.76.me_ref, bf16[4,1024,128]{2,1,0:T(8,128)(2,1)S(1)} %get-tuple-element.78.q_ref.refs_0_, bf16[4,128,1024]{2,1,0:T(8,128)(2,1)S(1)} %get-tuple-element.79.refs_1_.vt_ref, ...), custom_call_target="tpu_custom_call" | custom-call | flops 1073741824 | tf_op jit(solution)/shard_map/pallas_call | solution.py:420
  62.4 0.5 shard_map.103.rest_4_
  62.9 0.8 %shard_map.104 = f32[32,128]{1,0:T(8,128)S(1)} custom-call(s32[2]{0:T(128)S(4)} %get-tuple-element.76.me_ref, bf16[4,1024,128]{2,1,0:T(8,128)(2,1)S(1)} %get-tuple-element.80.k_ref, bf16[4,128,1024]{2,1,0:T(8,128)(2,1)S(1)} %get-tuple-element.79.refs_1_.vt_ref, f32[16,128]{1,0:T(8,128)S(1)} %get-tuple-element.82.wk_ref, ...), custom_call_target="tpu_custom_call" | custom-call | flops 167772160 | tf_op jit(solution)/shard_map/pallas_call | solution.py:420
  63.8 1.2 %collective-permute-done.20 = f32[32,128]{1,0:T(8,128)S(1)} collective-permute-done((f32[32,128]{1,0:T(8,128)S(1)}, f32[32,128]{1,0:T(8,128)S(1)}, u32[]{:S(2)}, u32[]{:S(2)}) %collective-permute-start.20) | collective-permute-done | bytes 16416 | tf_op jit(solution)/shard_map/ppermute | solution.py:435
  65.3 1.2 %collective-permute-start.22 = (f32[32,128]{1,0:T(8,128)S(1)}, f32[32,128]{1,0:T(8,128)S(1)}, u32[]{:S(2)}, u32[]{:S(2)}) collective-permute-start(f32[32,128]{1,0:T(8,128)S(1)} %add.45), channel_id=1, source_target_pairs={{0,17},{1,16},{8,25},{9,24},{16,1},{17,0},{24,9},{25,8},{2,19},{3,... | collective-permute-start | bytes 49160 | tf_op jit(solution)/shard_map/ppermute | solution.py:435
  66.5 1.5 %collective-permute-start.23 = (f32[32,128]{1,0:T(8,128)S(1)}, f32[32,128]{1,0:T(8,128)S(1)}, u32[]{:S(2)}, u32[]{:S(2)}) collective-permute-start(f32[32,128]{1,0:T(8,128)S(1)} %add.45), channel_id=1, source_target_pairs={{0,25},{1,24},{8,17},{9,16},{16,9},{17,8},{24,1},{25,0},{2,27},{3,... | collective-permute-start | bytes 49160 | tf_op jit(solution)/shard_map/ppermute | solution.py:435
  68.5 2.1 %collective-permute-done.23 = f32[32,128]{1,0:T(8,128)S(1)} collective-permute-done((f32[32,128]{1,0:T(8,128)S(1)}, f32[32,128]{1,0:T(8,128)S(1)}, u32[]{:S(2)}, u32[]{:S(2)}) %collective-permute-start.23) | collective-permute-done | bytes 16416 | tf_op jit(solution)/shard_map/ppermute | solution.py:435
  70.5 1.2 %collective-permute-start.24 = (f32[32,128]{1,0:T(8,128)S(1)}, f32[32,128]{1,0:T(8,128)S(1)}, u32[]{:S(2)}, u32[]{:S(2)}) collective-permute-start(f32[32,128]{1,0:T(8,128)S(1)} %add_add_fusion.3), channel_id=1, source_target_pairs={{0,3},{1,2},{2,1},{3,0},{4,7},{5,6},{6,5},{7,4},{8,11},{9,10},{10,... | collective-permute-start | bytes 49160 | tf_op jit(solution)/shard_map/ppermute | solution.py:435
  71.7 1.4 %collective-permute-start.25 = (f32[32,128]{1,0:T(8,128)S(1)}, f32[32,128]{1,0:T(8,128)S(1)}, u32[]{:S(2)}, u32[]{:S(2)}) collective-permute-start(f32[32,128]{1,0:T(8,128)S(1)} %add_add_fusion.3), channel_id=1, source_target_pairs={{0,5},{1,4},{2,7},{3,6},{4,1},{5,0},{6,3},{7,2},{8,13},{9,12},{10,... | collective-permute-start | bytes 49160 | tf_op jit(solution)/shard_map/ppermute | solution.py:435
  73.2 1.3 %collective-permute-start.26 = (f32[32,128]{1,0:T(8,128)S(1)}, f32[32,128]{1,0:T(8,128)S(1)}, u32[]{:S(2)}, u32[]{:S(2)}) collective-permute-start(f32[32,128]{1,0:T(8,128)S(1)} %add_add_fusion.3), channel_id=1, source_target_pairs={{0,7},{1,6},{2,5},{3,4},{4,3},{5,2},{6,1},{7,0},{8,15},{9,14},{10,... | collective-permute-start | bytes 49160 | tf_op jit(solution)/shard_map/ppermute | solution.py:435
  74.4 1.6 %collective-permute-done.25 = f32[32,128]{1,0:T(8,128)S(1)} collective-permute-done((f32[32,128]{1,0:T(8,128)S(1)}, f32[32,128]{1,0:T(8,128)S(1)}, u32[]{:S(2)}, u32[]{:S(2)}) %collective-permute-start.25) | collective-permute-done | bytes 16416 | tf_op jit(solution)/shard_map/ppermute | solution.py:435
  76.0 2.1 %collective-permute-done.26 = f32[32,128]{1,0:T(8,128)S(1)} collective-permute-done((f32[32,128]{1,0:T(8,128)S(1)}, f32[32,128]{1,0:T(8,128)S(1)}, u32[]{:S(2)}, u32[]{:S(2)}) %collective-permute-start.26) | collective-permute-done | bytes 16416 | tf_op jit(solution)/shard_map/ppermute | solution.py:435
  78.1 0.6 slice_bitcast_fusion
  (33 shorter events, 2.0 us)
Async XLA Ops:
  3.6 7.5 %collective-permute-start = (f32[160,128]{1,0:T(8,128)S(1)}, f32[160,128]{1,0:T(8,128)S(1)}, u32[]{:S(2)}, u32[]{:S(2)}) collective-permute-start(f32[160,128]{1,0:T(8,128)S(1)} %get-tuple-element.94), channel_id=1, source_target_pairs={{0,1},{1,0},{8,9},{9,8},{16,17},{17,16},{24,25},{25,24},{2,3},{3,2... | collective-permute-start | bytes 245768 | tf_op jit(solution)/shard_map/ppermute | solution.py:435
  4.1 6.9 %collective-permute-start.1 = (f32[160,128]{1,0:T(8,128)S(1)}, f32[160,128]{1,0:T(8,128)S(1)}, u32[]{:S(2)}, u32[]{:S(2)}) collective-permute-start(f32[160,128]{1,0:T(8,128)S(1)} %get-tuple-element.95), channel_id=1, source_target_pairs={{0,9},{1,8},{8,1},{9,0},{16,25},{17,24},{24,17},{25,16},{2,11},{3,... | collective-permute-start | bytes 245768 | tf_op jit(solution)/shard_map/ppermute | solution.py:435
  6.7 5.6 %collective-permute-start.2 = (f32[160,128]{1,0:T(8,128)S(1)}, f32[160,128]{1,0:T(8,128)S(1)}, u32[]{:S(2)}, u32[]{:S(2)}) collective-permute-start(f32[160,128]{1,0:T(8,128)S(1)} %get-tuple-element.96), channel_id=1, source_target_pairs={{0,17},{1,16},{8,25},{9,24},{16,1},{17,0},{24,9},{25,8},{2,19},{3,... | collective-permute-start | bytes 245768 | tf_op jit(solution)/shard_map/ppermute | solution.py:435
  7.9 5.0 %collective-permute-start.3 = (f32[160,128]{1,0:T(8,128)S(1)}, f32[160,128]{1,0:T(8,128)S(1)}, u32[]{:S(2)}, u32[]{:S(2)}) collective-permute-start(f32[160,128]{1,0:T(8,128)S(1)} %get-tuple-element.97), channel_id=1, source_target_pairs={{0,25},{1,24},{8,17},{9,16},{16,9},{17,8},{24,1},{25,0},{2,27},{3,... | collective-permute-start | bytes 245768 | tf_op jit(solution)/shard_map/ppermute | solution.py:435
  13.0 7.5 %collective-permute-start.4 = (f32[160,128]{1,0:T(8,128)S(1)}, f32[160,128]{1,0:T(8,128)S(1)}, u32[]{:S(2)}, u32[]{:S(2)}) collective-permute-start(f32[160,128]{1,0:T(8,128)S(1)} %add_add_fusion.1), channel_id=1, source_target_pairs={{0,2},{2,0},{4,6},{6,4},{1,3},{3,1},{5,7},{7,5},{8,10},{10,8},{12,... | collective-permute-start | bytes 245768 | tf_op jit(solution)/shard_map/ppermute | solution.py:435
  14.6 9.5 %collective-permute-start.5 = (f32[160,128]{1,0:T(8,128)S(1)}, f32[160,128]{1,0:T(8,128)S(1)}, u32[]{:S(2)}, u32[]{:S(2)}) collective-permute-start(f32[160,128]{1,0:T(8,128)S(1)} %add_add_fusion.1), channel_id=1, source_target_pairs={{0,4},{2,6},{4,0},{6,2},{1,5},{3,7},{5,1},{7,3},{8,12},{10,14},{12... | collective-permute-start | bytes 245768 | tf_op jit(solution)/shard_map/ppermute | solution.py:435
  17.2 6.9 %collective-permute-start.6 = (f32[160,128]{1,0:T(8,128)S(1)}, f32[160,128]{1,0:T(8,128)S(1)}, u32[]{:S(2)}, u32[]{:S(2)}) collective-permute-start(f32[160,128]{1,0:T(8,128)S(1)} %add_add_fusion.1), channel_id=1, source_target_pairs={{0,6},{2,4},{4,2},{6,0},{1,7},{3,5},{5,3},{7,1},{8,14},{10,12},{12... | collective-permute-start | bytes 245768 | tf_op jit(solution)/shard_map/ppermute | solution.py:435
  24.2 7.9 %collective-permute-start.10 = (f32[160,128]{1,0:T(8,128)S(1)}, f32[160,128]{1,0:T(8,128)S(1)}, u32[]{:S(2)}, u32[]{:S(2)}) collective-permute-start(f32[160,128]{1,0:T(8,128)S(1)} %get-tuple-element.120), channel_id=1, source_target_pairs={{0,25},{1,24},{8,17},{9,16},{16,9},{17,8},{24,1},{25,0},{2,27},{3,... | collective-permute-start | bytes 245768 | tf_op jit(solution)/shard_map/ppermute | solution.py:435
  24.3 10.1 %collective-permute-start.9 = (f32[160,128]{1,0:T(8,128)S(1)}, f32[160,128]{1,0:T(8,128)S(1)}, u32[]{:S(2)}, u32[]{:S(2)}) collective-permute-start(f32[160,128]{1,0:T(8,128)S(1)} %get-tuple-element.111), channel_id=1, source_target_pairs={{0,17},{1,16},{8,25},{9,24},{16,1},{17,0},{24,9},{25,8},{2,19},{3,... | collective-permute-start | bytes 245768 | tf_op jit(solution)/shard_map/ppermute | solution.py:435
  28.2 7.7 %collective-permute-start.8 = (f32[160,128]{1,0:T(8,128)S(1)}, f32[160,128]{1,0:T(8,128)S(1)}, u32[]{:S(2)}, u32[]{:S(2)}) collective-permute-start(f32[160,128]{1,0:T(8,128)S(1)} %get-tuple-element.109), channel_id=1, source_target_pairs={{0,9},{1,8},{8,1},{9,0},{16,25},{17,24},{24,17},{25,16},{2,11},{3,... | collective-permute-start | bytes 245768 | tf_op jit(solution)/shard_map/ppermute | solution.py:435
  31.3 12.0 %collective-permute-start.7 = (f32[160,128]{1,0:T(8,128)S(1)}, f32[160,128]{1,0:T(8,128)S(1)}, u32[]{:S(2)}, u32[]{:S(2)}) collective-permute-start(f32[160,128]{1,0:T(8,128)S(1)} %get-tuple-element.98), channel_id=1, source_target_pairs={{0,1},{1,0},{8,9},{9,8},{16,17},{17,16},{24,25},{25,24},{2,3},{3,2... | collective-permute-start | bytes 245768 | tf_op jit(solution)/shard_map/ppermute | solution.py:435
  32.9 11.4 %collective-permute-start.13 = (f32[160,128]{1,0:T(8,128)S(1)}, f32[160,128]{1,0:T(8,128)S(1)}, u32[]{:S(2)}, u32[]{:S(2)}) collective-permute-start(f32[160,128]{1,0:T(8,128)S(1)} %get-tuple-element.126), channel_id=1, source_target_pairs={{0,24},{8,16},{16,8},{24,0},{1,25},{9,17},{17,9},{25,1},{2,26},{10... | collective-permute-start | bytes 245768 | tf_op jit(solution)/shard_map/ppermute | solution.py:435
  35.2 9.0 %collective-permute-start.12 = (f32[160,128]{1,0:T(8,128)S(1)}, f32[160,128]{1,0:T(8,128)S(1)}, u32[]{:S(2)}, u32[]{:S(2)}) collective-permute-start(f32[160,128]{1,0:T(8,128)S(1)} %get-tuple-element.125), channel_id=1, source_target_pairs={{0,16},{8,24},{16,0},{24,8},{1,17},{9,25},{17,1},{25,9},{2,18},{10... | collective-permute-start | bytes 245768 | tf_op jit(solution)/shard_map/ppermute | solution.py:435
  36.8 7.5 %collective-permute-start.11 = (f32[160,128]{1,0:T(8,128)S(1)}, f32[160,128]{1,0:T(8,128)S(1)}, u32[]{:S(2)}, u32[]{:S(2)}) collective-permute-start(f32[160,128]{1,0:T(8,128)S(1)} %get-tuple-element.124), channel_id=1, source_target_pairs={{0,8},{8,0},{16,24},{24,16},{1,9},{9,1},{17,25},{25,17},{2,10},{10... | collective-permute-start | bytes 245768 | tf_op jit(solution)/shard_map/ppermute | solution.py:435
  44.3 7.1 %collective-permute-start.14 = (f32[160,128]{1,0:T(8,128)S(1)}, f32[160,128]{1,0:T(8,128)S(1)}, u32[]{:S(2)}, u32[]{:S(2)}) collective-permute-start(f32[160,128]{1,0:T(8,128)S(1)} %add_add_fusion), channel_id=1, source_target_pairs={{0,2},{2,0},{4,6},{6,4},{1,3},{3,1},{5,7},{7,5},{8,10},{10,8},{12,... | collective-permute-start | bytes 245768 | tf_op jit(solution)/shard_map/ppermute | solution.py:435
  46.1 8.5 %collective-permute-start.15 = (f32[160,128]{1,0:T(8,128)S(1)}, f32[160,128]{1,0:T(8,128)S(1)}, u32[]{:S(2)}, u32[]{:S(2)}) collective-permute-start(f32[160,128]{1,0:T(8,128)S(1)} %add_add_fusion), channel_id=1, source_target_pairs={{0,4},{2,6},{4,0},{6,2},{1,5},{3,7},{5,1},{7,3},{8,12},{10,14},{12... | collective-permute-start | bytes 245768 | tf_op jit(solution)/shard_map/ppermute | solution.py:435
  47.7 7.0 %collective-permute-start.16 = (f32[160,128]{1,0:T(8,128)S(1)}, f32[160,128]{1,0:T(8,128)S(1)}, u32[]{:S(2)}, u32[]{:S(2)}) collective-permute-start(f32[160,128]{1,0:T(8,128)S(1)} %add_add_fusion), channel_id=1, source_target_pairs={{0,6},{2,4},{4,2},{6,0},{1,7},{3,5},{5,3},{7,1},{8,14},{10,12},{12... | collective-permute-start | bytes 245768 | tf_op jit(solution)/shard_map/ppermute | solution.py:435
  54.8 7.6 %collective-permute-start.19 = (f32[160,128]{1,0:T(8,128)S(1)}, f32[160,128]{1,0:T(8,128)S(1)}, u32[]{:S(2)}, u32[]{:S(2)}) collective-permute-start(f32[160,128]{1,0:T(8,128)S(1)} %get-tuple-element.137), channel_id=1, source_target_pairs={{0,24},{8,16},{16,8},{24,0},{1,25},{9,17},{17,9},{25,1},{2,26},{10... | collective-permute-start | bytes 245768 | tf_op jit(solution)/shard_map/ppermute | solution.py:435
  56.1 6.8 %collective-permute-start.17 = (f32[160,128]{1,0:T(8,128)S(1)}, f32[160,128]{1,0:T(8,128)S(1)}, u32[]{:S(2)}, u32[]{:S(2)}) collective-permute-start(f32[160,128]{1,0:T(8,128)S(1)} %get-tuple-element.127), channel_id=1, source_target_pairs={{0,8},{8,0},{16,24},{24,16},{1,9},{9,1},{17,25},{25,17},{2,10},{10... | collective-permute-start | bytes 245768 | tf_op jit(solution)/shard_map/ppermute | solution.py:435
  57.5 5.4 %collective-permute-start.18 = (f32[160,128]{1,0:T(8,128)S(1)}, f32[160,128]{1,0:T(8,128)S(1)}, u32[]{:S(2)}, u32[]{:S(2)}) collective-permute-start(f32[160,128]{1,0:T(8,128)S(1)} %get-tuple-element.128), channel_id=1, source_target_pairs={{0,16},{8,24},{16,0},{24,8},{1,17},{9,25},{17,1},{25,9},{2,18},{10... | collective-permute-start | bytes 245768 | tf_op jit(solution)/shard_map/ppermute | solution.py:435
  63.7 1.2 %collective-permute-start.20 = (f32[32,128]{1,0:T(8,128)S(1)}, f32[32,128]{1,0:T(8,128)S(1)}, u32[]{:S(2)}, u32[]{:S(2)}) collective-permute-start(f32[32,128]{1,0:T(8,128)S(1)} %shard_map.104), channel_id=1, source_target_pairs={{0,1},{1,0},{2,3},{3,2},{4,5},{5,4},{6,7},{7,6},{8,9},{9,8},{10,11... | collective-permute-start | bytes 49160 | tf_op jit(solution)/shard_map/ppermute | solution.py:435
  65.0 3.2 %collective-permute-start.21 = (f32[32,128]{1,0:T(8,128)S(1)}, f32[32,128]{1,0:T(8,128)S(1)}, u32[]{:S(2)}, u32[]{:S(2)}) collective-permute-start(f32[32,128]{1,0:T(8,128)S(1)} %add.45), channel_id=1, source_target_pairs={{0,9},{1,8},{8,1},{9,0},{16,25},{17,24},{24,17},{25,16},{2,11},{3,... | collective-permute-start | bytes 49160 | tf_op jit(solution)/shard_map/ppermute | solution.py:435
  65.3 3.2 %collective-permute-start.22 = (f32[32,128]{1,0:T(8,128)S(1)}, f32[32,128]{1,0:T(8,128)S(1)}, u32[]{:S(2)}, u32[]{:S(2)}) collective-permute-start(f32[32,128]{1,0:T(8,128)S(1)} %add.45), channel_id=1, source_target_pairs={{0,17},{1,16},{8,25},{9,24},{16,1},{17,0},{24,9},{25,8},{2,19},{3,... | collective-permute-start | bytes 49160 | tf_op jit(solution)/shard_map/ppermute | solution.py:435
  66.5 4.1 %collective-permute-start.23 = (f32[32,128]{1,0:T(8,128)S(1)}, f32[32,128]{1,0:T(8,128)S(1)}, u32[]{:S(2)}, u32[]{:S(2)}) collective-permute-start(f32[32,128]{1,0:T(8,128)S(1)} %add.45), channel_id=1, source_target_pairs={{0,25},{1,24},{8,17},{9,16},{16,9},{17,8},{24,1},{25,0},{2,27},{3,... | collective-permute-start | bytes 49160 | tf_op jit(solution)/shard_map/ppermute | solution.py:435
  70.5 3.9 %collective-permute-start.24 = (f32[32,128]{1,0:T(8,128)S(1)}, f32[32,128]{1,0:T(8,128)S(1)}, u32[]{:S(2)}, u32[]{:S(2)}) collective-permute-start(f32[32,128]{1,0:T(8,128)S(1)} %add_add_fusion.3), channel_id=1, source_target_pairs={{0,3},{1,2},{2,1},{3,0},{4,7},{5,6},{6,5},{7,4},{8,11},{9,10},{10,... | collective-permute-start | bytes 49160 | tf_op jit(solution)/shard_map/ppermute | solution.py:435
  71.7 4.2 %collective-permute-start.25 = (f32[32,128]{1,0:T(8,128)S(1)}, f32[32,128]{1,0:T(8,128)S(1)}, u32[]{:S(2)}, u32[]{:S(2)}) collective-permute-start(f32[32,128]{1,0:T(8,128)S(1)} %add_add_fusion.3), channel_id=1, source_target_pairs={{0,5},{1,4},{2,7},{3,6},{4,1},{5,0},{6,3},{7,2},{8,13},{9,12},{10,... | collective-permute-start | bytes 49160 | tf_op jit(solution)/shard_map/ppermute | solution.py:435
  73.2 5.0 %collective-permute-start.26 = (f32[32,128]{1,0:T(8,128)S(1)}, f32[32,128]{1,0:T(8,128)S(1)}, u32[]{:S(2)}, u32[]{:S(2)}) collective-permute-start(f32[32,128]{1,0:T(8,128)S(1)} %add_add_fusion.3), channel_id=1, source_target_pairs={{0,7},{1,6},{2,5},{3,4},{4,3},{5,2},{6,1},{7,0},{8,15},{9,14},{10,... | collective-permute-start | bytes 49160 | tf_op jit(solution)/shard_map/ppermute | solution.py:435
